TPU v7x, 32 devices: a 4x4x1 block of a 4x4x8 slice. The times are simulated.
32 devices in a mesh: dp: 1 (over z), tp: 4 (over y), cp: 8 (over x, core).
Axes of the slice: x: 4, y: 4, z: 1, core: 2. Of those that a mesh axis runs over, the one named last changes fastest.
The devices are a block of a 4x4x8 slice.
Arguments:
- tokens_in: bfloat16 [8192, 4096], P(('dp', 'cp', 'tp'))
- grad_out: bfloat16 [8192, 4096], P(('dp', 'cp', 'tp'))
- w_query: bfloat16 [4096, 4096], P(None, 'tp')
- w_key: bfloat16 [4096, 4096], P(None, 'tp')
- w_value: bfloat16 [4096, 4096], P(None, 'tp')
- w_out: bfloat16 [4096, 4096], P('tp')
Outputs:
- output 1: bfloat16 [8192, 4096], P(('dp', 'cp', 'tp'))
- output 2: bfloat16 [8192, 4096], P(('dp', 'cp', 'tp'))
All inputs are finite; a program needn't handle non-finite values.
Results may differ from a plain program's by a relative error of at most 0.0104356.
Values are sent between devices in bfloat16 or wider.
A program may use at most 768 MiB of HBM per device.

v0:
```python
import jax
import jax.numpy as jnp
from jax import lax
from jax.sharding import PartitionSpec as P

HEAD_DIM = 128


def block_rows(piece_rows, key_rows, head_count):
    budget = max(1, (1 << 22) // (key_rows * head_count))
    row_count = 8
    for candidate in (16, 32, 64, 128):
        if candidate <= budget and piece_rows % candidate == 0:
            row_count = candidate
    return row_count


def fold_positions(row_ids, seq_loc, cp_size):
    piece_rows = seq_loc // 2
    shard_idx = row_ids // seq_loc
    within = row_ids % seq_loc
    piece_id = jnp.where(within < piece_rows, shard_idx, 2 * cp_size - 1 - shard_idx)
    return piece_id * piece_rows + within % piece_rows


def dot_transposed(left, right):
    return lax.dot_general(left, right, (((1,), (1,)), ((), ())), preferred_element_type=jnp.float32)


def solution(mesh):
    cp_size = mesh.shape['cp']
    row_spec = P(('dp', 'cp', 'tp'), None)

    def local_step(x_blk, dy_blk, w_query, w_key, w_value, w_out):
        cp_rank = lax.axis_index('cp')
        x_loc = lax.all_gather(x_blk, 'tp', axis=0, tiled=True)
        seq_loc = x_loc.shape[0]
        seq_all = seq_loc * cp_size
        piece_rows = seq_loc // 2
        heads_q = w_query.shape[1] // HEAD_DIM
        heads_kv = w_key.shape[1] // HEAD_DIM
        group_size = heads_q // heads_kv
        score_scale = HEAD_DIM ** -0.5
        query_loc = jnp.dot(x_loc, w_query, preferred_element_type=jnp.float32).astype(jnp.bfloat16).reshape(seq_loc, heads_kv, group_size, HEAD_DIM)
        keys_loc = jnp.dot(x_loc, w_key, preferred_element_type=jnp.float32).astype(jnp.bfloat16).reshape(seq_loc, heads_kv, HEAD_DIM)
        values_loc = jnp.dot(x_loc, w_value, preferred_element_type=jnp.float32).astype(jnp.bfloat16).reshape(seq_loc, heads_kv, HEAD_DIM)
        keys_all = lax.all_gather(keys_loc, 'cp', axis=0, tiled=True)
        values_all = lax.all_gather(values_loc, 'cp', axis=0, tiled=True)
        dy_loc = lax.all_gather(dy_blk, 'tp', axis=0, tiled=True)
        d_out = dot_transposed(dy_loc, w_out).astype(jnp.bfloat16).reshape(seq_loc, heads_kv, group_size, HEAD_DIM)
        key_pos = fold_positions(jnp.arange(seq_all, dtype=jnp.int32), seq_loc, cp_size)
        query_pos = fold_positions(cp_rank * seq_loc + jnp.arange(seq_loc, dtype=jnp.int32), seq_loc, cp_size)
        blk_rows = block_rows(piece_rows, seq_all, heads_q)
        block_count = seq_loc // blk_rows

        def block_step(acc_pair, blk_in):
            dk_acc, dv_acc = acc_pair
            q_blk, do_blk, pos_blk = blk_in
            scores = jnp.einsum('qhgd,khd->hgqk', q_blk, keys_all, preferred_element_type=jnp.float32) * score_scale
            allowed = pos_blk[:, None] >= key_pos[None, :]
            scores = jnp.where(allowed, scores, -jnp.inf)
            log_norm = jax.nn.logsumexp(scores, axis=-1, keepdims=True)
            prob_bf = jnp.exp(scores - log_norm).astype(jnp.bfloat16)
            out_blk = jnp.einsum('hgqk,khd->qhgd', prob_bf, values_all, preferred_element_type=jnp.float32).astype(jnp.bfloat16)
            row_delta = jnp.einsum('qhgd,qhgd->hgq', do_blk, out_blk, preferred_element_type=jnp.float32)
            d_prob = jnp.einsum('qhgd,khd->hgqk', do_blk, values_all, preferred_element_type=jnp.float32)
            d_score = (prob_bf.astype(jnp.float32) * (d_prob - row_delta[..., None])).astype(jnp.bfloat16)
            dq_blk = (jnp.einsum('hgqk,khd->qhgd', d_score, keys_all, preferred_element_type=jnp.float32) * score_scale).astype(jnp.bfloat16)
            dk_acc = dk_acc + jnp.einsum('hgqk,qhgd->khd', d_score, q_blk, preferred_element_type=jnp.float32) * score_scale
            dv_acc = dv_acc + jnp.einsum('hgqk,qhgd->khd', prob_bf, do_blk, preferred_element_type=jnp.float32)
            return (dk_acc, dv_acc), (out_blk, dq_blk)

        zeros_kv = jnp.zeros((seq_all, heads_kv, HEAD_DIM), jnp.float32)
        blk_inputs = (query_loc.reshape(block_count, blk_rows, heads_kv, group_size, HEAD_DIM), d_out.reshape(block_count, blk_rows, heads_kv, group_size, HEAD_DIM), query_pos.reshape(block_count, blk_rows))
        (dk_part, dv_part), (out_blocks, dq_blocks) = lax.scan(block_step, (zeros_kv, zeros_kv), blk_inputs)
        attn_out = out_blocks.reshape(seq_loc, heads_q * HEAD_DIM)
        d_query = dq_blocks.reshape(seq_loc, heads_q * HEAD_DIM)
        y_part = jnp.dot(attn_out, w_out, preferred_element_type=jnp.float32)
        y_blk = lax.psum_scatter(y_part, 'tp', scatter_dimension=0, tiled=True).astype(jnp.bfloat16)
        dk_own = lax.psum_scatter(dk_part, 'cp', scatter_dimension=0, tiled=True).astype(jnp.bfloat16).reshape(seq_loc, heads_kv * HEAD_DIM)
        dv_own = lax.psum_scatter(dv_part, 'cp', scatter_dimension=0, tiled=True).astype(jnp.bfloat16).reshape(seq_loc, heads_kv * HEAD_DIM)
        dx_part = dot_transposed(d_query, w_query) + dot_transposed(dk_own, w_key) + dot_transposed(dv_own, w_value)
        dx_blk = lax.psum_scatter(dx_part, 'tp', scatter_dimension=0, tiled=True).astype(jnp.bfloat16)
        return y_blk, dx_blk

    return jax.shard_map(local_step, mesh=mesh, in_specs=(row_spec, row_spec, P(None, 'tp'), P(None, 'tp'), P(None, 'tp'), P('tp', None)), out_specs=(row_spec, row_spec), check_vma=False)
```

profile of v0, /device:TPU:97, one launch (start us, length us, event | category | flops | bytes accessed | tf_op | source)
XLA Modules:
  0.0 2913.5 jit_solution(4390152946018825931)
XLA Ops:
  8.8 85.3 %all-gather.5.cloned.1.call-done = bf16[1024,4096]{1,0:T(8,128)(2,1)} async-done(((bf16[256,4096]{1,0:T(8,128)(2,1)}), bf16[1024,4096]{1,0:T(8,128)(2,1)}) %all-gather.5.cloned.1.call-update) | async-done | bytes 8388624 | tf_op jit(solution)/shard_map/all_gather | solution.py:36
  127.2 50.2 %all-gather.9.cloned.1.call-done = bf16[1024,4096]{1,0:T(8,128)(2,1)} async-done(((bf16[256,4096]{1,0:T(8,128)(2,1)}), bf16[1024,4096]{1,0:T(8,128)(2,1)}) %all-gather.9.cloned.1.call-update) | async-done | bytes 8388624 | tf_op jit(solution)/shard_map/all_gather | solution.py:49
  207.4 55.8 %all-gather.11.cloned.1.call-done = bf16[8192,8,128]{2,0,1:T(8,128)(2,1)} async-done(((bf16[1024,8,128]{2,0,1:T(8,128)(2,1)}), bf16[8192,8,128]{2,0,1:T(8,128)(2,1)}) %all-gather.11.cloned.1.call-update) | async-done | bytes 16777232 | tf_op jit(solution)/shard_map/all_gather | solution.py:48
  263.2 84.6 %all-gather.7.cloned.1.call-done = bf16[8192,8,128]{2,0,1:T(8,128)(2,1)} async-done(((bf16[1024,8,128]{2,0,1:T(8,128)(2,1)}), bf16[8192,8,128]{2,0,1:T(8,128)(2,1)}) %all-gather.7.cloned.1.call-update) | async-done | bytes 16777232 | tf_op jit(solution)/shard_map/all_gather | solution.py:47
  347.8 1921.5 %while.17 = (s32[]{:T(128)}, f32[8192,8,128]{0,2,1:T(8,128)}, f32[8192,8,128]{0,2,1:T(8,128)}, bf16[16,64,8,1,128]{4,2,1,0,3:T(8,128)(2,1)}, bf16[16,64,8,1,128]...) while((s32[]{:T(128)}, f32[8192,8,128]{0,2,1:T(8,128)}, ...), condition=%wide.region_3.4_spmd.clone, body=%wide.region_0.3_spmd.clone.sunk | while | flops 6548522496 | bytes 348085152 | solution.py:75
  513.5 26.9 bitcast_add_fusion.4
  635.1 26.9 bitcast_add_fusion.4
  756.7 26.9 bitcast_add_fusion.4
  878.2 26.9 bitcast_add_fusion.4
  999.8 26.9 bitcast_add_fusion.4
  1121.4 26.9 bitcast_add_fusion.4
  1242.9 26.9 bitcast_add_fusion.4
  1364.5 26.9 bitcast_add_fusion.4
  1486.1 26.9 bitcast_add_fusion.4
  1607.6 26.9 bitcast_add_fusion.4
  1729.2 26.9 bitcast_add_fusion.4
  1850.8 26.9 bitcast_add_fusion.4
  1972.3 26.9 bitcast_add_fusion.4
  2093.9 26.9 bitcast_add_fusion.4
  2215.5 26.9 bitcast_add_fusion.4
  2301.7 135.5 %reduce-scatter.7.cloned.1.call-done = f32[1024,8,128]{0,2,1:T(8,128)} async-done(((f32[8192,8,128]{0,2,1:T(8,128)}), f32[1024,8,128]{0,2,1:T(8,128)}) %reduce-scatter.7.cloned.1.call-update) | async-done | bytes 4194320 | tf_op jit(solution)/shard_map/reduce_scatter | solution.py:80
  2439.8 167.4 %reduce-scatter.9.cloned.1.call-done = f32[1024,8,128]{0,2,1:T(8,128)} async-done(((f32[8192,8,128]{0,2,1:T(8,128)}), f32[1024,8,128]{0,2,1:T(8,128)}) %reduce-scatter.9.cloned.1.call-update) | async-done | bytes 4194320 | tf_op jit(solution)/shard_map/reduce_scatter | solution.py:81
  2646.1 108.8 %reduce-scatter.5.cloned.1.call-done = f32[256,4096]{1,0:T(8,128)} async-done(((f32[1024,4096]{1,0:T(8,128)}), f32[256,4096]{1,0:T(8,128)}) %reduce-scatter.5.cloned.1.call-update) | async-done | bytes 4194320 | tf_op jit(solution)/shard_map/reduce_scatter | solution.py:79
  2758.7 143.8 %reduce-scatter.11.cloned.1.call-done = f32[256,4096]{1,0:T(8,128)} async-done(((f32[1024,4096]{1,0:T(8,128)}), f32[256,4096]{1,0:T(8,128)}) %reduce-scatter.11.cloned.1.call-update) | async-done | bytes 4194320 | tf_op jit(solution)/shard_map/reduce_scatter | solution.py:83
  (314 shorter events, 1663.1 us)
Async XLA Ops:
  7.2 86.9 %all-gather.5.cloned.1.call-start = ((), (), s32[]{:S(2)}) async-start(), calls=%async_computation.4 | async-start | bytes 10485760 | tf_op jit(solution)/shard_map/all_gather | solution.py:36
  8.0 169.4 %all-gather.9.cloned.1.call-start = ((), (), s32[]{:S(2)}) async-start(), calls=%async_computation.6 | async-start | bytes 10485760 | tf_op jit(solution)/shard_map/all_gather | solution.py:49
  8.8 254.4 %all-gather.11.cloned.1.call-start = ((), (), s32[]{:S(2)}) async-start(), calls=%async_computation.7 | async-start | bytes 18874368 | tf_op jit(solution)/shard_map/all_gather | solution.py:48
  110.3 237.5 %all-gather.7.cloned.1.call-start = ((), (), s32[]{:S(2)}) async-start(), calls=%async_computation.5 | async-start | bytes 18874368 | tf_op jit(solution)/shard_map/all_gather | solution.py:47
  126.6 2310.6 %reduce-scatter.7.cloned.1.call-start = ((), (), s32[]{:S(2)}) async-start(), calls=%async_computation.9 | async-start | bytes 37748736 | tf_op jit(solution)/shard_map/reduce_scatter | solution.py:80
  380.0 10.7 copy-start
  477.6 10.7 copy-start
  599.2 10.7 copy-start
  720.8 10.7 copy-start
  842.3 10.7 copy-start
  963.9 10.7 copy-start
  1085.5 10.7 copy-start
  1207.0 10.7 copy-start
  1328.6 10.7 copy-start
  1450.2 10.7 copy-start
  1571.7 10.7 copy-start
  1693.3 10.7 copy-start
  1814.9 10.7 copy-start
  1936.4 10.7 copy-start
  2058.0 10.7 copy-start
  2179.6 10.7 copy-start
  2269.5 337.7 %reduce-scatter.9.cloned.1.call-start = ((), (), s32[]{:S(2)}) async-start(), calls=%async_computation.10 | async-start | bytes 37748736 | tf_op jit(solution)/shard_map/reduce_scatter | solution.py:81
  2270.1 484.8 %reduce-scatter.5.cloned.1.call-start = ((), (), s32[]{:S(2)}) async-start(), calls=%async_computation.8 | async-start | bytes 20971520 | tf_op jit(solution)/shard_map/reduce_scatter | solution.py:79
  2285.7 616.8 %reduce-scatter.11.cloned.1.call-start = ((), (), s32[]{:S(2)}) async-start(), calls=%async_computation.11 | async-start | bytes 20971520 | tf_op jit(solution)/shard_map/reduce_scatter | solution.py:83
  (2 other events, 3.2 us)
Sparse Core Ops, SparseCore 0:
  9.6 84.4 all-gather.4
  95.7 81.6 all-gather.8
  179.0 84.1 all-gather.10
  264.6 83.1 all-gather.6
  2269.6 167.6 reduce-scatter.6
  2439.5 167.6 reduce-scatter.8
  2609.5 145.3 reduce-scatter.4
  2757.3 145.1 reduce-scatter.10
where the time goes:
time: 2920 us; the launch traced here: 2910 us
  matrix products  1720 us (59%)
  waiting for transfers between devices  834 us (29%)
  other arithmetic  303 us (10%)
  local copies, waits for them, and re-layouts  38.9 us (1%)
    dot_general x16, matrix products, block_step(): jnp.einsum('hgqk,qhgd->khd', d_score, q_blk, preferred_element_type=jnp.f...  418 us
    dot_general x16, matrix products, block_step(): jnp.einsum('hgqk,qhgd->khd', prob_bf, do_blk, preferred_element_type=jnp....  418 us
    dot_general x16, matrix products, block_step(): jnp.einsum('qhgd,khd->hgqk', do_blk, values_all, preferred_element_type=j...  210 us
    dot_general x16, matrix products, block_step(): jnp.einsum('qhgd,khd->hgqk', q_blk, keys_all, preferred_element_type=jnp....  206 us
    dot_general x16, matrix products, block_step(): jnp.einsum('hgqk,khd->qhgd', d_score, keys_all, preferred_element_type=jn...  179 us
    dot_general x16, matrix products, block_step(): jnp.einsum('hgqk,khd->qhgd', prob_bf, values_all, preferred_element_type=...  171 us
    reduce_scatter x1, waiting for transfers between devices, local_step(): lax.psum_scatter(dv_part, 'cp', scatter_dimension=0, tiled=True)  167 us
    reduce_sum x16, other arithmetic, block_step(): log_norm = jax.nn.logsumexp(scores, axis=-1, keepdims=True)  163 us
  transfers between devices with their start and end apart: 8, of which 8 were waited for; matrix products, arithmetic and copies ran while one was open for 5% of the time, Pallas kernels for 0%

commit v1 on v0

v1 whole, which is shorter than its diff:
```python
import functools, math
import jax
import jax.numpy as jnp
from jax import lax
from jax.experimental import pallas as pl
from jax.experimental.pallas import tpu as pltpu

HEAD_DIM = 128
F32, BF16 = jnp.float32, jnp.bfloat16
LOG2E = math.log2(math.e)


def dot_nt(a, b):
    return lax.dot_general(a, b, (((1,), (1,)), ((), ())), preferred_element_type=F32)


def dot_nn(a, b):
    return lax.dot_general(a, b, (((1,), (0,)), ((), ())), preferred_element_type=F32)


def attn_fwd_kernel(bq, sub, q_ref, k_ref, v_ref, o_ref, l_ref, vt_ref, s_ref, acc_ref):
    seq = q_ref.shape[0]
    nblk = seq // bq
    nsub = bq // sub
    c = HEAD_DIM ** -0.5 * LOG2E

    def transpose_step(b, _):
        rows = pl.ds(pl.multiple_of(b * bq, bq), bq)
        vt_ref[:, rows] = v_ref[rows, :].T
        return 0

    lax.fori_loop(0, nblk, transpose_step, 0)

    def fill(q, blk, m, masked):
        for r in range(nsub):
            rows = pl.ds(pl.multiple_of(blk * bq + r * sub, sub), sub)
            s = dot_nt(k_ref[rows, :], q)
            if masked:
                kk = lax.broadcasted_iota(jnp.int32, (sub, bq), 0) + r * sub
                qq = lax.broadcasted_iota(jnp.int32, (sub, bq), 1)
                s = jnp.where(kk <= qq, s, -jnp.inf)
            s_ref[r * sub:(r + 1) * sub, :] = s
            m = jnp.maximum(m, jnp.max(s, axis=0, keepdims=True))
        return m

    def use(blk, m, m_old, l):
        mc = m * c
        alpha = jnp.exp2(m_old * c - mc)
        part = jnp.zeros((1, bq), F32)
        out = None
        for r in range(nsub):
            cols = pl.ds(pl.multiple_of(blk * bq + r * sub, sub), sub)
            p = jnp.exp2(s_ref[r * sub:(r + 1) * sub, :] * c - mc)
            part = part + jnp.sum(p, axis=0, keepdims=True)
            d = dot_nn(vt_ref[:, cols], p.astype(BF16))
            out = d if out is None else out + d
        acc_ref[...] = acc_ref[...] * alpha + out
        return l * alpha + part

    def q_step(i, _):
        rows = pl.ds(pl.multiple_of(i * bq, bq), bq)
        q = q_ref[rows, :]
        acc_ref[...] = jnp.zeros_like(acc_ref)
        m0 = jnp.full((1, bq), -jnp.inf, F32)
        m1 = fill(q, i, m0, True)

        def body(t, carry):
            m_old, m, l = carry
            cur = jnp.where(t == 0, i, t - 1)
            mc = m * c
            alpha = jnp.exp2(m_old * c - mc)
            part = jnp.zeros((1, bq), F32)
            m_new = m
            out = None
            for r in range(nsub):
                cols = pl.ds(pl.multiple_of(cur * bq + r * sub, sub), sub)
                krows = pl.ds(pl.multiple_of(t * bq + r * sub, sub), sub)
                p = jnp.exp2(s_ref[r * sub:(r + 1) * sub, :] * c - mc)
                s = dot_nt(k_ref[krows, :], q)
                part = part + jnp.sum(p, axis=0, keepdims=True)
                d = dot_nn(vt_ref[:, cols], p.astype(BF16))
                out = d if out is None else out + d
                m_new = jnp.maximum(m_new, jnp.max(s, axis=0, keepdims=True))
                s_ref[r * sub:(r + 1) * sub, :] = s
            acc_ref[...] = acc_ref[...] * alpha + out
            return m, m_new, l * alpha + part

        m_old, m, l = lax.fori_loop(0, i, body, (m1, m1, jnp.zeros((1, bq), F32)))
        l = use(jnp.where(i == 0, i, i - 1), m, m_old, l)
        o_ref[rows, :] = (acc_ref[...] * (1.0 / l)).T.astype(BF16)
        l_ref[i] = jnp.broadcast_to(m * c + jnp.log2(l), (8, bq))
        return 0

    lax.fori_loop(0, nblk, q_step, 0)


def attn_fwd(q, k, v, bq=512, sub=256):
    seq = q.shape[0]
    full = pl.BlockSpec(memory_space=pltpu.VMEM)
    tiles = seq * seq // 2
    return pl.pallas_call(
        functools.partial(attn_fwd_kernel, bq, sub),
        out_shape=(jax.ShapeDtypeStruct((seq, HEAD_DIM), BF16), jax.ShapeDtypeStruct((seq // bq, 8, bq), F32)),
        in_specs=[full] * 3,
        out_specs=(full, full),
        scratch_shapes=[pltpu.VMEM((HEAD_DIM, seq), BF16), pltpu.VMEM((bq, bq), F32), pltpu.VMEM((HEAD_DIM, bq), F32)],
        compiler_params=pltpu.CompilerParams(vmem_limit_bytes=48 << 20),
        cost_estimate=pl.CostEstimate(flops=4 * tiles * HEAD_DIM, bytes_accessed=8 * seq * HEAD_DIM, transcendentals=tiles),
        name="attn_fwd",
    )(q, k, v)


def attn_bwd_kernel(bq, sub, q_ref, k_ref, v_ref, do_ref, o_ref, l_ref, dq_ref, dk_ref, dv_ref, kt_ref, p_ref, ds_ref, dqt_ref, dk_acc, dv_acc):
    seq = q_ref.shape[0]
    nblk = seq // bq
    nsub = bq // sub
    scale = HEAD_DIM ** -0.5
    c = scale * LOG2E

    def init_step(b, _):
        rows = pl.ds(pl.multiple_of(b * bq, bq), bq)
        kt_ref[:, rows] = k_ref[rows, :].T
        dk_acc[rows, :] = jnp.zeros((bq, HEAD_DIM), F32)
        dv_acc[rows, :] = jnp.zeros((bq, HEAD_DIM), F32)
        return 0

    lax.fori_loop(0, nblk, init_step, 0)

    def q_step(i, _):
        rows = pl.ds(pl.multiple_of(i * bq, bq), bq)
        q = q_ref[rows, :]
        do = do_ref[rows, :]
        prod = do.astype(F32) * o_ref[rows, :].astype(F32)
        delta = jnp.sum(prod.T, axis=0, keepdims=True)
        lse = l_ref[i][0:1, :]
        dqt_ref[...] = jnp.zeros_like(dqt_ref)

        def make(blk, r, masked):
            krows = pl.ds(pl.multiple_of(blk * bq + r * sub, sub), sub)
            s = dot_nt(k_ref[krows, :], q)
            dp = dot_nt(v_ref[krows, :], do)
            p = jnp.exp2(s * c - lse)
            if masked:
                kk = lax.broadcasted_iota(jnp.int32, (sub, bq), 0) + r * sub
                qq = lax.broadcasted_iota(jnp.int32, (sub, bq), 1)
                p = jnp.where(kk <= qq, p, 0.0)
            pb = p.astype(BF16)
            ds = (pb.astype(F32) * (dp - delta)).astype(BF16)
            return pb, ds

        def flush(blk, r, pb, ds):
            krows = pl.ds(pl.multiple_of(blk * bq + r * sub, sub), sub)
            dv_acc[krows, :] += dot_nn(pb, do)
            dk_acc[krows, :] += dot_nn(ds, q)
            return dot_nn(kt_ref[:, krows], ds)

        for r in range(nsub):
            sl = slice(r * sub, (r + 1) * sub)
            p_ref[sl, :], ds_ref[sl, :] = make(i, r, True)

        def body(t, _):
            cur = jnp.where(t == 0, i, t - 1)
            out = None
            for r in range(nsub):
                sl = slice(r * sub, (r + 1) * sub)
                d = flush(cur, r, p_ref[sl, :], ds_ref[sl, :])
                out = d if out is None else out + d
                p_ref[sl, :], ds_ref[sl, :] = make(t, r, False)
            dqt_ref[...] += out
            return 0

        lax.fori_loop(0, i, body, 0)
        cur = jnp.where(i == 0, i, i - 1)
        out = None
        for r in range(nsub):
            sl = slice(r * sub, (r + 1) * sub)
            d = flush(cur, r, p_ref[sl, :], ds_ref[sl, :])
            out = d if out is None else out + d
        dq_ref[rows, :] = ((dqt_ref[...] + out) * scale).T.astype(BF16)
        return 0

    lax.fori_loop(0, nblk, q_step, 0)

    def final_step(b, _):
        rows = pl.ds(pl.multiple_of(b * bq, bq), bq)
        dk_ref[rows, :] = (dk_acc[rows, :] * scale).astype(BF16)
        dv_ref[rows, :] = dv_acc[rows, :].astype(BF16)
        return 0

    lax.fori_loop(0, nblk, final_step, 0)


def attn_bwd(q, k, v, do, o, lse, bq=512, sub=256):
    seq = q.shape[0]
    full = pl.BlockSpec(memory_space=pltpu.VMEM)
    tiles = seq * seq // 2
    shape = jax.ShapeDtypeStruct((seq, HEAD_DIM), BF16)
    return pl.pallas_call(
        functools.partial(attn_bwd_kernel, bq, sub),
        out_shape=(shape, shape, shape),
        in_specs=[full] * 6,
        out_specs=(full, full, full),
        scratch_shapes=[
            pltpu.VMEM((HEAD_DIM, seq), BF16),
            pltpu.VMEM((bq, bq), BF16),
            pltpu.VMEM((bq, bq), BF16),
            pltpu.VMEM((HEAD_DIM, bq), F32),
            pltpu.VMEM((seq, HEAD_DIM), F32),
            pltpu.VMEM((seq, HEAD_DIM), F32),
        ],
        compiler_params=pltpu.CompilerParams(vmem_limit_bytes=56 << 20),
        cost_estimate=pl.CostEstimate(flops=10 * tiles * HEAD_DIM, bytes_accessed=16 * seq * HEAD_DIM, transcendentals=tiles),
        name="attn_bwd",
    )(q, k, v, do, o, lse)


from jax.sharding import PartitionSpec as P

MESH = pl.DeviceIdType.MESH


def exchange_kernel(cp_size, to_heads, *refs):
    count = (len(refs) - 4) // 2
    srcs, dsts = refs[:count], refs[count:2 * count]
    stage, local_sem, send_sem, recv_sem = refs[2 * count:]
    me = lax.axis_index('cp')
    piece = stage.shape[2]

    def by_rows(ref, owner, half):
        start = jnp.where(half == 0, owner, 2 * cp_size - 1 - owner) * piece
        return ref.at[pl.ds(pl.multiple_of(start, piece), piece), :]

    def by_head(ref, head, half):
        return ref.at[pl.ds(half * piece, piece), pl.ds(pl.multiple_of(head * HEAD_DIM, HEAD_DIM), HEAD_DIM)]

    def ends(a, peer, half):
        if to_heads:
            return by_head(srcs[a], peer, half), by_rows(dsts[a], me, half)
        return by_rows(srcs[a], peer, half), by_head(dsts[a], me, half)

    barrier = pltpu.get_barrier_semaphore()
    for d in range(1, cp_size):
        pl.semaphore_signal(barrier, inc=1, device_id={'cp': lax.rem(me + d, cp_size)}, device_id_type=MESH)
    pl.semaphore_wait(barrier, cp_size - 1)
    copies = []
    order = sorted(range(1, cp_size), key=lambda d: -min(d, cp_size - d))
    for a in range(count):
        for d in order:
            peer = lax.rem(me + d, cp_size)
            for half in range(2):
                src, dst = ends(a, peer, half)
                copy = pltpu.make_async_remote_copy(
                    src_ref=src, dst_ref=dst, send_sem=send_sem.at[a, d - 1, half], recv_sem=recv_sem.at[a, d - 1, half],
                    device_id={'cp': peer}, device_id_type=MESH)
                copy.start()
                copies.append(copy)
    pulls = []
    for a in range(count):
        for half in range(2):
            src, dst = ends(a, me, half)
            pull = pltpu.make_async_copy(src, stage.at[a, half], local_sem.at[a, half])
            pull.start()
            pulls.append((pull, a, half, dst))
    pushes = []
    for pull, a, half, dst in pulls:
        pull.wait()
        push = pltpu.make_async_copy(stage.at[a, half], dst, local_sem.at[a, half])
        push.start()
        pushes.append(push)
    for push in pushes:
        push.wait()
    for copy in copies:
        copy.wait()


def exchange(arrays, cp_size, to_heads, collective_id):
    count = len(arrays)
    rows, cols = arrays[0].shape
    piece = rows // 2 if to_heads else rows // (2 * cp_size)
    out = (rows * cp_size, cols // cp_size) if to_heads else (rows // cp_size, cols * cp_size)
    sent = count * rows * cols * 2 * (cp_size - 1) // cp_size
    anywhere = pl.BlockSpec(memory_space=pl.ANY)
    return pl.pallas_call(
        functools.partial(exchange_kernel, cp_size, to_heads),
        out_shape=tuple(jax.ShapeDtypeStruct(out, BF16) for _ in arrays),
        in_specs=[anywhere] * count,
        out_specs=(anywhere,) * count,
        scratch_shapes=[
            pltpu.VMEM((count, 2, piece, HEAD_DIM), BF16),
            pltpu.SemaphoreType.DMA((count, 2)),
            pltpu.SemaphoreType.DMA((count, cp_size - 1, 2)),
            pltpu.SemaphoreType.DMA((count, cp_size - 1, 2)),
        ],
        compiler_params=pltpu.CompilerParams(collective_id=collective_id, has_side_effects=True, vmem_limit_bytes=8 << 20),
        cost_estimate=pl.CostEstimate(flops=1000 * sent, bytes_accessed=2 * sent, transcendentals=0),
        name="exchange_to_heads" if to_heads else "exchange_to_rows",
    )(*arrays)


def project(a, w):
    return jnp.dot(a, w, preferred_element_type=F32).astype(BF16)


def solution(mesh):
    cp_size = mesh.shape['cp']
    row_spec = P(('dp', 'cp', 'tp'), None)

    def local_step(x_blk, dy_blk, w_query, w_key, w_value, w_out):
        x_loc = lax.all_gather(x_blk, 'tp', axis=0, tiled=True)
        x_loc, dy_blk = lax.optimization_barrier((x_loc, dy_blk))
        dy_loc = lax.all_gather(dy_blk, 'tp', axis=0, tiled=True)
        q, k, v = exchange([project(x_loc, w) for w in (w_query, w_key, w_value)], cp_size, True, 0)
        out, lse = attn_fwd(q, k, v)
        dy_loc, out = lax.optimization_barrier((dy_loc, out))
        d_out = dot_nt(dy_loc, w_out).astype(BF16)
        (out_rows,) = exchange([out], cp_size, False, 2)
        y_part = jnp.dot(out_rows, w_out, preferred_element_type=F32)
        d_out, y_part = lax.optimization_barrier((d_out, y_part))
        y_blk = lax.psum_scatter(y_part, 'tp', scatter_dimension=0, tiled=True).astype(BF16)
        (do,) = exchange([d_out], cp_size, True, 1)
        grads = attn_bwd(q, k, v, do, out, lse)
        dq, dk, dv = exchange(list(grads), cp_size, False, 3)
        dx_part = dot_nt(dq, w_query) + dot_nt(dk, w_key) + dot_nt(dv, w_value)
        dx_blk = lax.psum_scatter(dx_part, 'tp', scatter_dimension=0, tiled=True).astype(BF16)
        return y_blk, dx_blk

    weight = P(None, 'tp')
    return jax.shard_map(local_step, mesh=mesh, in_specs=(row_spec, row_spec, weight, weight, weight, P('tp', None)), out_specs=(row_spec, row_spec), check_vma=False)
```

time: 2920 us -> 763 us (0.26)
  matrix products: 1720 us -> 114 us
  waiting for transfers between devices: 834 us -> 228 us
  Pallas kernels: 0 us -> 387 us
  other arithmetic: 303 us -> 7.59 us
    dot_general x104 -> x8, matrix products: 1720 us -> 114 us  [the longest x4 67.5 us: dot_nt(): lax.dot_general(a, b, (((1,), (1,)), ((), ())), preferred_element_type=F32)]
    reduce_scatter x3 -> x1, waiting for transfers between devices: 412 us -> 0.02 us  [local_step(): lax.psum_scatter(y_part, 'tp', scatter_dimension=0, tiled=True).astype(BF16)]
    pallas_call x0 -> x6, Pallas kernels: none -> 387 us  [the longest x4 199 us: exchange(): pl.pallas_call(functools.partial(exchange_kernel, cp_size, to_heads), out...]
    reduce_sum x16 -> x0, other arithmetic: 163 us -> none  [block_step(): log_norm = jax.nn.logsumexp(scores, axis=-1, keepdims=True)]
    all_gather x2 -> x0, waiting for transfers between devices: 140 us -> none  [the longest x1 84.6 us: local_step(): keys_all = lax.all_gather(keys_loc, 'cp', axis=0, tiled=True)]
    convert_element_type x19 -> x1, other arithmetic: 130 us -> 3.79 us  [local_step(): lax.psum_scatter(y_part, 'tp', scatter_dimension=0, tiled=True).astype(BF16)]
    all_gather x1, waiting for transfers between devices: 50.2 us -> 0.01 us  [local_step(): dy_loc = lax.all_gather(dy_blk, 'tp', axis=0, tiled=True)]
  transfers between devices with their start and end apart: 8 -> 4, of which waited for: 8 -> 2; matrix products, arithmetic and copies ran while one was open for 5% -> 12% of each run, Pallas kernels for 0% -> 47%
where the time goes in v1:
time: 763 us
  Pallas kernels  387 us (51%)
  waiting for transfers between devices  228 us (30%)
  matrix products  114 us (15%)
  between operations  14 us (2%)
  local copies, waits for them, and re-layouts  12.3 us (2%)
    pallas_call x4, Pallas kernels, exchange(): pl.pallas_call(functools.partial(exchange_kernel, cp_size, to_heads), out...  199 us
    reduce_scatter x1, waiting for transfers between devices, local_step(): lax.psum_scatter(dx_part, 'tp', scatter_dimension=0, tiled=True)  142 us
    pallas_call x1, Pallas kernels, attn_bwd(): pl.pallas_call(functools.partial(attn_bwd_kernel, bq, sub), out_shape=(sh...  118 us
    all_gather x1, waiting for transfers between devices, local_step(): x_loc = lax.all_gather(x_blk, 'tp', axis=0, tiled=True)  85.9 us
    pallas_call x1, Pallas kernels, attn_fwd(): pl.pallas_call(functools.partial(attn_fwd_kernel, bq, sub), out_shape=(ja...  69.8 us
    dot_general x4, matrix products, dot_nt(): lax.dot_general(a, b, (((1,), (1,)), ((), ())), preferred_element_type=F32)  67.5 us
    dot_general x3, matrix products, project(): return jnp.dot(a, w, preferred_element_type=F32).astype(BF16)  34.5 us
  transfers between devices with their start and end apart: 4, of which 2 were waited for; matrix products, arithmetic and copies ran while one was open for 12% of the time, Pallas kernels for 47%

profile of v1, /device:TPU:97, one launch (start us, length us, event | category | flops | bytes accessed | tf_op | source)
XLA Modules:
  0.0 763.1 jit_solution(11118840306756033006)
XLA Ops:
  8.0 85.9 %all-gather.3.cloned.1.call-done = bf16[1024,4096]{1,0:T(8,128)(2,1)} async-done(((bf16[256,4096]{1,0:T(8,128)(2,1)}), bf16[1024,4096]{1,0:T(8,128)(2,1)}) %all-gather.3.cloned.1.call-update) | async-done | bytes 8388624 | tf_op jit(solution)/shard_map/all_gather | solution.py:309
  94.1 13.8 %convolution_convert_fusion.1.refs_2_ = bf16[1024,1024]{1,0:T(8,128)(2,1)S(1)} fusion(bf16[1024,4096]{1,0:T(8,128)(2,1)} %all-gather.3.cloned.1.call-done, bf16[4096,1024]{1,0:T(8,128)(2,1)} %param.10), kind=kOutput, calls=%fused_computation.2 | convolution fusion | flops 8590983168 | bytes 18874368 | tf_op jit(solution)/shard_map/dot_general | solution.py:301
  107.9 11.7 %convolution_convert_fusion.2.refs_1_ = bf16[1024,1024]{1,0:T(8,128)(2,1)S(1)} fusion(bf16[1024,4096]{1,0:T(8,128)(2,1)S(1)} %copy-done.10, bf16[4096,1024]{1,0:T(8,128)(2,1)} %param.9), kind=kOutput, calls=%fused_computation.3 | convolution fusion | flops 8590983168 | bytes 18874368 | tf_op jit(solution)/shard_map/dot_general | solution.py:301
  119.7 9.0 %convolution_convert_fusion.3.refs_0_ = bf16[1024,1024]{1,0:T(8,128)(2,1)S(1)} fusion(bf16[1024,4096]{1,0:T(8,128)(2,1)S(1)} %copy-done.10, bf16[4096,1024]{1,0:T(8,128)(2,1)S(1)} %bitcast.19), kind=kOutput, calls=%fused_computation.4 | convolution fusion | flops 8590983168 | bytes 18874368 | tf_op jit(solution)/shard_map/dot_general | solution.py:301
  128.7 73.4 %exchange_to_heads.2 = (bf16[8192,128]{1,0:T(8,128)(2,1)S(1)}, bf16[8192,128]{1,0:T(8,128)(2,1)S(1)}, bf16[8192,128]{1,0:T(8,128)(2,1)S(1)}) custom-call(bf16[1024,1024]{1,0:T(8,128)(2,1)S(1)} %convolution_convert_fusion.3.refs_0_, bf16[1024,1024]{1,0:T(8,128)(2,1)S(1)} %convolution_convert_fusion.2.refs_1_, ...), custom_call_target="tpu_custom_call" | custom-call | flops 5505024000 | bytes 11010048 | tf_op jit(solution)/shard_map/exchange_to_heads/pallas_call | solution.py:283
  204.7 69.8 %attn_fwd.1 = (bf16[8192,128]{1,0:T(8,128)(2,1)S(1)}, f32[16,8,512]{2,1,0:T(8,128)S(1)}) custom-call(bf16[8192,128]{1,0:T(8,128)(2,1)S(1)} %get-tuple-element.21.q_ref, bf16[8192,128]{1,0:T(8,128)(2,1)} %copy-done.4, bf16[8192,128]{1,0:T(8,128)(2,1)} %copy-done.5), custom_call_target="tpu_custom_call" | custom-call | flops 17179869184 | bytes 8388608 | tf_op jit(solution)/shard_map/attn_fwd/pallas_call | solution.py:101
  274.5 1.3 copy-done.3
  276.6 26.6 %exchange_to_rows.2 = bf16[1024,1024]{1,0:T(8,128)(2,1)S(1)} custom-call(bf16[8192,128]{1,0:T(8,128)(2,1)S(1)} %get-tuple-element.26.refs_0_.o_ref), custom_call_target="tpu_custom_call" | custom-call | flops 1835008000 | bytes 3670016 | tf_op jit(solution)/shard_map/exchange_to_rows/pallas_call | solution.py:283
  303.2 15.1 %convolution_convert_fusion.refs_0_ = bf16[1024,1024]{1,0:T(8,128)(2,1)} fusion(bf16[1024,4096]{1,0:T(8,128)(2,1)} %all-gather.5.cloned.1.call-done, bf16[1024,4096]{1,0:T(8,128)(2,1)} %param.11), kind=kOutput, calls=%fused_computation.1 | convolution fusion | flops 8590983168 | bytes 18874368 | tf_op jit(solution)/shard_map/dot_general | solution.py:14
  318.3 11.6 %fusion = f32[1024,4096]{1,0:T(8,128)} fusion(bf16[1024,1024]{1,0:T(8,128)(2,1)S(1)} %exchange_to_rows.2, bf16[1024,4096]{1,0:T(8,128)(2,1)S(1)} %bitcast.17), kind=kOutput, calls=%fused_computation.5 | convolution fusion | flops 8589934592 | bytes 27262976 | tf_op jit(solution)/shard_map/dot_general | solution.py:317
  330.1 1.5 copy-done.1
  331.5 27.1 %exchange_to_heads.3.do_ref = bf16[8192,128]{1,0:T(8,128)(2,1)S(1)} custom-call(bf16[1024,1024]{1,0:T(8,128)(2,1)S(1)} %copy-done.1), custom_call_target="tpu_custom_call" | custom-call | flops 1835008000 | bytes 3670016 | tf_op jit(solution)/shard_map/exchange_to_heads/pallas_call | solution.py:283
  358.6 1.4 copy-done.2
  360.0 117.8 %attn_bwd.1 = (bf16[8192,128]{1,0:T(8,128)(2,1)}, bf16[8192,128]{1,0:T(8,128)(2,1)}, bf16[8192,128]{1,0:T(8,128)(2,1)}) custom-call(bf16[8192,128]{1,0:T(8,128)(2,1)} %copy-done.3, bf16[8192,128]{1,0:T(8,128)(2,1)} %copy-done.4, bf16[8192,128]{1,0:T(8,128)(2,1)} %copy-done.5, bf16[8192,128]{1,0:T(8,128)(2,1)} %copy-done.2, bf16[8192,128]{1,0:T(8,128)(2,1)} %copy-done, ...), custom_call_target="tpu_custom_call" | custom-call | flops 42949672960 | bytes 16777216 | tf_op jit(solution)/shard_map/attn_bwd/pallas_call | solution.py:198
  477.7 1.6 copy-done.6
  479.3 1.6 copy-done.7
  480.9 1.6 copy-done.8
  482.5 72.4 %exchange_to_rows.3 = (bf16[1024,1024]{1,0:T(8,128)(2,1)S(1)}, bf16[1024,1024]{1,0:T(8,128)(2,1)S(1)}, bf16[1024,1024]{1,0:T(8,128)(2,1)S(1)}) custom-call(bf16[8192,128]{1,0:T(8,128)(2,1)S(1)} %copy-done.6, bf16[8192,128]{1,0:T(8,128)(2,1)S(1)} %copy-done.7, bf16[8192,128]{1,0:T(8,128)(2,1)S(1)} %copy-done.8), custom_call_target="tpu_custom_call" | custom-call | flops 5505024000 | bytes 11010048 | tf_op jit(solution)/shard_map/exchange_to_rows/pallas_call | solution.py:283
  554.9 14.5 %fusion.1 = f32[1024,4096]{1,0:T(8,128)} fusion(bf16[1024,1024]{1,0:T(8,128)(2,1)S(1)} %get-tuple-element.33, bf16[4096,1024]{1,0:T(8,128)(2,1)} %param.8), kind=kOutput, calls=%fused_computation.6 | convolution fusion | flops 8589934592 | bytes 27262976 | tf_op jit(solution)/shard_map/dot_general | solution.py:14
  569.4 14.5 %fusion.2 = f32[1024,4096]{1,0:T(8,128)} fusion(bf16[1024,1024]{1,0:T(8,128)(2,1)S(1)} %get-tuple-element.34, bf16[4096,1024]{1,0:T(8,128)(2,1)} %param.9), kind=kOutput, calls=%fused_computation.7 | convolution fusion | flops 8589934592 | bytes 27262976 | tf_op jit(solution)/shard_map/dot_general | solution.py:14
  583.8 23.5 %add_add_fusion = f32[1024,4096]{1,0:T(8,128)} fusion(f32[1024,4096]{1,0:T(8,128)} %fusion.1, f32[1024,4096]{1,0:T(8,128)} %fusion.2, bf16[1024,1024]{1,0:T(8,128)(2,1)S(1)} %get-tuple-element.35, bf16[4096,1024]{1,0:T(8,128)(2,1)} %param.10), kind=kOutput, calls=%fused_computation | convolution fusion | flops 8598323200 | bytes 60817408 | tf_op jit(solution)/shard_map/dot_general | solution.py:14
  607.4 3.8 convert_element_type.22
  611.2 141.5 %reduce-scatter.5.cloned.1.call-done = f32[256,4096]{1,0:T(8,128)} async-done(((f32[1024,4096]{1,0:T(8,128)}), f32[256,4096]{1,0:T(8,128)}) %reduce-scatter.5.cloned.1.call-update) | async-done | bytes 4194320 | tf_op jit(solution)/shard_map/reduce_scatter | solution.py:324
  752.8 3.8 convert_element_type.23
  (36 shorter events, 4.6 us)
Async XLA Ops:
  7.2 86.8 %all-gather.3.cloned.1.call-start = ((), (), s32[]{:S(2)}) async-start(), calls=%async_computation.2 | async-start | bytes 10485760 | tf_op jit(solution)/shard_map/all_gather | solution.py:309
  8.0 268.6 %all-gather.5.cloned.1.call-start = ((), (), s32[]{:S(2)}) async-start(), calls=%async_computation.3 | async-start | bytes 10485760 | tf_op jit(solution)/shard_map/all_gather | solution.py:311
  94.0 513.4 %reduce-scatter.3.cloned.1.call-start = ((), (), s32[]{:S(2)}) async-start(), calls=%async_computation.4 | async-start | bytes 20971520 | tf_op jit(solution)/shard_map/reduce_scatter | solution.py:319
  94.1 13.8 %copy-start.10 = (bf16[1024,4096]{1,0:T(8,128)(2,1)S(1)}, bf16[1024,4096]{1,0:T(8,128)(2,1)}, u32[]{:S(2)}) copy-start(bf16[1024,4096]{1,0:T(8,128)(2,1)} %all-gather.3.cloned.1.call-done) | copy-start | bytes 25165828
  94.1 25.6 %slice-start.2 = ((s8[8388608]{0:T(1024)(128)(4,1)}), s8[4194304]{0:T(1024)(128)(4,1)S(1)}, s32[]{:S(2)}) async-start(s8[8388608]{0:T(1024)(128)(4,1)} %bitcast.18), calls=%async_computation.8 | async-start | bytes 8388608
  107.9 11.8 %slice-start.3 = ((s8[8388608]{0:T(1024)(128)(4,1)}), s8[4194304]{0:T(1024)(128)(4,1)S(1)}, s32[]{:S(2)}) async-start(s8[8388608]{0:T(1024)(128)(4,1)} %bitcast.18), calls=%async_computation.9 | async-start | bytes 8388608
  202.1 1.3 copy-start.4
  203.4 1.3 copy-start.5
  274.5 1.3 copy-start.3
  275.9 0.7 copy-start.9
  276.6 41.7 %copy-start = (bf16[8192,128]{1,0:T(8,128)(2,1)}, bf16[8192,128]{1,0:T(8,128)(2,1)S(1)}, u32[]{:S(2)}) copy-start(bf16[8192,128]{1,0:T(8,128)(2,1)S(1)} %get-tuple-element.26.refs_0_.o_ref) | copy-start | bytes 6291460
  276.6 41.7 %slice-start = ((s8[8388608]{0:T(1024)(128)(4,1)}), s8[4194304]{0:T(1024)(128)(4,1)S(1)}, s32[]{:S(2)}) async-start(s8[8388608]{0:T(1024)(128)(4,1)} %bitcast.16), calls=%async_computation.6 | async-start | bytes 8388608
  303.2 15.1 %slice-start.1 = ((s8[8388608]{0:T(1024)(128)(4,1)}), s8[4194304]{0:T(1024)(128)(4,1)S(1)}, s32[]{:S(2)}) async-start(s8[8388608]{0:T(1024)(128)(4,1)} %bitcast.16), calls=%async_computation.7 | async-start | bytes 8388608
  329.9 1.6 copy-start.1
  330.0 422.8 %reduce-scatter.5.cloned.1.call-start = ((), (), s32[]{:S(2)}) async-start(), calls=%async_computation.5 | async-start | bytes 20971520 | tf_op jit(solution)/shard_map/reduce_scatter | solution.py:324
  358.6 1.4 copy-start.2
  477.7 1.6 copy-start.6
  479.3 1.6 copy-start.7
  480.9 1.6 copy-start.8
Sparse Core Ops, SparseCore 0:
  9.6 84.3 all-gather.2
  95.5 81.4 all-gather.4
  330.1 145.3 reduce-scatter.2
  607.5 145.1 reduce-scatter.4

commit v2 on v0

v2 whole, which is shorter than its diff:
```python
import functools
import math

import jax
import jax.numpy as jnp
from jax import lax
from jax.experimental import pallas as pl
from jax.experimental.pallas import tpu as pltpu
from jax.sharding import PartitionSpec as P

HEAD_DIM = 128
F32, BF16 = jnp.float32, jnp.bfloat16
LOG2E = math.log2(math.e)
MESH = pl.DeviceIdType.MESH
ANYWHERE = pl.BlockSpec(memory_space=pltpu.HBM)
DMA = pltpu.SemaphoreType.DMA


def dot_nt(a, b):
    return lax.dot_general(a, b, (((1,), (1,)), ((), ())), preferred_element_type=F32)


def dot_nn(a, b):
    return lax.dot_general(a, b, (((1,), (0,)), ((), ())), preferred_element_type=F32)


def rows_at(start, size):
    return pl.ds(pl.multiple_of(start, size), size)


def ring(axis, size):
    me = lax.axis_index(axis)
    return me, lax.rem(me + 1, size), lax.rem(me + size - 1, size)


def meet(cp_size, tp_size, use_cp, use_tp):
    barrier = pltpu.get_barrier_semaphore()
    count = 0
    if use_cp:
        me = lax.axis_index('cp')
        for d in range(1, cp_size):
            pl.semaphore_signal(barrier, inc=1, device_id={'cp': lax.rem(me + d, cp_size)}, device_id_type=MESH)
        count += cp_size - 1
    if use_tp:
        _, right, left = ring('tp', tp_size)
        for peer in (right, left):
            pl.semaphore_signal(barrier, inc=1, device_id={'tp': peer}, device_id_type=MESH)
        count += 2
    pl.semaphore_wait(barrier, count)


def params(collective_id):
    return pltpu.CompilerParams(collective_id=collective_id, has_side_effects=True, vmem_limit_bytes=63 << 20)


def far_first(cp_size):
    return sorted(range(1, cp_size), key=lambda d: -min(d, cp_size - d))


def group_rows(tp_size):
    me, right, left = ring('tp', tp_size)
    far = lax.rem(me + 2, tp_size)
    return ((me, 0), (me, 1)), ((right, 0), (left, 1)), ((right, 1), (left, 0)), ((far, 0), (far, 1))


def position(cp_size, tp_size, block, owner, half):
    piece = block * tp_size // 2
    first = owner < tp_size // 2
    cp_rank = lax.axis_index('cp')
    piece_id = jnp.where(first, cp_rank, 2 * cp_size - 1 - cp_rank)
    return piece_id * piece + jnp.where(first, owner, owner - tp_size // 2) * block + half * (block // 2)


class HeadSender:
    def __init__(self, cp_size, tp_size, res, dst, send, recv, local):
        self.cp_size, self.tp_size = cp_size, tp_size
        self.res, self.dst, self.sems = res, dst, (send, recv, local)
        self.copies = []

    def start(self, g):
        send, recv, local = self.sems
        me = lax.axis_index('cp')
        block = self.res.shape[3]
        for half, (owner, part) in enumerate(group_rows(self.tp_size)[g]):
            rows = rows_at(position(self.cp_size, self.tp_size, block, owner, part), block // 2)
            here = pl.ds(half * (block // 2), block // 2)
            for d in far_first(self.cp_size):
                peer = lax.rem(me + d, self.cp_size)
                copy = pltpu.make_async_remote_copy(
                    src_ref=self.res.at[g, peer, :, here, :], dst_ref=self.dst.at[:, rows, :],
                    send_sem=send.at[d - 1, g, half], recv_sem=recv.at[d - 1, g, half],
                    device_id={'cp': peer}, device_id_type=MESH)
                copy.start()
                self.copies.append(copy)
            copy = pltpu.make_async_copy(self.res.at[g, me, :, here, :], self.dst.at[:, rows, :], local.at[g, half])
            copy.start()
            self.copies.append(copy)

    def wait(self):
        for copy in self.copies:
            copy.wait()


def head_scratch(cp_size, arrays, block):
    return [
        pltpu.VMEM((4, cp_size, arrays, block, HEAD_DIM), BF16),
        DMA((cp_size - 1, 4, 2)),
        DMA((cp_size - 1, 4, 2)),
        DMA((4, 2)),
    ]


def project_kernel(cp_size, tp_size, x_ref, dy_ref, wq_ref, wk_ref, wv_ref, qkv_ref, dy1_ref, w_v, xg, res, send, recv, local, w_sem, x_sem, y_send, y_recv):
    block = x_ref.shape[0]
    half = block // 2
    low, high = pl.ds(0, half), pl.ds(half, half)
    _, right, left = ring('tp', tp_size)
    heads = HeadSender(cp_size, tp_size, res, qkv_ref, send, recv, local)

    def pass_on(k, src, dst, peer):
        copy = pltpu.make_async_remote_copy(
            src_ref=src, dst_ref=dst, send_sem=y_send.at[k], recv_sem=y_recv.at[k], device_id={'tp': peer}, device_id_type=MESH)
        copy.start()
        return copy

    own = pltpu.make_async_copy(x_ref, xg.at[0], x_sem)
    own.start()
    loads = [pltpu.make_async_copy(w, w_v.at[n], w_sem.at[n]) for n, w in enumerate((wq_ref, wk_ref, wv_ref))]
    meet(cp_size, tp_size, True, True)
    hops = [
        pass_on(0, x_ref.at[low, :], xg.at[1, low, :], left),
        pass_on(1, x_ref.at[high, :], xg.at[1, high, :], right),
        pass_on(2, x_ref.at[high, :], xg.at[2, low, :], left),
        pass_on(3, x_ref.at[low, :], xg.at[2, high, :], right),
    ]
    for load in loads:
        load.start()
    own.wait()

    wide = min(4, cp_size)
    cols = wide * HEAD_DIM
    steps = cp_size // wide

    def compute(g, n):
        def body(s, _):
            out = dot_nn(xg[g], w_v[n, :, rows_at(s * cols, cols)]).astype(BF16)
            for k in range(wide):
                res[g, wide * s + k, n] = out[:, k * HEAD_DIM:(k + 1) * HEAD_DIM]
            return 0

        lax.fori_loop(0, steps, body, 0)

    for n in range(3):
        loads[n].wait()
        compute(0, n)
    heads.start(0)
    hops[0].wait_recv()
    hops.append(pass_on(4, xg.at[1, low, :], xg.at[3, low, :], left))
    hops[1].wait_recv()
    hops.append(pass_on(5, xg.at[1, high, :], xg.at[3, high, :], right))
    hops.append(pass_on(6, dy_ref.at[low, :], dy1_ref.at[low, :], left))
    hops.append(pass_on(7, dy_ref.at[high, :], dy1_ref.at[high, :], right))
    for g, arrived in ((1, ()), (2, (2, 3)), (3, (4, 5))):
        for k in arrived:
            hops[k].wait_recv()
        for n in range(3):
            compute(g, n)
        heads.start(g)
    for k in range(6):
        hops[k].wait_send()
    for k in (6, 7):
        hops[k].wait()
    heads.wait()


def project(x_blk, dy_blk, weights, cp_size, tp_size):
    block, width = x_blk.shape
    cols = weights[0].shape[1]
    seq = block * tp_size * cp_size
    return pl.pallas_call(
        functools.partial(project_kernel, cp_size, tp_size),
        out_shape=(jax.ShapeDtypeStruct((3, seq, HEAD_DIM), BF16), jax.ShapeDtypeStruct((block, width), BF16)),
        in_specs=[ANYWHERE] * 5,
        out_specs=(ANYWHERE, ANYWHERE),
        scratch_shapes=[pltpu.VMEM((3, width, cols), BF16), pltpu.VMEM((4, block, width), BF16)] + head_scratch(cp_size, 3, block) + [
            DMA((3,)), DMA, DMA((8,)), DMA((8,))],
        compiler_params=params(0),
        cost_estimate=pl.CostEstimate(flops=6 * block * tp_size * width * cols, bytes_accessed=6 * width * cols, transcendentals=0),
        name="project_qkv",
    )(x_blk, dy_blk, *weights)


def send_piece(cp_size, i, src, dst_of, send, recv, local, start):
    me = lax.axis_index('cp')
    half = jnp.where(i < cp_size, 0, 1)
    owner = jnp.where(i < cp_size, i, 2 * cp_size - 1 - i)

    @pl.when(owner == me)
    def _():
        copy = pltpu.make_async_copy(src, dst_of(half, me), local.at[half])
        copy.start() if start else copy.wait()

    @pl.when(owner != me)
    def _():
        copy = pltpu.make_async_remote_copy(
            src_ref=src, dst_ref=dst_of(half, me), send_sem=send.at[i], recv_sem=recv.at[me, half],
            device_id={'cp': owner}, device_id_type=MESH)
        copy.start() if start else copy.wait_send()


def wait_pieces(cp_size, src_of, dst_of, send, recv, local):
    me = lax.axis_index('cp')

    def sent(i, _):
        send_piece(cp_size, i, src_of(i), dst_of, send, recv, local, False)
        return 0

    lax.fori_loop(0, 2 * cp_size, sent, 0)
    for d in range(1, cp_size):
        peer = lax.rem(me + d, cp_size)
        for half in range(2):
            pltpu.make_async_remote_copy(
                src_ref=src_of(0), dst_ref=dst_of(half, peer), send_sem=send.at[0], recv_sem=recv.at[peer, half],
                device_id={'cp': peer}, device_id_type=MESH).wait_recv()


def forward_kernel(cp_size, tp_size, qkv_ref, dy_ref, dy1_ref, o_ref, l_ref, rows_ref, dy23_ref,
                   qkv, o_v, l_v, vt_ref, s_ref, acc_ref, in_sem, send, recv, local, y_send, y_recv, out_sem):
    seq = qkv.shape[1]
    bq = s_ref.shape[0]
    nblk = seq // bq
    c = HEAD_DIM ** -0.5 * LOG2E
    _, right, left = ring('tp', tp_size)
    half = dy_ref.shape[0] // 2
    low, high = pl.ds(0, half), pl.ds(half, half)

    load = pltpu.make_async_copy(qkv_ref, qkv, in_sem)
    load.start()
    meet(cp_size, tp_size, True, True)
    hops = []
    for k, (src, dst, peer) in enumerate((
            (dy_ref.at[high, :], dy23_ref.at[0, low, :], left),
            (dy_ref.at[low, :], dy23_ref.at[0, high, :], right),
            (dy1_ref.at[low, :], dy23_ref.at[1, low, :], left),
            (dy1_ref.at[high, :], dy23_ref.at[1, high, :], right))):
        hop = pltpu.make_async_remote_copy(
            src_ref=src, dst_ref=dst, send_sem=y_send.at[k], recv_sem=y_recv.at[k], device_id={'tp': peer}, device_id_type=MESH)
        hop.start()
        hops.append(hop)
    load.wait()

    def transpose_step(b, _):
        rows = rows_at(b * bq, bq)
        vt_ref[:, rows] = qkv[2, rows, :].T
        return 0

    lax.fori_loop(0, nblk, transpose_step, 0)

    def src_of(i):
        return o_v.at[rows_at(i * bq, bq), :]

    def dst_of(part, head):
        return rows_ref.at[rows_at(part * bq, bq), rows_at(head * HEAD_DIM, HEAD_DIM)]

    def q_step(i, _):
        rows = rows_at(i * bq, bq)
        q = qkv[0, rows, :]
        acc_ref[...] = jnp.zeros_like(acc_ref)
        s = dot_nt(qkv[1, rows, :], q)
        kk = lax.broadcasted_iota(jnp.int32, (bq, bq), 0)
        qq = lax.broadcasted_iota(jnp.int32, (bq, bq), 1)
        s = jnp.where(kk <= qq, s, -jnp.inf)
        s_ref[...] = s
        first = jnp.max(s, axis=0, keepdims=True)

        def use(blk, m_old, m, l, following):
            mc = m * c
            alpha = jnp.exp2(m_old * c - mc)
            p = jnp.exp2(s_ref[...] * c - mc)
            m_new = m
            if following is not None:
                s = dot_nt(qkv[1, rows_at(following * bq, bq), :], q)
            part = jnp.sum(p, axis=0, keepdims=True)
            out = dot_nn(vt_ref[:, rows_at(blk * bq, bq)], p.astype(BF16))
            if following is not None:
                m_new = jnp.maximum(m, jnp.max(s, axis=0, keepdims=True))
                s_ref[...] = s
            acc_ref[...] = acc_ref[...] * alpha + out
            return m, m_new, l * alpha + part

        def body(t, carry):
            return use(jnp.where(t == 0, i, t - 1), *carry, t)

        carry = lax.fori_loop(0, i, body, (first, first, jnp.zeros((1, bq), F32)))
        m, _, l = use(jnp.where(i == 0, i, i - 1), *carry, None)
        o_v[rows, :] = (acc_ref[...] * (1.0 / l)).T.astype(BF16)
        l_v[i] = jnp.broadcast_to(m * c + jnp.log2(l), (8, bq))
        send_piece(cp_size, i, src_of(i), dst_of, send, recv, local, True)
        return 0

    lax.fori_loop(0, nblk, q_step, 0)
    out_o = pltpu.make_async_copy(o_v, o_ref, out_sem.at[0])
    out_l = pltpu.make_async_copy(l_v, l_ref, out_sem.at[1])
    out_o.start()
    out_l.start()
    wait_pieces(cp_size, src_of, dst_of, send, recv, local)
    for hop in hops:
        hop.wait()
    out_o.wait()
    out_l.wait()


def forward(qkv, dy_blk, dy1, cp_size, tp_size):
    seq = qkv.shape[1]
    bq = seq // (2 * cp_size)
    block, width = dy_blk.shape
    pairs = seq * seq // 2
    return pl.pallas_call(
        functools.partial(forward_kernel, cp_size, tp_size),
        out_shape=(
            jax.ShapeDtypeStruct((seq, HEAD_DIM), BF16),
            jax.ShapeDtypeStruct((seq // bq, 8, bq), F32),
            jax.ShapeDtypeStruct((2 * bq, cp_size * HEAD_DIM), BF16),
            jax.ShapeDtypeStruct((2, block, width), BF16),
        ),
        in_specs=[ANYWHERE] * 3,
        out_specs=(ANYWHERE,) * 4,
        scratch_shapes=[
            pltpu.VMEM((3, seq, HEAD_DIM), BF16),
            pltpu.VMEM((seq, HEAD_DIM), BF16),
            pltpu.VMEM((seq // bq, 8, bq), F32),
            pltpu.VMEM((HEAD_DIM, seq), BF16),
            pltpu.VMEM((bq, bq), F32),
            pltpu.VMEM((HEAD_DIM, bq), F32),
            DMA, DMA((2 * cp_size,)), DMA((cp_size, 2)), DMA((2,)), DMA((4,)), DMA((4,)), DMA((2,)),
        ],
        compiler_params=params(1),
        cost_estimate=pl.CostEstimate(flops=4 * pairs * HEAD_DIM, bytes_accessed=8 * seq * HEAD_DIM, transcendentals=pairs),
        name="attention_forward",
    )(qkv, dy_blk, dy1)


def middle_kernel(cp_size, tp_size, dy_ref, dy1_ref, dy23_ref, wo_ref, rows_ref, do_ref, y_ref,
                  dyg, wo, o_v, y_v, res, send, recv, local, in_sem, y_sem):
    block = dy_ref.shape[0]
    heads = HeadSender(cp_size, tp_size, res, do_ref, send, recv, local)
    loads = [
        pltpu.make_async_copy(wo_ref, wo, in_sem.at[0]),
        pltpu.make_async_copy(dy_ref, dyg.at[0], in_sem.at[1]),
        pltpu.make_async_copy(dy1_ref, dyg.at[1], in_sem.at[2]),
        pltpu.make_async_copy(dy23_ref, dyg.at[pl.ds(2, 2)], in_sem.at[3]),
        pltpu.make_async_copy(rows_ref, o_v, in_sem.at[4]),
    ]
    for load in loads:
        load.start()
    meet(cp_size, tp_size, True, False)
    per_step = min(4, cp_size)
    cols = per_step * HEAD_DIM
    loads[0].wait()
    for g in range(4):
        if g < 3:
            loads[g + 1].wait()

        def body(s, _):
            out = dot_nt(dyg[g], wo[rows_at(s * cols, cols), :]).astype(BF16)
            for k in range(per_step):
                res[g, per_step * s + k, 0] = out[:, k * HEAD_DIM:(k + 1) * HEAD_DIM]
            return 0

        lax.fori_loop(0, wo.shape[0] // cols, body, 0)
        heads.start(g)
    loads[4].wait()
    wide = y_v.shape[2]
    count = wo.shape[1] // wide

    def put(s, slot):
        return pltpu.make_async_copy(y_v.at[slot], y_ref.at[:, rows_at(s * wide, wide)], y_sem.at[slot])

    def y_step(s, _):
        slot = lax.rem(s, 2)

        @pl.when(s >= 2)
        def _():
            put(s - 2, slot).wait()

        y_v[slot] = dot_nn(o_v[...], wo[:, rows_at(s * wide, wide)])
        put(s, slot).start()
        return 0

    lax.fori_loop(0, count, y_step, 0)
    for s in range(count - 2, count):
        put(s, s % 2).wait()
    heads.wait()


def middle(dy_blk, dy1, dy23, w_out, o_rows, cp_size, tp_size):
    block, width = dy_blk.shape
    cols = w_out.shape[0]
    rows = block * tp_size
    wide = width // 8
    return pl.pallas_call(
        functools.partial(middle_kernel, cp_size, tp_size),
        out_shape=(jax.ShapeDtypeStruct((1, rows * cp_size, HEAD_DIM), BF16), jax.ShapeDtypeStruct((rows, width), F32)),
        in_specs=[ANYWHERE] * 5,
        out_specs=(ANYWHERE, ANYWHERE),
        scratch_shapes=[
            pltpu.VMEM((4, block, width), BF16),
            pltpu.VMEM((cols, width), BF16),
            pltpu.VMEM((rows, cols), BF16),
            pltpu.VMEM((2, rows, wide), F32),
        ] + head_scratch(cp_size, 1, block) + [DMA((5,)), DMA((2,))],
        compiler_params=params(2),
        cost_estimate=pl.CostEstimate(flops=4 * rows * width * cols, bytes_accessed=8 * rows * width, transcendentals=0),
        name="project_middle",
    )(dy_blk, dy1, dy23, w_out, o_rows)


def backward_kernel(cp_size, qkv_ref, do_ref, o_ref, l_ref, rows_ref,
                    qkv, do_v, o_v, l_v, kt_ref, p_ref, ds_ref, dqt_ref, dk_acc, dv_acc, grads, in_sem, send, recv, local):
    seq = qkv.shape[1]
    bq = p_ref.shape[0]
    nblk = seq // bq
    sub = bq // 2
    scale = HEAD_DIM ** -0.5
    c = scale * LOG2E
    loads = [
        pltpu.make_async_copy(qkv_ref, qkv, in_sem.at[0]),
        pltpu.make_async_copy(do_ref.at[0], do_v, in_sem.at[1]),
        pltpu.make_async_copy(o_ref, o_v, in_sem.at[2]),
        pltpu.make_async_copy(l_ref, l_v, in_sem.at[3]),
    ]
    for load in loads:
        load.start()
    meet(cp_size, 0, True, False)
    for load in loads:
        load.wait()

    def init_step(b, _):
        rows = rows_at(b * bq, bq)
        kt_ref[:, rows] = qkv[1, rows, :].T
        dk_acc[rows, :] = jnp.zeros((bq, HEAD_DIM), F32)
        dv_acc[rows, :] = jnp.zeros((bq, HEAD_DIM), F32)
        return 0

    lax.fori_loop(0, nblk, init_step, 0)

    def src_of(i):
        return grads.at[:, rows_at(i * bq, bq), :]

    def dst_of(part, head):
        return rows_ref.at[:, rows_at(part * bq, bq), rows_at(head * HEAD_DIM, HEAD_DIM)]

    def q_step(back, _):
        i = nblk - 1 - back
        rows = rows_at(i * bq, bq)
        q = qkv[0, rows, :]
        do = do_v[rows, :]
        prod = do.astype(F32) * o_v[rows, :].astype(F32)
        delta = jnp.sum(prod.T, axis=0, keepdims=True)
        lse = l_v[i][0:1, :]
        dqt_ref[...] = jnp.zeros_like(dqt_ref)

        def make(blk, r, masked):
            krows = rows_at(blk * bq + r * sub, sub)
            s = dot_nt(qkv[1, krows, :], q)
            dp = dot_nt(qkv[2, krows, :], do)
            p = jnp.exp2(s * c - lse)
            if masked:
                kk = lax.broadcasted_iota(jnp.int32, (sub, bq), 0) + r * sub
                qq = lax.broadcasted_iota(jnp.int32, (sub, bq), 1)
                p = jnp.where(kk <= qq, p, 0.0)
            pb = p.astype(BF16)
            ds = (pb.astype(F32) * (dp - delta)).astype(BF16)
            return pb, ds

        def flush(blk, r):
            krows = rows_at(blk * bq + r * sub, sub)
            sl = slice(r * sub, (r + 1) * sub)
            ds = ds_ref[sl, :]
            dv_acc[krows, :] += dot_nn(p_ref[sl, :], do)
            dk_acc[krows, :] += dot_nn(ds, q)
            return dot_nn(kt_ref[:, krows], ds)

        for r in range(2):
            sl = slice(r * sub, (r + 1) * sub)
            p_ref[sl, :], ds_ref[sl, :] = make(i, r, True)

        def body(t, _):
            cur = jnp.where(t == 0, i, t - 1)
            out = None
            for r in range(2):
                sl = slice(r * sub, (r + 1) * sub)
                d = flush(cur, r)
                out = d if out is None else out + d
                p_ref[sl, :], ds_ref[sl, :] = make(t, r, False)
            dqt_ref[...] += out
            return 0

        lax.fori_loop(0, i, body, 0)
        cur = jnp.where(i == 0, i, i - 1)
        out = flush(cur, 0) + flush(cur, 1)
        grads[0, rows, :] = ((dqt_ref[...] + out) * scale).T.astype(BF16)
        grads[1, rows, :] = (dk_acc[rows, :] * scale).astype(BF16)
        grads[2, rows, :] = dv_acc[rows, :].astype(BF16)
        send_piece(cp_size, i, src_of(i), dst_of, send, recv, local, True)
        return 0

    lax.fori_loop(0, nblk, q_step, 0)
    wait_pieces(cp_size, src_of, dst_of, send, recv, local)


def backward(qkv, do, o, lse, cp_size):
    seq = qkv.shape[1]
    bq = seq // (2 * cp_size)
    pairs = seq * seq // 2
    return pl.pallas_call(
        functools.partial(backward_kernel, cp_size),
        out_shape=jax.ShapeDtypeStruct((3, 2 * bq, cp_size * HEAD_DIM), BF16),
        in_specs=[ANYWHERE] * 4,
        out_specs=ANYWHERE,
        scratch_shapes=[
            pltpu.VMEM((3, seq, HEAD_DIM), BF16),
            pltpu.VMEM((seq, HEAD_DIM), BF16),
            pltpu.VMEM((seq, HEAD_DIM), BF16),
            pltpu.VMEM((seq // bq, 8, bq), F32),
            pltpu.VMEM((HEAD_DIM, seq), BF16),
            pltpu.VMEM((bq, bq), BF16),
            pltpu.VMEM((bq, bq), BF16),
            pltpu.VMEM((HEAD_DIM, bq), F32),
            pltpu.VMEM((seq, HEAD_DIM), F32),
            pltpu.VMEM((seq, HEAD_DIM), F32),
            pltpu.VMEM((3, seq, HEAD_DIM), BF16),
            DMA((4,)), DMA((2 * cp_size,)), DMA((cp_size, 2)), DMA((2,)),
        ],
        compiler_params=params(3),
        cost_estimate=pl.CostEstimate(flops=10 * pairs * HEAD_DIM, bytes_accessed=16 * seq * HEAD_DIM, transcendentals=pairs),
        name="attention_backward",
    )(qkv, do, o, lse)


def reduce_kernel(tp_size, chunks, rows_ref, wq_ref, wk_ref, wv_ref, out_ref,
                  g_v, w_v, part, mid, last, out_v, in_sem, w_sem, out_sem, sends, recvs):
    me, right, left = ring('tp', tp_size)
    far = lax.rem(me + 2, tp_size)
    block = part.shape[1]
    half = block // 2
    low, high = pl.ds(0, half), pl.ds(half, half)
    wide = part.shape[2] // chunks
    weights = (wq_ref, wk_ref, wv_ref)

    def w_load(n, a):
        return pltpu.make_async_copy(weights[a].at[rows_at(n * wide, wide), :], w_v.at[lax.rem(n, 2), a], w_sem.at[lax.rem(n, 2), a])

    load = pltpu.make_async_copy(rows_ref, g_v, in_sem)
    load.start()
    for a in range(3):
        w_load(0, a).start()
    meet(0, tp_size, False, True)

    def hop(kind, n):
        cols = rows_at(n * wide, wide)
        src, dst, peer = {
            'far_r': (part.at[0, low, cols], mid.at[0, :, cols], right),
            'far_l': (part.at[0, high, cols], mid.at[1, :, cols], left),
            'plain_r': (part.at[1, high, cols], last.at[0, high, cols], right),
            'plain_l': (part.at[2, low, cols], last.at[1, low, cols], left),
            'sum_r': (part.at[1, low, cols], last.at[0, low, cols], right),
            'sum_l': (part.at[2, high, cols], last.at[1, high, cols], left),
        }[kind]
        k = ('far_r', 'far_l', 'plain_r', 'plain_l', 'sum_r', 'sum_l').index(kind)
        return pltpu.make_async_remote_copy(
            src_ref=src, dst_ref=dst, send_sem=sends.at[k, n], recv_sem=recvs.at[k, n], device_id={'tp': peer}, device_id_type=MESH)

    load.wait()
    owners = (far, right, left, me)

    def compute(n, _):
        slot = lax.rem(n, 2)

        @pl.when(n + 1 < chunks)
        def _():
            for a in range(3):
                w_load(n + 1, a).start()

        for a in range(3):
            w_load(n, a).wait()
        cols = rows_at(n * wide, wide)
        for k in range(4):
            rows = rows_at(owners[k] * block, block)
            total = dot_nt(g_v[0, rows, :], w_v[slot, 0])
            total = total + dot_nt(g_v[1, rows, :], w_v[slot, 1])
            part[k, :, cols] = total + dot_nt(g_v[2, rows, :], w_v[slot, 2])
        for kind in ('far_r', 'far_l', 'plain_r', 'plain_l'):
            hop(kind, n).start()
        return 0

    lax.fori_loop(0, chunks, compute, 0)

    def forward_sums(n, _):
        cols = rows_at(n * wide, wide)
        hop('far_r', n).wait_recv()
        part[1, :half, cols] += mid[0, :, cols]
        hop('sum_r', n).start()
        hop('far_l', n).wait_recv()
        part[2, half:, cols] += mid[1, :, cols]
        hop('sum_l', n).start()
        return 0

    lax.fori_loop(0, chunks, forward_sums, 0)

    def put(n):
        cols = rows_at(n * wide, wide)
        return pltpu.make_async_copy(out_v.at[:, cols], out_ref.at[:, cols], out_sem.at[n])

    def finish(n, _):
        cols = rows_at(n * wide, wide)
        for kind in ('plain_r', 'plain_l', 'sum_r', 'sum_l'):
            hop(kind, n).wait_recv()
        out_v[:, cols] = (part[3, :, cols] + last[0, :, cols] + last[1, :, cols]).astype(BF16)
        put(n).start()
        return 0

    lax.fori_loop(0, chunks, finish, 0)

    def close(n, _):
        put(n).wait()
        for kind in ('far_r', 'far_l', 'plain_r', 'plain_l', 'sum_r', 'sum_l'):
            hop(kind, n).wait_send()
        return 0

    lax.fori_loop(0, chunks, close, 0)


def reduce_out(grad_rows, weights, tp_size):
    width, cols = weights[0].shape
    rows = grad_rows.shape[1]
    block = rows // tp_size
    chunks = 8
    wide = width // chunks
    return pl.pallas_call(
        functools.partial(reduce_kernel, tp_size, chunks),
        out_shape=jax.ShapeDtypeStruct((block, width), BF16),
        in_specs=[ANYWHERE] * 4,
        out_specs=ANYWHERE,
        scratch_shapes=[
            pltpu.VMEM((3, rows, cols), BF16),
            pltpu.VMEM((2, 3, wide, cols), BF16),
            pltpu.VMEM((4, block, width), F32),
            pltpu.VMEM((2, block // 2, width), F32),
            pltpu.VMEM((2, block, width), F32),
            pltpu.VMEM((block, width), BF16),
            DMA, DMA((2, 3)), DMA((chunks,)), DMA((6, chunks)), DMA((6, chunks)),
        ],
        compiler_params=params(4),
        cost_estimate=pl.CostEstimate(flops=6 * rows * width * cols, bytes_accessed=6 * width * cols, transcendentals=0),
        name="project_reduce",
    )(grad_rows, *weights)


def solution(mesh):
    cp_size, tp_size = mesh.shape['cp'], mesh.shape['tp']
    row_spec = P(('dp', 'cp', 'tp'), None)

    def local_step(x_blk, dy_blk, w_query, w_key, w_value, w_out):
        weights = (w_query, w_key, w_value)
        qkv, dy1 = project(x_blk, dy_blk, weights, cp_size, tp_size)
        o, lse, o_rows, dy23 = forward(qkv, dy_blk, dy1, cp_size, tp_size)
        do, y_part = middle(dy_blk, dy1, dy23, w_out, o_rows, cp_size, tp_size)
        y_blk = lax.psum_scatter(y_part, 'tp', scatter_dimension=0, tiled=True).astype(BF16)
        grad_rows = backward(qkv, do, o, lse, cp_size)
        dx_blk = reduce_out(grad_rows, weights, tp_size)
        return y_blk, dx_blk

    weight = P(None, 'tp')
    return jax.shard_map(local_step, mesh=mesh, in_specs=(row_spec, row_spec, weight, weight, weight, P('tp', None)), out_specs=(row_spec, row_spec), check_vma=False)
```

time: 2920 us -> 517 us (0.18)
  matrix products: 1720 us -> 0 us
  waiting for transfers between devices: 834 us -> 0.08 us
  Pallas kernels: 0 us -> 494 us
  other arithmetic: 303 us -> 3.94 us
  local copies, waits for them, and re-layouts: 38.9 us -> 1.32 us
    dot_general x104 -> x0, matrix products: 1720 us -> none  [the longest x16 418 us: block_step(): jnp.einsum('hgqk,qhgd->khd', d_score, q_blk, preferred_element_type=jnp.f...]
    reduce_scatter x4 -> x1, waiting for transfers between devices: 555 us -> 0.02 us  [local_step(): lax.psum_scatter(y_part, 'tp', scatter_dimension=0, tiled=True).astype(BF16)]
    pallas_call x0 -> x5, Pallas kernels: none -> 494 us  [the longest x1 146 us: backward(): pl.pallas_call(functools.partial(backward_kernel, cp_size), out_shape=jax...]
    all_gather x4 -> x0, waiting for transfers between devices: 276 us -> none  [the longest x1 85.3 us: local_step(): x_loc = lax.all_gather(x_blk, 'tp', axis=0, tiled=True)]
    reduce_sum x16 -> x0, other arithmetic: 163 us -> none  [block_step(): log_norm = jax.nn.logsumexp(scores, axis=-1, keepdims=True)]
    convert_element_type x20 -> x1, other arithmetic: 134 us -> 3.94 us  [local_step(): lax.psum_scatter(y_part, 'tp', scatter_dimension=0, tiled=True).astype(BF16)]
  transfers between devices with their start and end apart: 8 -> 1, of which waited for: 8 -> 0; matrix products, arithmetic and copies ran while one was open for 5% -> 0% of each run, Pallas kernels for 0% -> 56%
where the time goes in v2:
time: 517 us; the launch traced here: 514 us
  Pallas kernels  494 us (96%)
  between operations  14.1 us (3%)
    pallas_call x1, Pallas kernels, backward(): pl.pallas_call(functools.partial(backward_kernel, cp_size), out_shape=jax...  146 us
    pallas_call x1, Pallas kernels, reduce_out(): pl.pallas_call(functools.partial(reduce_kernel, tp_size, chunks), out_sha...  141 us
    pallas_call x1, Pallas kernels, project(): pl.pallas_call(functools.partial(project_kernel, cp_size, tp_size), out_s...  104 us
    pallas_call x1, Pallas kernels, forward(): pl.pallas_call(functools.partial(forward_kernel, cp_size, tp_size), out_s...  66 us
    pallas_call x1, Pallas kernels, middle(): pl.pallas_call(functools.partial(middle_kernel, cp_size, tp_size), out_sh...  37 us
  transfers between devices with their start and end apart: 1, of which 0 were waited for; matrix products, arithmetic and copies ran while one was open for 0% of the time, Pallas kernels for 56%

profile of v2, /device:TPU:97, one launch (start us, length us, event | category | flops | bytes accessed | tf_op | source)
XLA Modules:
  0.0 513.8 jit_solution(13917442440627750594)
XLA Ops:
  7.2 0.1 reduce-scatter.2.cloned.1.call-start
  7.2 104.4 %project_qkv.1 = (bf16[3,8192,128]{2,1,0:T(8,128)(2,1)}, bf16[256,4096]{1,0:T(8,128)(2,1)}) custom-call(bf16[256,4096]{1,0:T(8,128)(2,1)} %x_ref.1, bf16[256,4096]{1,0:T(8,128)(2,1)} %dy_ref.5, bf16[4096,1024]{1,0:T(8,128)(2,1)} %wq_ref.3, bf16[4096,1024]{1,0:T(8,128)(2,1)} %wk_ref.3, bf16[4096,1024]{1,0:T(8,128)(2,1)} %wv_ref.3), custom_call_target="tpu_custom_call" | custom-call | flops 25769803776 | bytes 25165824 | tf_op jit(solution)/shard_map/project_qkv/pallas_call | solution.py:180
  111.7 66.0 %attention_forward.1 = (bf16[8192,128]{1,0:T(8,128)(2,1)}, f32[16,8,512]{2,1,0:T(8,128)}, bf16[1024,1024]{1,0:T(8,128)(2,1)}, bf16[2,256,4096]{2,1,0:T(8,128)(2,1)}) custom-call(bf16[3,8192,128]{2,1,0:T(8,128)(2,1)} %get-tuple-element.11.qkv_ref, bf16[256,4096]{1,0:T(8,128)(2,1)} %dy_ref.5, bf16[256,4096]{1,0:T(8,128)(2,1)} %get-tuple-element.10.dy1_ref), custom_call_target="tpu_custom_call" | custom-call | flops 17179869184 | bytes 8388608 | tf_op jit(solution)/shard_map/attention_forward/pallas_call | solution.py:318
  177.7 37.0 %project_middle.1 = (bf16[1,8192,128]{2,1,0:T(8,128)(2,1)}, f32[1024,4096]{1,0:T(8,128)}) custom-call(bf16[256,4096]{1,0:T(8,128)(2,1)} %dy_ref.5, bf16[256,4096]{1,0:T(8,128)(2,1)} %get-tuple-element.10.dy1_ref, bf16[2,256,4096]{2,1,0:T(8,128)(2,1)} %get-tuple-element.12.dy23_ref, bf16[1024,4096]{1,0:T(8,128)(2,1)} %wo_ref.1, ...), custom_call_target="tpu_custom_call" | custom-call | flops 17179869184 | bytes 33554432 | tf_op jit(solution)/shard_map/project_middle/pallas_call | solution.py:401
  214.6 0.1 reduce-scatter.2.cloned.1.call-update
  214.7 145.8 %attention_backward.1.rows_ref = bf16[3,1024,1024]{2,1,0:T(8,128)(2,1)} custom-call(bf16[3,8192,128]{2,1,0:T(8,128)(2,1)} %get-tuple-element.11.qkv_ref, bf16[1,8192,128]{2,1,0:T(8,128)(2,1)} %get-tuple-element.15.do_ref, bf16[8192,128]{1,0:T(8,128)(2,1)} %get-tuple-element.16.o_ref, f32[16,8,512]{2,1,0:T(8,128)} %get-tuple-element.17.l_ref), custom_call_target="tpu_custom_call" | custom-call | flops 42949672960 | bytes 16777216 | tf_op jit(solution)/shard_map/attention_backward/pallas_call | solution.py:516
  360.5 141.1 %project_reduce.1 = bf16[256,4096]{1,0:T(8,128)(2,1)} custom-call(bf16[3,1024,1024]{2,1,0:T(8,128)(2,1)} %attention_backward.1.rows_ref, bf16[4096,1024]{1,0:T(8,128)(2,1)} %wq_ref.3, bf16[4096,1024]{1,0:T(8,128)(2,1)} %wk_ref.3, bf16[4096,1024]{1,0:T(8,128)(2,1)} %wv_ref.3), custom_call_target="tpu_custom_call" | custom-call | flops 25769803776 | bytes 25165824 | tf_op jit(solution)/shard_map/project_reduce/pallas_call | solution.py:640
  501.6 0.0 copy-start
  501.6 0.0 reduce-scatter.2.cloned.1.call-done
  501.7 3.9 convert_element_type.3
  505.6 0.0 copy-done
  505.6 1.3 copy.9
Async XLA Ops:
  7.2 494.5 %reduce-scatter.2.cloned.1.call-start = ((), (), s32[]{:S(2)}) async-start(), calls=%async_computation.1 | async-start | bytes 20971520 | tf_op jit(solution)/shard_map/reduce_scatter | solution.py:669
  501.6 4.0 copy-start
Sparse Core Ops, SparseCore 0:
  214.8 143.3 reduce-scatter.1

commit v3 on v2

v3 whole, which is shorter than its diff:
```python
import functools
import math

import jax
import jax.numpy as jnp
from jax import lax
from jax.experimental import pallas as pl
from jax.experimental.pallas import tpu as pltpu
from jax.sharding import PartitionSpec as P

HEAD_DIM = 128
F32, BF16 = jnp.float32, jnp.bfloat16
LOG2E = math.log2(math.e)
MESH = pl.DeviceIdType.MESH
ANYWHERE = pl.BlockSpec(memory_space=pltpu.HBM)
DMA = pltpu.SemaphoreType.DMA


def dot_nt(a, b):
    return lax.dot_general(a, b, (((1,), (1,)), ((), ())), preferred_element_type=F32)


def dot_nn(a, b):
    return lax.dot_general(a, b, (((1,), (0,)), ((), ())), preferred_element_type=F32)


def rows_at(start, size):
    return pl.ds(pl.multiple_of(start, size), size)


def ring(axis, size):
    me = lax.axis_index(axis)
    return me, lax.rem(me + 1, size), lax.rem(me + size - 1, size)


def meet(*peers):
    barrier = pltpu.get_barrier_semaphore()
    for peer in peers:
        pl.semaphore_signal(barrier, inc=1, device_id=peer, device_id_type=MESH)
    pl.semaphore_wait(barrier, len(peers))


def others(axis, size):
    me = lax.axis_index(axis)
    return [{axis: lax.rem(me + d, size)} for d in range(1, size)]


def beside(tp_size):
    _, right, left = ring('tp', tp_size)
    return [{'tp': right}, {'tp': left}]


def partner():
    me = lax.axis_index('cp')
    return me + 1 - 2 * lax.rem(me, 2)


def params(collective_id):
    return pltpu.CompilerParams(collective_id=collective_id, has_side_effects=True, vmem_limit_bytes=63 << 20)


def far_first(cp_size):
    return sorted(range(1, cp_size), key=lambda d: -min(d, cp_size - d))


def row_groups(tp_size, block, split_last):
    me, right, left = ring('tp', tp_size)
    far = lax.rem(me + 2, tp_size)
    half, part = block // 2, block // 4
    groups = [
        (0, half, ((me, 0), (me, half))),
        (block, half, ((right, 0), (left, half))),
        (2 * block, half, ((right, half), (left, 0))),
    ]
    if not split_last:
        return groups + [(3 * block, half, ((far, 0), (far, half)))]
    return groups + [
        (3 * block, part, ((far, 0), (far, half))),
        (3 * block + half, part, ((far, part), (far, half + part))),
    ]


def position(cp_size, tp_size, block, owner, row):
    piece = block * tp_size // 2
    first = owner < tp_size // 2
    cp_rank = lax.axis_index('cp')
    piece_id = jnp.where(first, cp_rank, 2 * cp_size - 1 - cp_rank)
    return piece_id * piece + jnp.where(first, owner, owner - tp_size // 2) * block + row


class HeadSender:
    def __init__(self, cp_size, tp_size, block, groups, res, dst, send, recv, local):
        self.cp_size, self.tp_size, self.block, self.groups = cp_size, tp_size, block, groups
        self.res, self.dst, self.sems = res, dst, (send, recv, local)

    def copies(self, g):
        send, recv, local = self.sems
        me = lax.axis_index('cp')
        start, length, parts = self.groups[g]
        for n, (owner, row) in enumerate(parts):
            rows = rows_at(position(self.cp_size, self.tp_size, self.block, owner, row), length)
            here = pl.ds(start + n * length, length)
            for d in far_first(self.cp_size):
                peer = lax.rem(me + d, self.cp_size)
                yield pltpu.make_async_remote_copy(
                    src_ref=self.res.at[peer, :, here, :], dst_ref=self.dst.at[:, rows, :],
                    send_sem=send.at[d - 1, g, n], recv_sem=recv.at[d - 1, g, n],
                    device_id={'cp': peer}, device_id_type=MESH)
            yield pltpu.make_async_copy(self.res.at[me, :, here, :], self.dst.at[:, rows, :], local.at[g, n])

    def start(self, g):
        for copy in self.copies(g):
            copy.start()

    def wait(self):
        for g in range(len(self.groups)):
            for copy in self.copies(g):
                copy.wait()


def head_scratch(cp_size, arrays, rows, groups):
    return [
        pltpu.VMEM((cp_size, arrays, rows, HEAD_DIM), BF16),
        DMA((cp_size - 1, groups, 2)),
        DMA((cp_size - 1, groups, 2)),
        DMA((groups, 2)),
    ]


def project_kernel(cp_size, tp_size, x_ref, dy_ref, wq_ref, wk_ref, wv_ref, qkv_ref, dy1_ref, w_v, xg, res, send, recv, local, w_sem, x_sem, y_send, y_recv):
    block = x_ref.shape[0]
    half, part = block // 2, block // 4
    _, right, left = ring('tp', tp_size)
    groups = row_groups(tp_size, block, True)
    heads = HeadSender(cp_size, tp_size, block, groups, res, qkv_ref, send, recv, local)

    def pass_on(k, src, dst, peer):
        copy = pltpu.make_async_remote_copy(
            src_ref=src, dst_ref=dst, send_sem=y_send.at[k], recv_sem=y_recv.at[k], device_id={'tp': peer}, device_id_type=MESH)
        copy.start()
        return copy

    def landed(start, size):
        return xg.at[pl.ds(start, size), :]

    low, high = x_ref.at[pl.ds(0, half), :], x_ref.at[pl.ds(half, half), :]
    own = pltpu.make_async_copy(x_ref, landed(0, block), x_sem)
    own.start()
    loads = [pltpu.make_async_copy(w, w_v.at[n], w_sem.at[n]) for n, w in enumerate((wq_ref, wk_ref, wv_ref))]
    meet(*others('cp', cp_size), *beside(tp_size))
    hops = [
        pass_on(0, low, landed(block, half), left),
        pass_on(1, high, landed(block + half, half), right),
        pass_on(2, high, landed(2 * block, half), left),
        pass_on(3, low, landed(2 * block + half, half), right),
    ]
    for load in loads:
        load.start()
    own.wait()

    wide = min(4, cp_size)
    cols = wide * HEAD_DIM
    steps = cp_size // wide

    def compute(g, n):
        start, length, _ = groups[g]
        rows = pl.ds(start, 2 * length)

        def body(s, _):
            out = dot_nn(xg[rows, :], w_v[n, :, rows_at(s * cols, cols)]).astype(BF16)
            for k in range(wide):
                res[wide * s + k, n, rows, :] = out[:, k * HEAD_DIM:(k + 1) * HEAD_DIM]
            return 0

        lax.fori_loop(0, steps, body, 0)

    for n in range(3):
        loads[n].wait()
        compute(0, n)
    heads.start(0)
    hops[0].wait_recv()
    hops.append(pass_on(4, landed(block, part), landed(3 * block, part), left))
    hops.append(pass_on(5, landed(block + part, part), landed(3 * block + half, part), left))
    hops[1].wait_recv()
    hops.append(pass_on(6, landed(block + half, part), landed(3 * block + part, part), right))
    hops.append(pass_on(7, landed(block + half + part, part), landed(3 * block + half + part, part), right))
    hops.append(pass_on(8, dy_ref.at[pl.ds(0, half), :], dy1_ref.at[pl.ds(0, half), :], left))
    hops.append(pass_on(9, dy_ref.at[pl.ds(half, half), :], dy1_ref.at[pl.ds(half, half), :], right))
    for g, arrived in ((1, ()), (2, (2, 3)), (3, (4, 6)), (4, (5, 7))):
        for k in arrived:
            hops[k].wait_recv()
        for n in range(3):
            compute(g, n)
        heads.start(g)
    for k in range(8):
        hops[k].wait_send()
    for k in (8, 9):
        hops[k].wait()
    heads.wait()


def project(x_blk, dy_blk, weights, cp_size, tp_size):
    block, width = x_blk.shape
    cols = weights[0].shape[1]
    seq = block * tp_size * cp_size
    return pl.pallas_call(
        functools.partial(project_kernel, cp_size, tp_size),
        out_shape=(jax.ShapeDtypeStruct((3, seq, HEAD_DIM), BF16), jax.ShapeDtypeStruct((block, width), BF16)),
        in_specs=[ANYWHERE] * 5,
        out_specs=(ANYWHERE, ANYWHERE),
        scratch_shapes=[pltpu.VMEM((3, width, cols), BF16), pltpu.VMEM((4 * block, width), BF16)]
        + head_scratch(cp_size, 3, 4 * block, 5) + [DMA((3,)), DMA, DMA((10,)), DMA((10,))],
        compiler_params=params(0),
        cost_estimate=pl.CostEstimate(flops=6 * block * tp_size * width * cols, bytes_accessed=6 * width * cols, transcendentals=0),
        name="project_qkv",
    )(x_blk, dy_blk, *weights)


def send_piece(cp_size, i, src, dst_of, send, recv, local, start):
    me = lax.axis_index('cp')
    half = jnp.where(i < cp_size, 0, 1)
    owner = jnp.where(i < cp_size, i, 2 * cp_size - 1 - i)

    @pl.when(owner == me)
    def _():
        copy = pltpu.make_async_copy(src, dst_of(half, me), local.at[half])
        copy.start() if start else copy.wait()

    @pl.when(owner != me)
    def _():
        copy = pltpu.make_async_remote_copy(
            src_ref=src, dst_ref=dst_of(half, me), send_sem=send.at[i], recv_sem=recv.at[me, half],
            device_id={'cp': owner}, device_id_type=MESH)
        copy.start() if start else copy.wait_send()


def wait_pieces(cp_size, src_of, dst_of, send, recv, local):
    me = lax.axis_index('cp')

    def sent(i, _):
        send_piece(cp_size, i, src_of(i), dst_of, send, recv, local, False)
        return 0

    lax.fori_loop(0, 2 * cp_size, sent, 0)
    for d in range(1, cp_size):
        peer = lax.rem(me + d, cp_size)
        for half in range(2):
            pltpu.make_async_remote_copy(
                src_ref=src_of(0), dst_ref=dst_of(half, peer), send_sem=send.at[0], recv_sem=recv.at[peer, half],
                device_id={'cp': peer}, device_id_type=MESH).wait_recv()


def forward_kernel(cp_size, tp_size, qkv_ref, dy_ref, dy1_ref, wo_ref, o_ref, l_ref, rows_ref, do_ref,
                   qkv, o_v, l_v, vt_ref, s_ref, acc_ref, dyg, wo, res, h_send, h_recv, h_local,
                   in_sem, send, recv, local, y_send, y_recv, out_sem):
    seq = qkv.shape[1]
    bq = s_ref.shape[0]
    nblk = seq // bq
    c = HEAD_DIM ** -0.5 * LOG2E
    _, right, left = ring('tp', tp_size)
    block = dy_ref.shape[0]
    half = block // 2
    low, high = pl.ds(0, half), pl.ds(half, half)
    groups = row_groups(tp_size, block, False)
    heads = HeadSender(cp_size, tp_size, block, groups, res, do_ref, h_send, h_recv, h_local)

    loads = [
        pltpu.make_async_copy(dy_ref, dyg.at[pl.ds(0, block), :], in_sem.at[0]),
        pltpu.make_async_copy(dy1_ref, dyg.at[pl.ds(block, block), :], in_sem.at[1]),
        pltpu.make_async_copy(wo_ref, wo, in_sem.at[2]),
        pltpu.make_async_copy(qkv_ref, qkv, in_sem.at[3]),
    ]
    for load in loads:
        load.start()
    meet(*others('cp', cp_size), *beside(tp_size))
    hops = []
    for k, (src, start, peer) in enumerate((
            (dy_ref.at[high, :], 2 * block, left),
            (dy_ref.at[low, :], 2 * block + half, right),
            (dy1_ref.at[low, :], 3 * block, left),
            (dy1_ref.at[high, :], 3 * block + half, right))):
        hop = pltpu.make_async_remote_copy(
            src_ref=src, dst_ref=dyg.at[pl.ds(start, half), :], send_sem=y_send.at[k], recv_sem=y_recv.at[k],
            device_id={'tp': peer}, device_id_type=MESH)
        hop.start()
        hops.append(hop)

    per_step = min(4, cp_size)
    cols = per_step * HEAD_DIM

    def compute(g):
        rows = pl.ds(groups[g][0], block)

        def body(s, _):
            out = dot_nt(dyg[rows, :], wo[rows_at(s * cols, cols), :]).astype(BF16)
            for k in range(per_step):
                res[per_step * s + k, 0, rows, :] = out[:, k * HEAD_DIM:(k + 1) * HEAD_DIM]
            return 0

        lax.fori_loop(0, cp_size // per_step, body, 0)
        heads.start(g)

    for load in loads[:3]:
        load.wait()
    compute(0)
    compute(1)
    loads[3].wait()

    def transpose_step(b, _):
        rows = rows_at(b * bq, bq)
        vt_ref[:, rows] = qkv[2, rows, :].T
        return 0

    lax.fori_loop(0, nblk, transpose_step, 0)

    def src_of(i):
        return o_v.at[rows_at(i * bq, bq), :]

    def dst_of(part, head):
        return rows_ref.at[rows_at(part * bq, bq), rows_at(head * HEAD_DIM, HEAD_DIM)]

    def q_step(i, _):
        @pl.when(i == nblk - 2)
        def _():
            for hop in hops:
                hop.wait()
            compute(2)
            compute(3)

        rows = rows_at(i * bq, bq)
        q = qkv[0, rows, :]
        acc_ref[...] = jnp.zeros_like(acc_ref)
        s = dot_nt(qkv[1, rows, :], q)
        kk = lax.broadcasted_iota(jnp.int32, (bq, bq), 0)
        qq = lax.broadcasted_iota(jnp.int32, (bq, bq), 1)
        s = jnp.where(kk <= qq, s, -jnp.inf)
        s_ref[...] = s
        first = jnp.max(s, axis=0, keepdims=True)

        def use(blk, m_old, m, l, following):
            mc = m * c
            alpha = jnp.exp2(m_old * c - mc)
            p = jnp.exp2(s_ref[...] * c - mc)
            m_new = m
            if following is not None:
                s = dot_nt(qkv[1, rows_at(following * bq, bq), :], q)
            part = jnp.sum(p, axis=0, keepdims=True)
            out = dot_nn(vt_ref[:, rows_at(blk * bq, bq)], p.astype(BF16))
            if following is not None:
                m_new = jnp.maximum(m, jnp.max(s, axis=0, keepdims=True))
                s_ref[...] = s
            acc_ref[...] = acc_ref[...] * alpha + out
            return m, m_new, l * alpha + part

        def body(t, carry):
            return use(jnp.where(t == 0, i, t - 1), *carry, t)

        carry = lax.fori_loop(0, i, body, (first, first, jnp.zeros((1, bq), F32)))
        m, _, l = use(jnp.where(i == 0, i, i - 1), *carry, None)
        o_v[rows, :] = (acc_ref[...] * (1.0 / l)).T.astype(BF16)
        l_v[i] = jnp.broadcast_to(m * c + jnp.log2(l), (8, bq))
        send_piece(cp_size, i, src_of(i), dst_of, send, recv, local, True)
        return 0

    lax.fori_loop(0, nblk, q_step, 0)
    out_o = pltpu.make_async_copy(o_v, o_ref, out_sem.at[0])
    out_l = pltpu.make_async_copy(l_v, l_ref, out_sem.at[1])
    out_o.start()
    out_l.start()
    wait_pieces(cp_size, src_of, dst_of, send, recv, local)
    heads.wait()
    out_o.wait()
    out_l.wait()


def forward(qkv, dy_blk, dy1, w_out, cp_size, tp_size):
    seq = qkv.shape[1]
    bq = seq // (2 * cp_size)
    block, width = dy_blk.shape
    cols = w_out.shape[0]
    pairs = seq * seq // 2
    return pl.pallas_call(
        functools.partial(forward_kernel, cp_size, tp_size),
        out_shape=(
            jax.ShapeDtypeStruct((seq, HEAD_DIM), BF16),
            jax.ShapeDtypeStruct((seq // bq, 8, bq), F32),
            jax.ShapeDtypeStruct((2 * bq, cp_size * HEAD_DIM), BF16),
            jax.ShapeDtypeStruct((1, seq, HEAD_DIM), BF16),
        ),
        in_specs=[ANYWHERE] * 4,
        out_specs=(ANYWHERE,) * 4,
        scratch_shapes=[
            pltpu.VMEM((3, seq, HEAD_DIM), BF16),
            pltpu.VMEM((seq, HEAD_DIM), BF16),
            pltpu.VMEM((seq // bq, 8, bq), F32),
            pltpu.VMEM((HEAD_DIM, seq), BF16),
            pltpu.VMEM((bq, bq), F32),
            pltpu.VMEM((HEAD_DIM, bq), F32),
            pltpu.VMEM((4 * block, width), BF16),
            pltpu.VMEM((cols, width), BF16),
        ] + head_scratch(cp_size, 1, 4 * block, 4) + [
            DMA((4,)), DMA((2 * cp_size,)), DMA((cp_size, 2)), DMA((2,)), DMA((4,)), DMA((4,)), DMA((2,)),
        ],
        compiler_params=params(1),
        cost_estimate=pl.CostEstimate(flops=4 * pairs * HEAD_DIM, bytes_accessed=8 * seq * HEAD_DIM, transcendentals=pairs),
        name="attention_forward",
    )(qkv, dy_blk, dy1, w_out)


def backward_kernel(cp_size, tp_size, qkv_ref, do_ref, o_ref, l_ref, o_rows_ref, wo_ref, rows_ref, oy_ref, wy_ref, wx_ref,
                    qkv, do_v, o_v, l_v, kt_ref, p_ref, ds_ref, dst_ref, qt_ref, dot_ref, dqt_ref, dk_acc, dv_acc, grads,
                    in_sem, send, recv, local, y_send, y_recv, x_send, x_recv):
    seq = qkv.shape[1]
    bq = p_ref.shape[0]
    nblk = seq // bq
    sub = bq // 2
    scale = HEAD_DIM ** -0.5
    c = scale * LOG2E
    loads = [
        pltpu.make_async_copy(qkv_ref, qkv, in_sem.at[0]),
        pltpu.make_async_copy(do_ref.at[0], do_v, in_sem.at[1]),
        pltpu.make_async_copy(o_ref, o_v, in_sem.at[2]),
        pltpu.make_async_copy(l_ref, l_v, in_sem.at[3]),
    ]
    for load in loads:
        load.start()
    meet(*others('cp', cp_size), *others('tp', tp_size))
    me_c, me_t = lax.axis_index('cp'), lax.axis_index('tp')
    share = wy_ref.shape[1]
    block = oy_ref.shape[1]
    y_hops = []
    for r in range(1, tp_size):
        peer = lax.rem(me_t + r, tp_size)
        y_hops.append((wo_ref.at[rows_at(me_c * share, share), :], wy_ref.at[r - 1], peer))
    for r in range(1, tp_size):
        peer = lax.rem(me_t + r, tp_size)
        y_hops.append((o_rows_ref.at[rows_at(peer * block, block), :], oy_ref.at[r - 1], peer))
    y_hops = [
        pltpu.make_async_remote_copy(
            src_ref=src, dst_ref=dst, send_sem=y_send.at[k], recv_sem=y_recv.at[k], device_id={'tp': peer}, device_id_type=MESH)
        for k, (src, dst, peer) in enumerate(y_hops)]
    x_hops = [
        pltpu.make_async_remote_copy(
            src_ref=wy_ref.at[0], dst_ref=wx_ref.at[k - 1], send_sem=x_send.at[k - 1], recv_sem=x_recv.at[k - 1],
            device_id={'cp': lax.rem(me_c + 2 * k, cp_size)}, device_id_type=MESH)
        for k in range(1, cp_size // 2)]
    for hop in y_hops:
        hop.start()
    for load in loads:
        load.wait()

    def init_step(b, _):
        rows = rows_at(b * bq, bq)
        kt_ref[:, rows] = qkv[1, rows, :].T
        dk_acc[:, rows] = jnp.zeros((HEAD_DIM, bq), F32)
        dv_acc[:, rows] = jnp.zeros((HEAD_DIM, bq), F32)
        return 0

    lax.fori_loop(0, nblk, init_step, 0)

    def src_of(i):
        return grads.at[:, rows_at(i * bq, bq), :]

    def dst_of(part, head):
        return rows_ref.at[:, rows_at(part * bq, bq), rows_at(head * HEAD_DIM, HEAD_DIM)]

    def q_step(back, _):
        i = nblk - 1 - back
        rows = rows_at(i * bq, bq)
        q = qkv[0, rows, :]
        do = do_v[rows, :]
        prod = do.astype(F32) * o_v[rows, :].astype(F32)
        delta = jnp.sum(prod.T, axis=0, keepdims=True)
        lse = l_v[i][0:1, :]
        dqt_ref[...] = jnp.zeros_like(dqt_ref)
        qt_ref[...] = q.T
        dot_ref[...] = do.T

        @pl.when(back == 3)
        def _():
            y_hops[0].wait_recv()
            for hop in x_hops:
                hop.start()

        def make(blk, r, masked):
            krows = rows_at(blk * bq + r * sub, sub)
            s = dot_nt(qkv[1, krows, :], q)
            dp = dot_nt(qkv[2, krows, :], do)
            p = jnp.exp2(s * c - lse)
            if masked:
                kk = lax.broadcasted_iota(jnp.int32, (sub, bq), 0) + r * sub
                qq = lax.broadcasted_iota(jnp.int32, (sub, bq), 1)
                p = jnp.where(kk <= qq, p, 0.0)
            pb = p.astype(BF16)
            ds = (pb.astype(F32) * (dp - delta)).astype(BF16)
            return pb.T, ds, ds.T

        def put(r, made):
            sl = slice(r * sub, (r + 1) * sub)
            p_ref[:, sl], ds_ref[sl, :], dst_ref[:, sl] = made

        def take(r):
            sl = slice(r * sub, (r + 1) * sub)
            return p_ref[:, sl], ds_ref[sl, :], dst_ref[:, sl]

        def flush(blk, r, p, ds_t, ds):
            krows = rows_at(blk * bq + r * sub, sub)
            dv_acc[:, krows] += dot_nn(dot_ref[...], p)
            dk_acc[:, krows] += dot_nn(qt_ref[...], ds)
            return dot_nn(kt_ref[:, krows], ds_t)

        for r in range(2):
            put(r, make(i, r, True))

        def body(t, _):
            cur = jnp.where(t == 0, i, t - 1)
            out = None
            for r in range(2):
                old = take(r)
                new = make(t, r, False)
                d = flush(cur, r, *old)
                out = d if out is None else out + d
                put(r, new)
            dqt_ref[...] += out
            return 0

        lax.fori_loop(0, i, body, 0)
        cur = jnp.where(i == 0, i, i - 1)
        out = flush(cur, 0, *take(0)) + flush(cur, 1, *take(1))
        grads[0, rows, :] = ((dqt_ref[...] + out) * scale).T.astype(BF16)
        grads[1, rows, :] = (dk_acc[:, rows] * scale).T.astype(BF16)
        grads[2, rows, :] = dv_acc[:, rows].T.astype(BF16)
        send_piece(cp_size, i, src_of(i), dst_of, send, recv, local, True)
        return 0

    lax.fori_loop(0, nblk, q_step, 0)
    wait_pieces(cp_size, src_of, dst_of, send, recv, local)
    for k, hop in enumerate(y_hops):
        hop.wait_send() if k == 0 else hop.wait()
    for hop in x_hops:
        hop.wait()


def backward(qkv, do, o, lse, o_rows, w_out, cp_size, tp_size):
    seq = qkv.shape[1]
    cols, width = w_out.shape
    block = o_rows.shape[0] // tp_size
    share = cols // cp_size
    bq = seq // (2 * cp_size)
    pairs = seq * seq // 2
    return pl.pallas_call(
        functools.partial(backward_kernel, cp_size, tp_size),
        out_shape=(
            jax.ShapeDtypeStruct((3, 2 * bq, cp_size * HEAD_DIM), BF16),
            jax.ShapeDtypeStruct((tp_size - 1, block, cols), BF16),
            jax.ShapeDtypeStruct((tp_size - 1, share, width), BF16),
            jax.ShapeDtypeStruct((max(1, cp_size // 2 - 1), share, width), BF16),
        ),
        in_specs=[ANYWHERE] * 6,
        out_specs=(ANYWHERE,) * 4,
        scratch_shapes=[
            pltpu.VMEM((3, seq, HEAD_DIM), BF16),
            pltpu.VMEM((seq, HEAD_DIM), BF16),
            pltpu.VMEM((seq, HEAD_DIM), BF16),
            pltpu.VMEM((seq // bq, 8, bq), F32),
            pltpu.VMEM((HEAD_DIM, seq), BF16),
            pltpu.VMEM((bq, bq), BF16),
            pltpu.VMEM((bq, bq), BF16),
            pltpu.VMEM((bq, bq), BF16),
            pltpu.VMEM((HEAD_DIM, bq), BF16),
            pltpu.VMEM((HEAD_DIM, bq), BF16),
            pltpu.VMEM((HEAD_DIM, bq), F32),
            pltpu.VMEM((HEAD_DIM, seq), F32),
            pltpu.VMEM((HEAD_DIM, seq), F32),
            pltpu.VMEM((3, seq, HEAD_DIM), BF16),
            DMA((4,)), DMA((2 * cp_size,)), DMA((cp_size, 2)), DMA((2,)), DMA((6,)), DMA((6,)), DMA((cp_size,)), DMA((cp_size,)),
        ],
        compiler_params=params(2),
        cost_estimate=pl.CostEstimate(flops=10 * pairs * HEAD_DIM, bytes_accessed=16 * seq * HEAD_DIM, transcendentals=pairs),
        name="attention_backward",
    )(qkv, do, o, lse, o_rows, w_out)


def reduce_kernel(cp_size, tp_size, chunks, rows_ref, wq_ref, wk_ref, wv_ref, o_rows_ref, oy_ref, wo_ref, wy_ref, wx_ref,
                  out_ref, y_ref, wx2_ref, sib_ref,
                  g_v, w_v, part, mid, last, out_v, stage, y_acc, o_v, in_sem, w_sem, out_sem, sends, recvs,
                  x_send, x_recv, d_send, d_recv, o_sem, s_sem):
    me, right, left = ring('tp', tp_size)
    far = lax.rem(me + 2, tp_size)
    block = part.shape[1]
    half = block // 2
    low, high = pl.ds(0, half), pl.ds(half, half)
    wide = part.shape[2] // chunks
    weights = (wq_ref, wk_ref, wv_ref)

    def w_load(n, a):
        return pltpu.make_async_copy(weights[a].at[rows_at(n * wide, wide), :], w_v.at[lax.rem(n, 2), a], w_sem.at[lax.rem(n, 2), a])

    load = pltpu.make_async_copy(rows_ref, g_v, in_sem)
    load.start()
    for a in range(3):
        w_load(0, a).start()
    me_c, mate = lax.axis_index('cp'), partner()
    steps = range(1, cp_size // 2)
    meet(*beside(tp_size), {'cp': mate}, *({'cp': lax.rem(me_c + 2 * k, cp_size)} for k in steps))

    def share_ref(s, k):
        if k == 0:
            return wy_ref.at[s]
        return wx_ref.at[k - 1] if s == 0 else wx2_ref.at[s - 1, k - 1]

    def along(s, k):
        return pltpu.make_async_remote_copy(
            src_ref=wy_ref.at[s], dst_ref=wx2_ref.at[s - 1, k - 1], send_sem=x_send.at[s - 1, k - 1], recv_sem=x_recv.at[s - 1, k - 1],
            device_id={'cp': lax.rem(me_c + 2 * k, cp_size)}, device_id_type=MESH)

    def across(s, k):
        return pltpu.make_async_remote_copy(
            src_ref=share_ref(s, k), dst_ref=sib_ref.at[s, k], send_sem=d_send.at[s, k], recv_sem=d_recv.at[s, k],
            device_id={'cp': mate}, device_id_type=MESH)

    for s in range(1, tp_size - 1):
        for k in steps:
            along(s, k).start()
    for s in range(tp_size - 1):
        across(s, 0).start()
    for k in steps:
        across(0, k).start()
    o_loads = [pltpu.make_async_copy(o_rows_ref.at[rows_at(me * (o_rows_ref.shape[0] // tp_size), o_rows_ref.shape[0] // tp_size), :], o_v.at[0], o_sem.at[0])]
    for s in range(tp_size - 1):
        o_loads.append(pltpu.make_async_copy(oy_ref.at[s], o_v.at[s + 1], o_sem.at[s + 1]))
    for copy in o_loads:
        copy.start()

    def hop(kind, n):
        cols = rows_at(n * wide, wide)
        src, dst, peer = {
            'far_r': (part.at[0, low, cols], mid.at[0, :, cols], right),
            'far_l': (part.at[0, high, cols], mid.at[1, :, cols], left),
            'plain_r': (part.at[1, high, cols], last.at[0, high, cols], right),
            'plain_l': (part.at[2, low, cols], last.at[1, low, cols], left),
            'sum_r': (part.at[1, low, cols], last.at[0, low, cols], right),
            'sum_l': (part.at[2, high, cols], last.at[1, high, cols], left),
        }[kind]
        k = ('far_r', 'far_l', 'plain_r', 'plain_l', 'sum_r', 'sum_l').index(kind)
        return pltpu.make_async_remote_copy(
            src_ref=src, dst_ref=dst, send_sem=sends.at[k, n], recv_sem=recvs.at[k, n], device_id={'tp': peer}, device_id_type=MESH)

    load.wait()
    owners = (far, right, left, me)

    def compute(n, _):
        slot = lax.rem(n, 2)

        @pl.when(n + 1 < chunks)
        def _():
            for a in range(3):
                w_load(n + 1, a).start()

        for a in range(3):
            w_load(n, a).wait()
        cols = rows_at(n * wide, wide)
        for k in range(4):
            rows = rows_at(owners[k] * block, block)
            total = dot_nt(g_v[0, rows, :], w_v[slot, 0])
            total = total + dot_nt(g_v[1, rows, :], w_v[slot, 1])
            part[k, :, cols] = total + dot_nt(g_v[2, rows, :], w_v[slot, 2])
        for kind in ('far_r', 'far_l', 'plain_r', 'plain_l'):
            hop(kind, n).start()
        return 0

    lax.fori_loop(0, chunks, compute, 0)

    def forward_sums(n, _):
        cols = rows_at(n * wide, wide)
        hop('far_r', n).wait_recv()
        part[1, :half, cols] += mid[0, :, cols]
        hop('sum_r', n).start()
        hop('far_l', n).wait_recv()
        part[2, half:, cols] += mid[1, :, cols]
        hop('sum_l', n).start()
        return 0

    lax.fori_loop(0, chunks, forward_sums, 0)

    for s in range(1, tp_size - 1):
        for k in steps:
            along(s, k).wait_recv()
            across(s, k).start()
    for copy in o_loads:
        copy.wait()
    share = wy_ref.shape[1]
    span = stage.shape[2]
    halves = y_acc.shape[1] // span

    def stage_copies(n):
        s, h = divmod(n, halves)
        cols = pl.ds(h * span, span)
        slot = n % 2
        if s == 0:
            return [pltpu.make_async_copy(wo_ref.at[:, cols], stage.at[slot], s_sem.at[slot, 0])]
        copies = []
        for k in range(cp_size // 2):
            mine, its = lax.rem(me_c + cp_size - 2 * k, cp_size), lax.rem(mate + cp_size - 2 * k, cp_size)
            copies.append(pltpu.make_async_copy(
                share_ref(s - 1, k).at[:, cols], stage.at[slot, rows_at(mine * share, share), :], s_sem.at[slot, 2 * k]))
            copies.append(pltpu.make_async_copy(
                sib_ref.at[s - 1, k, :, cols], stage.at[slot, rows_at(its * share, share), :], s_sem.at[slot, 2 * k + 1]))
        return copies

    def stage_start(n):
        s, h = divmod(n, halves)
        if s > 0 and h == 0:
            for k in range(cp_size // 2):
                across(s - 1, k).wait_recv()
        for copy in stage_copies(n):
            copy.start()

    total_steps = tp_size * halves
    stage_start(0)
    for n in range(total_steps):
        if n + 1 < total_steps:
            stage_start(n + 1)
        for copy in stage_copies(n):
            copy.wait()
        s, h = divmod(n, halves)
        tile = min(512, span)

        def y_step(j, _):
            cols = rows_at(j * tile, tile)
            out = rows_at(h * span + j * tile, tile)
            product = dot_nn(o_v[s], stage[n % 2, :, cols])
            if s == 0:
                y_acc[:, out] = product
            elif s < tp_size - 1:
                y_acc[:, out] += product
            else:
                out_v[:, out] = (y_acc[:, out] + product).astype(BF16)
            return 0

        lax.fori_loop(0, span // tile, y_step, 0)
    y_out = pltpu.make_async_copy(out_v, y_ref, in_sem)
    y_out.start()
    y_out.wait()

    def put(n):
        cols = rows_at(n * wide, wide)
        return pltpu.make_async_copy(out_v.at[:, cols], out_ref.at[:, cols], out_sem.at[n])

    def finish(n, _):
        cols = rows_at(n * wide, wide)
        for kind in ('plain_r', 'plain_l', 'sum_r', 'sum_l'):
            hop(kind, n).wait_recv()
        out_v[:, cols] = (part[3, :, cols] + last[0, :, cols] + last[1, :, cols]).astype(BF16)
        put(n).start()
        return 0

    lax.fori_loop(0, chunks, finish, 0)

    def close(n, _):
        put(n).wait()
        for kind in ('far_r', 'far_l', 'plain_r', 'plain_l', 'sum_r', 'sum_l'):
            hop(kind, n).wait_send()
        return 0

    lax.fori_loop(0, chunks, close, 0)
    for s in range(tp_size - 1):
        for k in range(cp_size // 2):
            across(s, k).wait_send()
            if s > 0 and k > 0:
                along(s, k).wait_send()


def reduce_out(grad_rows, weights, o_rows, oy, w_out, wy, wx, cp_size, tp_size):
    width, cols = weights[0].shape
    share = wy.shape[1]
    pairs = cp_size // 2
    rows = grad_rows.shape[1]
    block = rows // tp_size
    chunks = 8
    wide = width // chunks
    return pl.pallas_call(
        functools.partial(reduce_kernel, cp_size, tp_size, chunks),
        out_shape=(
            jax.ShapeDtypeStruct((block, width), BF16),
            jax.ShapeDtypeStruct((block, width), BF16),
            jax.ShapeDtypeStruct((tp_size - 2, max(1, pairs - 1), share, width), BF16),
            jax.ShapeDtypeStruct((tp_size - 1, pairs, share, width), BF16),
        ),
        in_specs=[ANYWHERE] * 9,
        out_specs=(ANYWHERE,) * 4,
        scratch_shapes=[
            pltpu.VMEM((3, rows, cols), BF16),
            pltpu.VMEM((2, 3, wide, cols), BF16),
            pltpu.VMEM((4, block, width), F32),
            pltpu.VMEM((2, block // 2, width), F32),
            pltpu.VMEM((2, block, width), F32),
            pltpu.VMEM((block, width), BF16),
            pltpu.VMEM((2, cols, width // 2), BF16),
            pltpu.VMEM((block, width), F32),
            pltpu.VMEM((tp_size, block, cols), BF16),
            DMA, DMA((2, 3)), DMA((chunks,)), DMA((6, chunks)), DMA((6, chunks)),
            DMA((tp_size - 2, pairs)), DMA((tp_size - 2, pairs)), DMA((tp_size - 1, pairs)), DMA((tp_size - 1, pairs)),
            DMA((tp_size,)), DMA((2, cp_size)),
        ],
        compiler_params=params(3),
        cost_estimate=pl.CostEstimate(flops=6 * rows * width * cols, bytes_accessed=6 * width * cols, transcendentals=0),
        name="project_reduce",
    )(grad_rows, *weights, o_rows, oy, w_out, wy, wx)


def solution(mesh):
    cp_size, tp_size = mesh.shape['cp'], mesh.shape['tp']
    row_spec = P(('dp', 'cp', 'tp'), None)

    def local_step(x_blk, dy_blk, w_query, w_key, w_value, w_out):
        weights = (w_query, w_key, w_value)
        qkv, dy1 = project(x_blk, dy_blk, weights, cp_size, tp_size)
        o, lse, o_rows, do = forward(qkv, dy_blk, dy1, w_out, cp_size, tp_size)
        grad_rows, oy, wy, wx = backward(qkv, do, o, lse, o_rows, w_out, cp_size, tp_size)
        dx_blk, y_blk, _, _ = reduce_out(grad_rows, weights, o_rows, oy, w_out, wy, wx, cp_size, tp_size)
        return y_blk, dx_blk

    weight = P(None, 'tp')
    return jax.shard_map(local_step, mesh=mesh, in_specs=(row_spec, row_spec, weight, weight, weight, P('tp', None)), out_specs=(row_spec, row_spec), check_vma=False)
```

time: 517 us -> 489 us (0.946)
  between operations: 14.1 us -> 0.67 us
  Pallas kernels: 494 us -> 484 us
    pallas_call x3 -> x2, Pallas kernels: 324 us -> 297 us  [the longest x1 150 us: backward(): pl.pallas_call(functools.partial(backward_kernel, cp_size, tp_size), out_...]
    pallas_call x1, Pallas kernels: 66 us -> 85.3 us  [forward(): pl.pallas_call(functools.partial(forward_kernel, cp_size, tp_size), out_s...]
  transfers between devices with their start and end apart: 1 -> 0, of which waited for: 0 -> 0; matrix products, arithmetic and copies ran while one was open for 0% -> 0% of each run, Pallas kernels for 56% -> 0%
where the time goes in v3:
time: 489 us
  Pallas kernels  484 us (99%)
    pallas_call x1, Pallas kernels, backward(): pl.pallas_call(functools.partial(backward_kernel, cp_size, tp_size), out_...  150 us
    pallas_call x1, Pallas kernels, reduce_out(): pl.pallas_call(functools.partial(reduce_kernel, cp_size, tp_size, chunks)...  147 us
    pallas_call x1, Pallas kernels, project(): pl.pallas_call(functools.partial(project_kernel, cp_size, tp_size), out_s...  101 us
    pallas_call x1, Pallas kernels, forward(): pl.pallas_call(functools.partial(forward_kernel, cp_size, tp_size), out_s...  85.3 us

profile of v3, /device:TPU:97, one launch (start us, length us, event | category | flops | bytes accessed | tf_op | source)
XLA Modules:
  0.0 489.1 jit_solution(14157430519049090222)
XLA Ops:
  0.6 101.3 %project_qkv.1 = (bf16[3,8192,128]{2,1,0:T(8,128)(2,1)}, bf16[256,4096]{1,0:T(8,128)(2,1)}) custom-call(bf16[256,4096]{1,0:T(8,128)(2,1)} %x_ref.1, bf16[256,4096]{1,0:T(8,128)(2,1)} %dy_ref.3, bf16[4096,1024]{1,0:T(8,128)(2,1)} %wq_ref.3, bf16[4096,1024]{1,0:T(8,128)(2,1)} %wk_ref.3, bf16[4096,1024]{1,0:T(8,128)(2,1)} %wv_ref.3), custom_call_target="tpu_custom_call" | custom-call | flops 25769803776 | bytes 25165824 | tf_op jit(solution)/shard_map/project_qkv/pallas_call | solution.py:206
  101.9 85.3 %attention_forward.1 = (bf16[8192,128]{1,0:T(8,128)(2,1)}, f32[16,8,512]{2,1,0:T(8,128)}, bf16[1024,1024]{1,0:T(8,128)(2,1)}, bf16[1,8192,128]{2,1,0:T(8,128)(2,1)}) custom-call(bf16[3,8192,128]{2,1,0:T(8,128)(2,1)} %get-tuple-element.14.qkv_ref, bf16[256,4096]{1,0:T(8,128)(2,1)} %dy_ref.3, bf16[256,4096]{1,0:T(8,128)(2,1)} %get-tuple-element.15.dy1_ref, ...), custom_call_target="tpu_custom_call" | custom-call | flops 17179869184 | bytes 8388608 | tf_op jit(solution)/shard_map/attention_forward/pallas_call | solution.py:382
  187.2 150.3 %attention_backward.1 = (bf16[3,1024,1024]{2,1,0:T(8,128)(2,1)}, bf16[3,256,1024]{2,1,0:T(8,128)(2,1)}, bf16[3,128,4096]{2,1,0:T(8,128)(2,1)}, bf16[3,128,4096]{2,1,0:T(8,128)(2,1)}) custom-call(bf16[3,8192,128]{2,1,0:T(8,128)(2,1)} %get-tuple-element.14.qkv_ref, bf16[1,8192,128]{2,1,0:T(8,128)(2,1)} %get-tuple-element.16.do_ref, ...), custom_call_target="tpu_custom_call" | custom-call | flops 42949672960 | bytes 16777216 | tf_op jit(solution)/shard_map/attention_backward/pallas_call | solution.py:551
  337.5 147.0 %project_reduce.1 = (bf16[256,4096]{1,0:T(8,128)(2,1)}, bf16[256,4096]{1,0:T(8,128)(2,1)}, bf16[2,3,128,4096]{3,2,1,0:T(8,128)(2,1)}, bf16[3,4,128,4096]{3,2,1,0:T(8,128)(2,1)}) custom-call(bf16[3,1024,1024]{2,1,0:T(8,128)(2,1)} %get-tuple-element.20.rows_ref, bf16[4096,1024]{1,0:T(8,128)(2,1)} %wq_ref.3, bf16[4096,1024]{1,0:T(8,128)(2,1)} %wk_ref.3, ...), custom_call_target="tpu_custom_call" | custom-call | flops 25769803776 | bytes 25165824 | tf_op jit(solution)/shard_map/project_reduce/pallas_call | solution.py:782
  484.5 0.0 copy-start
  484.5 3.3 copy.10
  487.8 0.0 copy-done
  487.8 1.3 copy.11
Async XLA Ops:
  484.5 3.3 copy-start

commit v4 on v3

--- a/solution.py
+++ b/solution.py
@@ -14,6 +14,7 @@
 MESH = pl.DeviceIdType.MESH
 ANYWHERE = pl.BlockSpec(memory_space=pltpu.HBM)
 DMA = pltpu.SemaphoreType.DMA
+FAR, RIGHT, LEFT, OWN = range(4)
 
 
 def dot_nt(a, b):
@@ -184,8 +185,8 @@
     hops[1].wait_recv()
     hops.append(pass_on(6, landed(block + half, part), landed(3 * block + part, part), right))
     hops.append(pass_on(7, landed(block + half + part, part), landed(3 * block + half + part, part), right))
-    hops.append(pass_on(8, dy_ref.at[pl.ds(0, half), :], dy1_ref.at[pl.ds(0, half), :], left))
-    hops.append(pass_on(9, dy_ref.at[pl.ds(half, half), :], dy1_ref.at[pl.ds(half, half), :], right))
+    hops.append(pass_on(8, dy_ref.at[pl.ds(0, part), :], dy1_ref.at[pl.ds(0, part), :], left))
+    hops.append(pass_on(9, dy_ref.at[pl.ds(half, part), :], dy1_ref.at[pl.ds(part, part), :], right))
     for g, arrived in ((1, ()), (2, (2, 3)), (3, (4, 6)), (4, (5, 7))):
         for k in arrived:
             hops[k].wait_recv()
@@ -205,7 +206,7 @@
     seq = block * tp_size * cp_size
     return pl.pallas_call(
         functools.partial(project_kernel, cp_size, tp_size),
-        out_shape=(jax.ShapeDtypeStruct((3, seq, HEAD_DIM), BF16), jax.ShapeDtypeStruct((block, width), BF16)),
+        out_shape=(jax.ShapeDtypeStruct((3, seq, HEAD_DIM), BF16), jax.ShapeDtypeStruct((block // 2, width), BF16)),
         in_specs=[ANYWHERE] * 5,
         out_specs=(ANYWHERE, ANYWHERE),
         scratch_shapes=[pltpu.VMEM((3, width, cols), BF16), pltpu.VMEM((4 * block, width), BF16)]
@@ -259,31 +260,38 @@
     c = HEAD_DIM ** -0.5 * LOG2E
     _, right, left = ring('tp', tp_size)
     block = dy_ref.shape[0]
-    half = block // 2
-    low, high = pl.ds(0, half), pl.ds(half, half)
+    half, part = block // 2, block // 4
     groups = row_groups(tp_size, block, False)
     heads = HeadSender(cp_size, tp_size, block, groups, res, do_ref, h_send, h_recv, h_local)
 
+    def gathered(start, size):
+        return dyg.at[pl.ds(start, size), :]
+
     loads = [
-        pltpu.make_async_copy(dy_ref, dyg.at[pl.ds(0, block), :], in_sem.at[0]),
-        pltpu.make_async_copy(dy1_ref, dyg.at[pl.ds(block, block), :], in_sem.at[1]),
-        pltpu.make_async_copy(wo_ref, wo, in_sem.at[2]),
-        pltpu.make_async_copy(qkv_ref, qkv, in_sem.at[3]),
+        pltpu.make_async_copy(dy_ref, gathered(0, block), in_sem.at[0]),
+        pltpu.make_async_copy(wo_ref, wo, in_sem.at[1]),
+        pltpu.make_async_copy(dy1_ref.at[pl.ds(0, part), :], gathered(block, part), in_sem.at[2]),
+        pltpu.make_async_copy(dy1_ref.at[pl.ds(part, part), :], gathered(block + half, part), in_sem.at[3]),
+        pltpu.make_async_copy(qkv_ref, qkv, in_sem.at[4]),
     ]
     for load in loads:
         load.start()
     meet(*others('cp', cp_size), *beside(tp_size))
-    hops = []
-    for k, (src, start, peer) in enumerate((
-            (dy_ref.at[high, :], 2 * block, left),
-            (dy_ref.at[low, :], 2 * block + half, right),
-            (dy1_ref.at[low, :], 3 * block, left),
-            (dy1_ref.at[high, :], 3 * block + half, right))):
-        hop = pltpu.make_async_remote_copy(
-            src_ref=src, dst_ref=dyg.at[pl.ds(start, half), :], send_sem=y_send.at[k], recv_sem=y_recv.at[k],
+    hops = [
+        pltpu.make_async_remote_copy(
+            src_ref=src, dst_ref=gathered(start, size), send_sem=y_send.at[k], recv_sem=y_recv.at[k],
             device_id={'tp': peer}, device_id_type=MESH)
+        for k, (src, start, size, peer) in enumerate((
+            (dy_ref.at[pl.ds(part, part), :], block + part, part, left),
+            (dy_ref.at[pl.ds(half + part, part), :], block + half + part, part, right),
+            (dy_ref.at[pl.ds(half, half), :], 2 * block, half, left),
+            (dy_ref.at[pl.ds(0, half), :], 2 * block + half, half, right),
+            (dy1_ref.at[pl.ds(0, part), :], 3 * block, part, left),
+            (dy1_ref.at[pl.ds(part, part), :], 3 * block + half, part, right),
+            (gathered(block + part, part), 3 * block + part, part, left),
+            (gathered(block + half + part, part), 3 * block + half + part, part, right)))]
+    for hop in hops[:6]:
         hop.start()
-        hops.append(hop)
 
     per_step = min(4, cp_size)
     cols = per_step * HEAD_DIM
@@ -300,11 +308,11 @@
         lax.fori_loop(0, cp_size // per_step, body, 0)
         heads.start(g)
 
-    for load in loads[:3]:
+    for load in loads[:2]:
         load.wait()
     compute(0)
-    compute(1)
-    loads[3].wait()
+    for load in loads[2:]:
+        load.wait()
 
     def transpose_step(b, _):
         rows = rows_at(b * bq, bq)
@@ -320,10 +328,17 @@
         return rows_ref.at[rows_at(part * bq, bq), rows_at(head * HEAD_DIM, HEAD_DIM)]
 
     def q_step(i, _):
-        @pl.when(i == nblk - 2)
+        @pl.when(i == nblk // 2)
         def _():
-            for hop in hops:
-                hop.wait()
+            for arrived, hop in zip(hops, hops[6:]):
+                arrived.wait_recv()
+                hop.start()
+            compute(1)
+
+        @pl.when(i == nblk - 1)
+        def _():
+            for k, hop in enumerate(hops):
+                hop.wait_send() if k < 2 else hop.wait()
             compute(2)
             compute(3)
 
@@ -399,7 +414,7 @@
             pltpu.VMEM((4 * block, width), BF16),
             pltpu.VMEM((cols, width), BF16),
         ] + head_scratch(cp_size, 1, 4 * block, 4) + [
-            DMA((4,)), DMA((2 * cp_size,)), DMA((cp_size, 2)), DMA((2,)), DMA((4,)), DMA((4,)), DMA((2,)),
+            DMA((5,)), DMA((2 * cp_size,)), DMA((cp_size, 2)), DMA((2,)), DMA((8,)), DMA((8,)), DMA((2,)),
         ],
         compiler_params=params(1),
         cost_estimate=pl.CostEstimate(flops=4 * pairs * HEAD_DIM, bytes_accessed=8 * seq * HEAD_DIM, transcendentals=pairs),
@@ -407,12 +422,12 @@
     )(qkv, dy_blk, dy1, w_out)
 
 
-def backward_kernel(cp_size, tp_size, qkv_ref, do_ref, o_ref, l_ref, o_rows_ref, wo_ref, rows_ref, oy_ref, wy_ref, wx_ref,
-                    qkv, do_v, o_v, l_v, kt_ref, p_ref, ds_ref, dst_ref, qt_ref, dot_ref, dqt_ref, dk_acc, dv_acc, grads,
-                    in_sem, send, recv, local, y_send, y_recv, x_send, x_recv):
+def backward_kernel(cp_size, tp_size, qkv_ref, do_ref, o_ref, l_ref, o_rows_ref, wo_ref, rows_ref, oy_ref, wy_ref,
+                    qkv, do_v, o_v, l_v, delta_v, kt_ref, qt_ref, dot_ref, p_ref, ds_ref, dst_ref, dq_acc, dk_acc, dv_acc, grads,
+                    in_sem, send, recv, local, y_send, y_recv):
     seq = qkv.shape[1]
     bq = p_ref.shape[0]
-    nblk = seq // bq
+    nblk, half_blk = 2 * cp_size, cp_size
     sub = bq // 2
     scale = HEAD_DIM ** -0.5
     c = scale * LOG2E
@@ -426,118 +441,150 @@
         load.start()
     meet(*others('cp', cp_size), *others('tp', tp_size))
     me_c, me_t = lax.axis_index('cp'), lax.axis_index('tp')
-    share = wy_ref.shape[1]
-    block = oy_ref.shape[1]
+    share, block = wy_ref.shape[1], oy_ref.shape[1]
     y_hops = []
     for r in range(1, tp_size):
         peer = lax.rem(me_t + r, tp_size)
         y_hops.append((wo_ref.at[rows_at(me_c * share, share), :], wy_ref.at[r - 1], peer))
-    for r in range(1, tp_size):
-        peer = lax.rem(me_t + r, tp_size)
         y_hops.append((o_rows_ref.at[rows_at(peer * block, block), :], oy_ref.at[r - 1], peer))
     y_hops = [
         pltpu.make_async_remote_copy(
             src_ref=src, dst_ref=dst, send_sem=y_send.at[k], recv_sem=y_recv.at[k], device_id={'tp': peer}, device_id_type=MESH)
         for k, (src, dst, peer) in enumerate(y_hops)]
-    x_hops = [
-        pltpu.make_async_remote_copy(
-            src_ref=wy_ref.at[0], dst_ref=wx_ref.at[k - 1], send_sem=x_send.at[k - 1], recv_sem=x_recv.at[k - 1],
-            device_id={'cp': lax.rem(me_c + 2 * k, cp_size)}, device_id_type=MESH)
-        for k in range(1, cp_size // 2)]
     for hop in y_hops:
         hop.start()
     for load in loads:
         load.wait()
 
+    def piece(i):
+        return rows_at(i * bq, bq)
+
     def init_step(b, _):
-        rows = rows_at(b * bq, bq)
+        rows = piece(b)
         kt_ref[:, rows] = qkv[1, rows, :].T
-        dk_acc[:, rows] = jnp.zeros((HEAD_DIM, bq), F32)
-        dv_acc[:, rows] = jnp.zeros((HEAD_DIM, bq), F32)
+        qt_ref[:, rows] = qkv[0, rows, :].T
+        dot_ref[:, rows] = do_v[rows, :].T
+        prod = do_v[rows, :].astype(F32) * o_v[rows, :].astype(F32)
+        delta_v[b] = jnp.broadcast_to(jnp.sum(prod.T, axis=0, keepdims=True), (8, bq))
+        for acc in (dq_acc, dk_acc, dv_acc):
+            acc[:, rows] = jnp.zeros((HEAD_DIM, bq), F32)
         return 0
 
     lax.fori_loop(0, nblk, init_step, 0)
 
-    def src_of(i):
-        return grads.at[:, rows_at(i * bq, bq), :]
-
-    def dst_of(part, head):
-        return rows_ref.at[:, rows_at(part * bq, bq), rows_at(head * HEAD_DIM, HEAD_DIM)]
-
-    def q_step(back, _):
-        i = nblk - 1 - back
-        rows = rows_at(i * bq, bq)
-        q = qkv[0, rows, :]
-        do = do_v[rows, :]
-        prod = do.astype(F32) * o_v[rows, :].astype(F32)
-        delta = jnp.sum(prod.T, axis=0, keepdims=True)
-        lse = l_v[i][0:1, :]
-        dqt_ref[...] = jnp.zeros_like(dqt_ref)
-        qt_ref[...] = q.T
-        dot_ref[...] = do.T
-
-        @pl.when(back == 3)
+    def half_pair(r, q, k, prev, masked):
+        sl = slice(r * sub, (r + 1) * sub)
+        krows = rows_at(k * bq + r * sub, sub)
+        if prev is not None:
+            prev_q, prev_k = piece(prev[0]), rows_at(prev[1] * bq + r * sub, sub)
+            old_p, old_ds_t, old_ds = p_ref[:, sl], ds_ref[sl, :], dst_ref[:, sl]
+        s = dot_nt(qkv[1, krows, :], qkv[0, piece(q), :])
+        if prev is not None:
+            dv_acc[:, prev_k] += dot_nn(dot_ref[:, prev_q], old_p)
+        p = jnp.exp2(s * c - l_v[q][0:1, :])
+        if masked:
+            kk = lax.broadcasted_iota(jnp.int32, (sub, bq), 0) + r * sub
+            p = jnp.where(kk <= lax.broadcasted_iota(jnp.int32, (sub, bq), 1), p, 0.0)
+        p = p.astype(BF16)
+        dp = dot_nt(qkv[2, krows, :], do_v[piece(q), :])
+        if prev is not None:
+            dk_acc[:, prev_k] += dot_nn(qt_ref[:, prev_q], old_ds)
+        ds = (p.astype(F32) * (dp - delta_v[q][0:1, :])).astype(BF16)
+        out = dot_nn(kt_ref[:, prev_k], old_ds_t) if prev is not None else None
+        p_ref[:, sl], ds_ref[sl, :], dst_ref[:, sl] = p.T, ds, ds.T
+        return out
+
+    def pair(q, k, prev, masked=False):
+        out = half_pair(0, q, k, prev, masked)
+        out = out + half_pair(1, q, k, prev, masked)
+        dq_acc[:, piece(prev[0])] += out
+        return q, k
+
+    def send_q(i, start):
+        send_piece(cp_size, i, grads.at[pl.ds(0, 1), piece(i), :], lambda part, head: rows_ref.at[pl.ds(0, 1), piece(part), rows_at(head * HEAD_DIM, HEAD_DIM)],
+                   send.at[0], recv.at[0], local.at[0], start)
+
+    def send_kv(i, start):
+        send_piece(cp_size, i, grads.at[pl.ds(1, 2), piece(i), :], lambda part, head: rows_ref.at[pl.ds(1, 2), piece(part), rows_at(head * HEAD_DIM, HEAD_DIM)],
+                   send.at[1], recv.at[1], local.at[1], start)
+
+    def finish_q(i):
+        grads[0, piece(i), :] = (dq_acc[:, piece(i)] * scale).T.astype(BF16)
+        send_q(i, True)
+
+    def finish_kv(i):
+        grads[1, piece(i), :] = (dk_acc[:, piece(i)] * scale).T.astype(BF16)
+        grads[2, piece(i), :] = dv_acc[:, piece(i)].T.astype(BF16)
+        send_kv(i, True)
+
+    for r in range(2):
+        half_pair(r, 0, 0, None, True)
+    prev = lax.fori_loop(1, nblk, lambda i, prev: pair(i, i, prev, True), (0, 0))
+
+    def late_column(k, prev):
+        prev = pair(k + 1, k, prev)
+        finish_kv(jnp.where(k == half_blk, nblk - 1, k - 1))
+        return lax.fori_loop(k + 2, nblk, lambda q, prev: pair(q, k, prev), prev)
+
+    prev = lax.fori_loop(half_blk, nblk - 1, late_column, prev)
+
+    def row(q, prev):
+        prev = pair(q, 0, prev)
+
+        @pl.when(q == 1)
         def _():
-            y_hops[0].wait_recv()
-            for hop in x_hops:
-                hop.start()
-
-        def make(blk, r, masked):
-            krows = rows_at(blk * bq + r * sub, sub)
-            s = dot_nt(qkv[1, krows, :], q)
-            dp = dot_nt(qkv[2, krows, :], do)
-            p = jnp.exp2(s * c - lse)
-            if masked:
-                kk = lax.broadcasted_iota(jnp.int32, (sub, bq), 0) + r * sub
-                qq = lax.broadcasted_iota(jnp.int32, (sub, bq), 1)
-                p = jnp.where(kk <= qq, p, 0.0)
-            pb = p.astype(BF16)
-            ds = (pb.astype(F32) * (dp - delta)).astype(BF16)
-            return pb.T, ds, ds.T
-
-        def put(r, made):
-            sl = slice(r * sub, (r + 1) * sub)
-            p_ref[:, sl], ds_ref[sl, :], dst_ref[:, sl] = made
-
-        def take(r):
-            sl = slice(r * sub, (r + 1) * sub)
-            return p_ref[:, sl], ds_ref[sl, :], dst_ref[:, sl]
-
-        def flush(blk, r, p, ds_t, ds):
-            krows = rows_at(blk * bq + r * sub, sub)
-            dv_acc[:, krows] += dot_nn(dot_ref[...], p)
-            dk_acc[:, krows] += dot_nn(qt_ref[...], ds)
-            return dot_nn(kt_ref[:, krows], ds_t)
-
-        for r in range(2):
-            put(r, make(i, r, True))
-
-        def body(t, _):
-            cur = jnp.where(t == 0, i, t - 1)
-            out = None
-            for r in range(2):
-                old = take(r)
-                new = make(t, r, False)
-                d = flush(cur, r, *old)
-                out = d if out is None else out + d
-                put(r, new)
-            dqt_ref[...] += out
-            return 0
-
-        lax.fori_loop(0, i, body, 0)
-        cur = jnp.where(i == 0, i, i - 1)
-        out = flush(cur, 0, *take(0)) + flush(cur, 1, *take(1))
-        grads[0, rows, :] = ((dqt_ref[...] + out) * scale).T.astype(BF16)
-        grads[1, rows, :] = (dk_acc[:, rows] * scale).T.astype(BF16)
-        grads[2, rows, :] = dv_acc[:, rows].T.astype(BF16)
-        send_piece(cp_size, i, src_of(i), dst_of, send, recv, local, True)
+            finish_kv(nblk - 2)
+
+        finish_q(q - 1)
+        return lax.fori_loop(1, jnp.minimum(q, half_blk), lambda k, prev: pair(q, k, prev), prev)
+
+    rows_done = half_blk + 2
+    prev = lax.fori_loop(1, rows_done, row, prev)
+
+    def column(n, prev):
+        def key(n):
+            return jnp.where(n < half_blk // 2, 2 * n, 2 * (n - half_blk // 2) + 1)
+
+        prev = pair(rows_done, key(n), prev)
+
+        @pl.when(n == 0)
+        def _():
+            finish_q(rows_done - 1)
+
+        @pl.when(n > 0)
+        def _():
+            finish_kv(key(n - 1))
+
+        return lax.fori_loop(rows_done + 1, nblk, lambda q, prev: pair(q, key(n), prev), prev)
+
+    if rows_done < nblk:
+        prev = lax.fori_loop(0, half_blk, column, prev)
+    last_q, last_k = piece(prev[0]), piece(prev[1])
+    dv_acc[:, last_k] += dot_nn(dot_ref[:, last_q], p_ref[...])
+    dk_acc[:, last_k] += dot_nn(qt_ref[:, last_q], dst_ref[...])
+    dq_acc[:, last_q] += dot_nn(kt_ref[:, last_k], ds_ref[...])
+    if rows_done < nblk:
+        finish_kv(half_blk - 1)
+        lax.fori_loop(rows_done, nblk, lambda q, _: (finish_q(q), 0)[1], 0)
+    else:
+        lax.fori_loop(0, half_blk, lambda k, _: (finish_kv(k), 0)[1], 0)
+        finish_q(rows_done - 1)
+
+    def sent(i, _):
+        send_q(i, False)
+        send_kv(i, False)
         return 0
 
-    lax.fori_loop(0, nblk, q_step, 0)
-    wait_pieces(cp_size, src_of, dst_of, send, recv, local)
-    for k, hop in enumerate(y_hops):
-        hop.wait_send() if k == 0 else hop.wait()
-    for hop in x_hops:
+    lax.fori_loop(0, nblk, sent, 0)
+    for d in range(1, cp_size):
+        peer = lax.rem(me_c + d, cp_size)
+        for half in range(2):
+            for kind, parts in enumerate((pl.ds(0, 1), pl.ds(1, 2))):
+                pltpu.make_async_remote_copy(
+                    src_ref=grads.at[parts, piece(0), :], dst_ref=rows_ref.at[parts, piece(half), rows_at(peer * HEAD_DIM, HEAD_DIM)],
+                    send_sem=send.at[kind, 0], recv_sem=recv.at[kind, peer, half],
+                    device_id={'cp': peer}, device_id_type=MESH).wait_recv()
+    for hop in y_hops:
         hop.wait()
 
 
@@ -548,32 +595,27 @@
     share = cols // cp_size
     bq = seq // (2 * cp_size)
     pairs = seq * seq // 2
+    turned = pltpu.VMEM((HEAD_DIM, seq), BF16)
+    total = pltpu.VMEM((HEAD_DIM, seq), F32)
+    square = pltpu.VMEM((bq, bq), BF16)
     return pl.pallas_call(
         functools.partial(backward_kernel, cp_size, tp_size),
         out_shape=(
             jax.ShapeDtypeStruct((3, 2 * bq, cp_size * HEAD_DIM), BF16),
             jax.ShapeDtypeStruct((tp_size - 1, block, cols), BF16),
             jax.ShapeDtypeStruct((tp_size - 1, share, width), BF16),
-            jax.ShapeDtypeStruct((max(1, cp_size // 2 - 1), share, width), BF16),
         ),
         in_specs=[ANYWHERE] * 6,
-        out_specs=(ANYWHERE,) * 4,
+        out_specs=(ANYWHERE,) * 3,
         scratch_shapes=[
             pltpu.VMEM((3, seq, HEAD_DIM), BF16),
             pltpu.VMEM((seq, HEAD_DIM), BF16),
             pltpu.VMEM((seq, HEAD_DIM), BF16),
             pltpu.VMEM((seq // bq, 8, bq), F32),
-            pltpu.VMEM((HEAD_DIM, seq), BF16),
-            pltpu.VMEM((bq, bq), BF16),
-            pltpu.VMEM((bq, bq), BF16),
-            pltpu.VMEM((bq, bq), BF16),
-            pltpu.VMEM((HEAD_DIM, bq), BF16),
-            pltpu.VMEM((HEAD_DIM, bq), BF16),
-            pltpu.VMEM((HEAD_DIM, bq), F32),
-            pltpu.VMEM((HEAD_DIM, seq), F32),
-            pltpu.VMEM((HEAD_DIM, seq), F32),
+            pltpu.VMEM((seq // bq, 8, bq), F32),
+            turned, turned, turned, square, square, square, total, total, total,
             pltpu.VMEM((3, seq, HEAD_DIM), BF16),
-            DMA((4,)), DMA((2 * cp_size,)), DMA((cp_size, 2)), DMA((2,)), DMA((6,)), DMA((6,)), DMA((cp_size,)), DMA((cp_size,)),
+            DMA((4,)), DMA((2, 2 * cp_size)), DMA((2, cp_size, 2)), DMA((2, 2)), DMA((6,)), DMA((6,)),
         ],
         compiler_params=params(2),
         cost_estimate=pl.CostEstimate(flops=10 * pairs * HEAD_DIM, bytes_accessed=16 * seq * HEAD_DIM, transcendentals=pairs),
@@ -581,8 +623,8 @@
     )(qkv, do, o, lse, o_rows, w_out)
 
 
-def reduce_kernel(cp_size, tp_size, chunks, rows_ref, wq_ref, wk_ref, wv_ref, o_rows_ref, oy_ref, wo_ref, wy_ref, wx_ref,
-                  out_ref, y_ref, wx2_ref, sib_ref,
+def reduce_kernel(cp_size, tp_size, chunks, rows_ref, wq_ref, wk_ref, wv_ref, o_rows_ref, oy_ref, wo_ref, wy_ref,
+                  out_ref, y_ref, wx_ref, sib_ref,
                   g_v, w_v, part, mid, last, out_v, stage, y_acc, o_v, in_sem, w_sem, out_sem, sends, recvs,
                   x_send, x_recv, d_send, d_recv, o_sem, s_sem):
     me, right, left = ring('tp', tp_size)
@@ -601,53 +643,59 @@
     for a in range(3):
         w_load(0, a).start()
     me_c, mate = lax.axis_index('cp'), partner()
-    steps = range(1, cp_size // 2)
-    meet(*beside(tp_size), {'cp': mate}, *({'cp': lax.rem(me_c + 2 * k, cp_size)} for k in steps))
+    chips = cp_size // 2
+    ahead, behind = lax.rem(me_c + 2, cp_size), lax.rem(me_c + cp_size - 2, cp_size)
+    nearest = (1, chips - 1) if chips > 2 else (1,)
+    meet(*beside(tp_size), {'cp': mate}, *({'cp': peer} for peer in (ahead, behind)[:len(nearest)]))
+    share = wy_ref.shape[1]
 
     def share_ref(s, k):
-        if k == 0:
-            return wy_ref.at[s]
-        return wx_ref.at[k - 1] if s == 0 else wx2_ref.at[s - 1, k - 1]
-
-    def along(s, k):
+        return wy_ref.at[s] if k == 0 else wx_ref.at[s, k - 1]
+
+    def x_copy(s, n, src, dst, peer):
         return pltpu.make_async_remote_copy(
-            src_ref=wy_ref.at[s], dst_ref=wx2_ref.at[s - 1, k - 1], send_sem=x_send.at[s - 1, k - 1], recv_sem=x_recv.at[s - 1, k - 1],
-            device_id={'cp': lax.rem(me_c + 2 * k, cp_size)}, device_id_type=MESH)
+            src_ref=src, dst_ref=dst, send_sem=x_send.at[s, n], recv_sem=x_recv.at[s, n], device_id={'cp': peer}, device_id_type=MESH)
+
+    def along(s, n):
+        return x_copy(s, n, wy_ref.at[s], wx_ref.at[s, nearest[n] - 1], (ahead, behind)[n])
+
+    def relay(s, n):
+        rows = pl.ds(n * (share // 2), share // 2)
+        return x_copy(s, 2 + n, wx_ref.at[s, nearest[n] - 1, rows, :], wx_ref.at[s, 1, rows, :], (ahead, behind)[n])
 
     def across(s, k):
         return pltpu.make_async_remote_copy(
             src_ref=share_ref(s, k), dst_ref=sib_ref.at[s, k], send_sem=d_send.at[s, k], recv_sem=d_recv.at[s, k],
             device_id={'cp': mate}, device_id_type=MESH)
 
-    for s in range(1, tp_size - 1):
-        for k in steps:
-            along(s, k).start()
-    for s in range(tp_size - 1):
+    slots = range(tp_size - 1)
+    for s in slots:
+        for n in range(len(nearest)):
+            along(s, n).start()
         across(s, 0).start()
-    for k in steps:
-        across(0, k).start()
     o_loads = [pltpu.make_async_copy(o_rows_ref.at[rows_at(me * (o_rows_ref.shape[0] // tp_size), o_rows_ref.shape[0] // tp_size), :], o_v.at[0], o_sem.at[0])]
     for s in range(tp_size - 1):
         o_loads.append(pltpu.make_async_copy(oy_ref.at[s], o_v.at[s + 1], o_sem.at[s + 1]))
     for copy in o_loads:
         copy.start()
 
+    kinds = ('far_r', 'far_l', 'plain_r', 'plain_l', 'sum_r', 'sum_l')
+
     def hop(kind, n):
         cols = rows_at(n * wide, wide)
         src, dst, peer = {
-            'far_r': (part.at[0, low, cols], mid.at[0, :, cols], right),
-            'far_l': (part.at[0, high, cols], mid.at[1, :, cols], left),
-            'plain_r': (part.at[1, high, cols], last.at[0, high, cols], right),
-            'plain_l': (part.at[2, low, cols], last.at[1, low, cols], left),
-            'sum_r': (part.at[1, low, cols], last.at[0, low, cols], right),
-            'sum_l': (part.at[2, high, cols], last.at[1, high, cols], left),
+            'far_r': (part.at[FAR, low, cols], mid.at[0, :, cols], right),
+            'far_l': (part.at[FAR, high, cols], mid.at[1, :, cols], left),
+            'plain_r': (part.at[RIGHT, high, cols], last.at[0, high, cols], right),
+            'plain_l': (part.at[LEFT, low, cols], last.at[1, low, cols], left),
+            'sum_r': (part.at[RIGHT, low, cols], last.at[0, low, cols], right),
+            'sum_l': (part.at[LEFT, high, cols], last.at[1, high, cols], left),
         }[kind]
-        k = ('far_r', 'far_l', 'plain_r', 'plain_l', 'sum_r', 'sum_l').index(kind)
+        k = kinds.index(kind)
         return pltpu.make_async_remote_copy(
             src_ref=src, dst_ref=dst, send_sem=sends.at[k, n], recv_sem=recvs.at[k, n], device_id={'tp': peer}, device_id_type=MESH)
 
     load.wait()
-    owners = (far, right, left, me)
 
     def compute(n, _):
         slot = lax.rem(n, 2)
@@ -660,36 +708,43 @@
         for a in range(3):
             w_load(n, a).wait()
         cols = rows_at(n * wide, wide)
-        for k in range(4):
-            rows = rows_at(owners[k] * block, block)
+        ready = {FAR: ('far_r', 'far_l'), RIGHT: ('plain_r',), LEFT: ('plain_l',), OWN: ()}
+        for k, owner in enumerate((far, right, left, me)):
+            rows = rows_at(owner * block, block)
             total = dot_nt(g_v[0, rows, :], w_v[slot, 0])
             total = total + dot_nt(g_v[1, rows, :], w_v[slot, 1])
             part[k, :, cols] = total + dot_nt(g_v[2, rows, :], w_v[slot, 2])
-        for kind in ('far_r', 'far_l', 'plain_r', 'plain_l'):
-            hop(kind, n).start()
+            for kind in ready[k]:
+                hop(kind, n).start()
         return 0
 
     lax.fori_loop(0, chunks, compute, 0)
+    for s in slots:
+        for n, k in enumerate(nearest):
+            along(s, n).wait_recv()
+            if chips > 2:
+                relay(s, n).start()
+            across(s, k).start()
 
     def forward_sums(n, _):
         cols = rows_at(n * wide, wide)
         hop('far_r', n).wait_recv()
-        part[1, :half, cols] += mid[0, :, cols]
+        part[RIGHT, :half, cols] += mid[0, :, cols]
         hop('sum_r', n).start()
         hop('far_l', n).wait_recv()
-        part[2, half:, cols] += mid[1, :, cols]
+        part[LEFT, half:, cols] += mid[1, :, cols]
         hop('sum_l', n).start()
         return 0
 
     lax.fori_loop(0, chunks, forward_sums, 0)
 
-    for s in range(1, tp_size - 1):
-        for k in steps:
-            along(s, k).wait_recv()
-            across(s, k).start()
+    if chips > 2:
+        for s in slots:
+            for n in range(2):
+                relay(s, n).wait_recv()
+            across(s, 2).start()
     for copy in o_loads:
         copy.wait()
-    share = wy_ref.shape[1]
     span = stage.shape[2]
     halves = y_acc.shape[1] // span
 
@@ -751,7 +806,7 @@
         cols = rows_at(n * wide, wide)
         for kind in ('plain_r', 'plain_l', 'sum_r', 'sum_l'):
             hop(kind, n).wait_recv()
-        out_v[:, cols] = (part[3, :, cols] + last[0, :, cols] + last[1, :, cols]).astype(BF16)
+        out_v[:, cols] = (part[OWN, :, cols] + last[0, :, cols] + last[1, :, cols]).astype(BF16)
         put(n).start()
         return 0
 
@@ -759,19 +814,21 @@
 
     def close(n, _):
         put(n).wait()
-        for kind in ('far_r', 'far_l', 'plain_r', 'plain_l', 'sum_r', 'sum_l'):
+        for kind in kinds:
             hop(kind, n).wait_send()
         return 0
 
     lax.fori_loop(0, chunks, close, 0)
-    for s in range(tp_size - 1):
-        for k in range(cp_size // 2):
+    for s in slots:
+        for k in range(chips):
             across(s, k).wait_send()
-            if s > 0 and k > 0:
-                along(s, k).wait_send()
-
-
-def reduce_out(grad_rows, weights, o_rows, oy, w_out, wy, wx, cp_size, tp_size):
+        for n in range(len(nearest)):
+            along(s, n).wait_send()
+            if chips > 2:
+                relay(s, n).wait_send()
+
+
+def reduce_out(grad_rows, weights, o_rows, oy, w_out, wy, cp_size, tp_size):
     width, cols = weights[0].shape
     share = wy.shape[1]
     pairs = cp_size // 2
@@ -784,10 +841,10 @@
         out_shape=(
             jax.ShapeDtypeStruct((block, width), BF16),
             jax.ShapeDtypeStruct((block, width), BF16),
-            jax.ShapeDtypeStruct((tp_size - 2, max(1, pairs - 1), share, width), BF16),
+            jax.ShapeDtypeStruct((tp_size - 1, pairs - 1, share, width), BF16),
             jax.ShapeDtypeStruct((tp_size - 1, pairs, share, width), BF16),
         ),
-        in_specs=[ANYWHERE] * 9,
+        in_specs=[ANYWHERE] * 8,
         out_specs=(ANYWHERE,) * 4,
         scratch_shapes=[
             pltpu.VMEM((3, rows, cols), BF16),
@@ -796,17 +853,17 @@
             pltpu.VMEM((2, block // 2, width), F32),
             pltpu.VMEM((2, block, width), F32),
             pltpu.VMEM((block, width), BF16),
-            pltpu.VMEM((2, cols, width // 2), BF16),
+            pltpu.VMEM((2, cols, width // 4), BF16),
             pltpu.VMEM((block, width), F32),
             pltpu.VMEM((tp_size, block, cols), BF16),
             DMA, DMA((2, 3)), DMA((chunks,)), DMA((6, chunks)), DMA((6, chunks)),
-            DMA((tp_size - 2, pairs)), DMA((tp_size - 2, pairs)), DMA((tp_size - 1, pairs)), DMA((tp_size - 1, pairs)),
+            DMA((tp_size - 1, 4)), DMA((tp_size - 1, 4)), DMA((tp_size - 1, pairs)), DMA((tp_size - 1, pairs)),
             DMA((tp_size,)), DMA((2, cp_size)),
         ],
         compiler_params=params(3),
         cost_estimate=pl.CostEstimate(flops=6 * rows * width * cols, bytes_accessed=6 * width * cols, transcendentals=0),
         name="project_reduce",
-    )(grad_rows, *weights, o_rows, oy, w_out, wy, wx)
+    )(grad_rows, *weights, o_rows, oy, w_out, wy)
 
 
 def solution(mesh):
@@ -817,8 +874,8 @@
         weights = (w_query, w_key, w_value)
         qkv, dy1 = project(x_blk, dy_blk, weights, cp_size, tp_size)
         o, lse, o_rows, do = forward(qkv, dy_blk, dy1, w_out, cp_size, tp_size)
-        grad_rows, oy, wy, wx = backward(qkv, do, o, lse, o_rows, w_out, cp_size, tp_size)
-        dx_blk, y_blk, _, _ = reduce_out(grad_rows, weights, o_rows, oy, w_out, wy, wx, cp_size, tp_size)
+        grad_rows, oy, wy = backward(qkv, do, o, lse, o_rows, w_out, cp_size, tp_size)
+        dx_blk, y_blk, _, _ = reduce_out(grad_rows, weights, o_rows, oy, w_out, wy, cp_size, tp_size)
         return y_blk, dx_blk
 
     weight = P(None, 'tp')

time: 489 us -> 459 us (0.939)
  Pallas kernels: 484 us -> 451 us
    pallas_call x1, Pallas kernels: 150 us -> 119 us  [backward(): pl.pallas_call(functools.partial(backward_kernel, cp_size, tp_size), out_...]
where the time goes in v4:
time: 459 us; the launch traced here: 456 us
  Pallas kernels  451 us (98%)
  local copies, waits for them, and re-layouts  4.6 us (1%)
    pallas_call x1, Pallas kernels, reduce_out(): pl.pallas_call(functools.partial(reduce_kernel, cp_size, tp_size, chunks)...  145 us
    pallas_call x1, Pallas kernels, backward(): pl.pallas_call(functools.partial(backward_kernel, cp_size, tp_size), out_...  119 us
    pallas_call x1, Pallas kernels, project(): pl.pallas_call(functools.partial(project_kernel, cp_size, tp_size), out_s...  99.1 us
    pallas_call x1, Pallas kernels, forward(): pl.pallas_call(functools.partial(forward_kernel, cp_size, tp_size), out_s...  87.8 us

profile of v4, /device:TPU:97, one launch (start us, length us, event | category | flops | bytes accessed | tf_op | source)
XLA Modules:
  0.0 456.5 jit_solution(16157533404972828899)
XLA Ops:
  0.6 99.1 %project_qkv.1 = (bf16[3,8192,128]{2,1,0:T(8,128)(2,1)}, bf16[128,4096]{1,0:T(8,128)(2,1)}) custom-call(bf16[256,4096]{1,0:T(8,128)(2,1)} %x_ref.1, bf16[256,4096]{1,0:T(8,128)(2,1)} %dy_ref.3, bf16[4096,1024]{1,0:T(8,128)(2,1)} %wq_ref.3, bf16[4096,1024]{1,0:T(8,128)(2,1)} %wk_ref.3, bf16[4096,1024]{1,0:T(8,128)(2,1)} %wv_ref.3), custom_call_target="tpu_custom_call" | custom-call | flops 25769803776 | bytes 25165824 | tf_op jit(solution)/shard_map/project_qkv/pallas_call | solution.py:207
  99.8 87.8 %attention_forward.1 = (bf16[8192,128]{1,0:T(8,128)(2,1)}, f32[16,8,512]{2,1,0:T(8,128)}, bf16[1024,1024]{1,0:T(8,128)(2,1)}, bf16[1,8192,128]{2,1,0:T(8,128)(2,1)}) custom-call(bf16[3,8192,128]{2,1,0:T(8,128)(2,1)} %get-tuple-element.13.qkv_ref, bf16[256,4096]{1,0:T(8,128)(2,1)} %dy_ref.3, bf16[128,4096]{1,0:T(8,128)(2,1)} %get-tuple-element.14.dy1_ref, ...), custom_call_target="tpu_custom_call" | custom-call | flops 17179869184 | bytes 8388608 | tf_op jit(solution)/shard_map/attention_forward/pallas_call | solution.py:397
  187.5 118.9 %attention_backward.1 = (bf16[3,1024,1024]{2,1,0:T(8,128)(2,1)}, bf16[3,256,1024]{2,1,0:T(8,128)(2,1)}, bf16[3,128,4096]{2,1,0:T(8,128)(2,1)}) custom-call(bf16[3,8192,128]{2,1,0:T(8,128)(2,1)} %get-tuple-element.13.qkv_ref, bf16[1,8192,128]{2,1,0:T(8,128)(2,1)} %get-tuple-element.15.do_ref, bf16[8192,128]{1,0:T(8,128)(2,1)} %get-tuple-element.16.o_ref, ...), custom_call_target="tpu_custom_call" | custom-call | flops 42949672960 | bytes 16777216 | tf_op jit(solution)/shard_map/attention_backward/pallas_call | solution.py:601
  306.4 145.5 %project_reduce.1 = (bf16[256,4096]{1,0:T(8,128)(2,1)}, bf16[256,4096]{1,0:T(8,128)(2,1)}, bf16[3,3,128,4096]{3,2,1,0:T(8,128)(2,1)}, bf16[3,4,128,4096]{3,2,1,0:T(8,128)(2,1)}) custom-call(bf16[3,1024,1024]{2,1,0:T(8,128)(2,1)} %get-tuple-element.19.rows_ref, bf16[4096,1024]{1,0:T(8,128)(2,1)} %wq_ref.3, bf16[4096,1024]{1,0:T(8,128)(2,1)} %wk_ref.3, ...), custom_call_target="tpu_custom_call" | custom-call | flops 25769803776 | bytes 25165824 | tf_op jit(solution)/shard_map/project_reduce/pallas_call | solution.py:839
  451.9 0.0 copy-start
  451.9 3.3 copy.10
  455.2 0.0 copy-done
  455.2 1.3 copy.11
Async XLA Ops:
  451.9 3.3 copy-start

commit v5 on v4

--- a/solution.py
+++ b/solution.py
@@ -64,23 +64,6 @@
     return sorted(range(1, cp_size), key=lambda d: -min(d, cp_size - d))
 
 
-def row_groups(tp_size, block, split_last):
-    me, right, left = ring('tp', tp_size)
-    far = lax.rem(me + 2, tp_size)
-    half, part = block // 2, block // 4
-    groups = [
-        (0, half, ((me, 0), (me, half))),
-        (block, half, ((right, 0), (left, half))),
-        (2 * block, half, ((right, half), (left, 0))),
-    ]
-    if not split_last:
-        return groups + [(3 * block, half, ((far, 0), (far, half)))]
-    return groups + [
-        (3 * block, part, ((far, 0), (far, half))),
-        (3 * block + half, part, ((far, part), (far, half + part))),
-    ]
-
-
 def position(cp_size, tp_size, block, owner, row):
     piece = block * tp_size // 2
     first = owner < tp_size // 2
@@ -89,72 +72,115 @@
     return piece_id * piece + jnp.where(first, owner, owner - tp_size // 2) * block + row
 
 
+class Gather:
+    STEPS = 6
+
+    def __init__(self, tp_size, src, buf, send, recv):
+        self.src, self.buf, self.sems = src, buf, (send, recv)
+        self.me, self.right, self.left = ring('tp', tp_size)
+        self.far = lax.rem(self.me + 2, tp_size)
+        self.block = src.shape[0]
+        self.part = self.block // 4
+
+    def start_row(self, j):
+        return self.block + (j - 1) * (2 * self.part)
+
+    def rows(self, j, side):
+        return self.buf.at[rows_at(self.start_row(j) + side * self.part, self.part), :]
+
+    def first_row(self, j, side):
+        return lax.rem(j + (1 if side else 3), 4) * self.part
+
+    def parts(self, j):
+        near = j <= 4
+        return (
+            (jnp.where(near, self.right, self.far), self.first_row(j, 0)),
+            (jnp.where(near, self.left, self.far), self.first_row(j, 1)),
+        )
+
+    def hop(self, j, side, relayed, dst=None):
+        src = self.rows(j - 4, side) if relayed else self.src.at[rows_at(self.first_row(j, side), self.part), :]
+        return pltpu.make_async_remote_copy(
+            src_ref=src, dst_ref=self.rows(j, side) if dst is None else dst,
+            send_sem=self.sems[0].at[j - 1, side], recv_sem=self.sems[1].at[j - 1, side],
+            device_id={'tp': self.right if side else self.left}, device_id_type=MESH)
+
+    def start(self, j, relayed):
+        for side in range(2):
+            self.hop(j, side, relayed).start()
+
+    def arrive(self, j):
+        for side in range(2):
+            self.hop(j, side, False).wait_recv()
+
+    def leave(self, j):
+        for side in range(2):
+            self.hop(j, side, False).wait_send()
+
+
 class HeadSender:
-    def __init__(self, cp_size, tp_size, block, groups, res, dst, send, recv, local):
-        self.cp_size, self.tp_size, self.block, self.groups = cp_size, tp_size, block, groups
+    def __init__(self, cp_size, tp_size, gather, res, dst, send, recv, local):
+        self.cp_size, self.tp_size, self.gather = cp_size, tp_size, gather
         self.res, self.dst, self.sems = res, dst, (send, recv, local)
 
-    def copies(self, g):
+    def copies(self, j):
         send, recv, local = self.sems
         me = lax.axis_index('cp')
-        start, length, parts = self.groups[g]
+        own = isinstance(j, int)
+        block = self.gather.block
+        if own:
+            start, length, parts = 0, block // 2, ((self.gather.me, 0), (self.gather.me, block // 2))
+        else:
+            start, length, parts = self.gather.start_row(j), self.gather.part, self.gather.parts(j)
         for n, (owner, row) in enumerate(parts):
-            rows = rows_at(position(self.cp_size, self.tp_size, self.block, owner, row), length)
-            here = pl.ds(start + n * length, length)
+            rows = rows_at(position(self.cp_size, self.tp_size, block, owner, row), length)
+            here = rows_at(start + n * length, length)
             for d in far_first(self.cp_size):
                 peer = lax.rem(me + d, self.cp_size)
                 yield pltpu.make_async_remote_copy(
                     src_ref=self.res.at[peer, :, here, :], dst_ref=self.dst.at[:, rows, :],
-                    send_sem=send.at[d - 1, g, n], recv_sem=recv.at[d - 1, g, n],
+                    send_sem=send.at[d - 1, j, n], recv_sem=recv.at[d - 1, j, n],
                     device_id={'cp': peer}, device_id_type=MESH)
-            yield pltpu.make_async_copy(self.res.at[me, :, here, :], self.dst.at[:, rows, :], local.at[g, n])
-
-    def start(self, g):
-        for copy in self.copies(g):
+            yield pltpu.make_async_copy(self.res.at[me, :, here, :], self.dst.at[:, rows, :], local.at[j, n])
+
+    def start(self, j):
+        for copy in self.copies(j):
             copy.start()
 
     def wait(self):
-        for g in range(len(self.groups)):
-            for copy in self.copies(g):
+        for copy in self.copies(0):
+            copy.wait()
+
+        def step(j, _):
+            for copy in self.copies(j):
                 copy.wait()
-
-
-def head_scratch(cp_size, arrays, rows, groups):
-    return [
-        pltpu.VMEM((cp_size, arrays, rows, HEAD_DIM), BF16),
-        DMA((cp_size - 1, groups, 2)),
-        DMA((cp_size - 1, groups, 2)),
-        DMA((groups, 2)),
-    ]
-
-
-def project_kernel(cp_size, tp_size, x_ref, dy_ref, wq_ref, wk_ref, wv_ref, qkv_ref, dy1_ref, w_v, xg, res, send, recv, local, w_sem, x_sem, y_send, y_recv):
+            return 0
+
+        lax.fori_loop(1, Gather.STEPS + 1, step, 0)
+
+
+def head_scratch(cp_size, arrays, rows):
+    each = (cp_size - 1, Gather.STEPS + 1, 2)
+    return [pltpu.VMEM((cp_size, arrays, rows, HEAD_DIM), BF16), DMA(each), DMA(each), DMA(each[1:])]
+
+
+def project_kernel(cp_size, tp_size, x_ref, dy_ref, wq_ref, wk_ref, wv_ref, qkv_ref, dy1_ref,
+                   w_v, xg, res, send, recv, local, w_sem, x_sem, y_send, y_recv, dy_send, dy_recv):
     block = x_ref.shape[0]
-    half, part = block // 2, block // 4
-    _, right, left = ring('tp', tp_size)
-    groups = row_groups(tp_size, block, True)
-    heads = HeadSender(cp_size, tp_size, block, groups, res, qkv_ref, send, recv, local)
-
-    def pass_on(k, src, dst, peer):
-        copy = pltpu.make_async_remote_copy(
-            src_ref=src, dst_ref=dst, send_sem=y_send.at[k], recv_sem=y_recv.at[k], device_id={'tp': peer}, device_id_type=MESH)
-        copy.start()
-        return copy
-
-    def landed(start, size):
-        return xg.at[pl.ds(start, size), :]
-
-    low, high = x_ref.at[pl.ds(0, half), :], x_ref.at[pl.ds(half, half), :]
-    own = pltpu.make_async_copy(x_ref, landed(0, block), x_sem)
+    gather = Gather(tp_size, x_ref, xg, y_send, y_recv)
+    early = Gather(tp_size, dy_ref, None, dy_send, dy_recv)
+    heads = HeadSender(cp_size, tp_size, gather, res, qkv_ref, send, recv, local)
+    part = gather.part
+
+    def early_hop(side):
+        return early.hop(1, side, False, dy1_ref.at[pl.ds(side * part, part), :])
+
+    own = pltpu.make_async_copy(x_ref, xg.at[pl.ds(0, block), :], x_sem)
     own.start()
     loads = [pltpu.make_async_copy(w, w_v.at[n], w_sem.at[n]) for n, w in enumerate((wq_ref, wk_ref, wv_ref))]
     meet(*others('cp', cp_size), *beside(tp_size))
-    hops = [
-        pass_on(0, low, landed(block, half), left),
-        pass_on(1, high, landed(block + half, half), right),
-        pass_on(2, high, landed(2 * block, half), left),
-        pass_on(3, low, landed(2 * block + half, half), right),
-    ]
+    for j in range(1, 5):
+        gather.start(j, False)
     for load in loads:
         load.start()
     own.wait()
@@ -163,10 +189,7 @@
     cols = wide * HEAD_DIM
     steps = cp_size // wide
 
-    def compute(g, n):
-        start, length, _ = groups[g]
-        rows = pl.ds(start, 2 * length)
-
+    def compute(rows, n):
         def body(s, _):
             out = dot_nn(xg[rows, :], w_v[n, :, rows_at(s * cols, cols)]).astype(BF16)
             for k in range(wide):
@@ -175,44 +198,49 @@
 
         lax.fori_loop(0, steps, body, 0)
 
-    for n in range(3):
-        loads[n].wait()
-        compute(0, n)
+    for n, load in enumerate(loads):
+        load.wait()
+        compute(pl.ds(0, block), n)
     heads.start(0)
-    hops[0].wait_recv()
-    hops.append(pass_on(4, landed(block, part), landed(3 * block, part), left))
-    hops.append(pass_on(5, landed(block + part, part), landed(3 * block + half, part), left))
-    hops[1].wait_recv()
-    hops.append(pass_on(6, landed(block + half, part), landed(3 * block + part, part), right))
-    hops.append(pass_on(7, landed(block + half + part, part), landed(3 * block + half + part, part), right))
-    hops.append(pass_on(8, dy_ref.at[pl.ds(0, part), :], dy1_ref.at[pl.ds(0, part), :], left))
-    hops.append(pass_on(9, dy_ref.at[pl.ds(half, part), :], dy1_ref.at[pl.ds(part, part), :], right))
-    for g, arrived in ((1, ()), (2, (2, 3)), (3, (4, 6)), (4, (5, 7))):
-        for k in arrived:
-            hops[k].wait_recv()
-        for n in range(3):
-            compute(g, n)
-        heads.start(g)
-    for k in range(8):
-        hops[k].wait_send()
-    for k in (8, 9):
-        hops[k].wait()
+
+    def step(j, _):
+        gather.arrive(j)
+
+        @pl.when(j <= 2)
+        def _():
+            gather.start(j + 4, True)
+
+        @pl.when(j == 2)
+        def _():
+            for side in range(2):
+                early_hop(side).start()
+
+        rows = rows_at(gather.start_row(j), 2 * part)
+        lax.fori_loop(0, len(loads), lambda n, _: (compute(rows, n), 0)[1], 0)
+        heads.start(j)
+        return 0
+
+    lax.fori_loop(1, Gather.STEPS + 1, step, 0)
+    lax.fori_loop(1, Gather.STEPS + 1, lambda j, _: (gather.leave(j), 0)[1], 0)
+    for side in range(2):
+        early_hop(side).wait()
     heads.wait()
 
 
 def project(x_blk, dy_blk, weights, cp_size, tp_size):
     block, width = x_blk.shape
     cols = weights[0].shape[1]
-    seq = block * tp_size * cp_size
+    rows = block * tp_size
+    each = DMA((Gather.STEPS, 2))
     return pl.pallas_call(
         functools.partial(project_kernel, cp_size, tp_size),
-        out_shape=(jax.ShapeDtypeStruct((3, seq, HEAD_DIM), BF16), jax.ShapeDtypeStruct((block // 2, width), BF16)),
+        out_shape=(jax.ShapeDtypeStruct((len(weights), rows * cp_size, HEAD_DIM), BF16), jax.ShapeDtypeStruct((block // 2, width), BF16)),
         in_specs=[ANYWHERE] * 5,
         out_specs=(ANYWHERE, ANYWHERE),
-        scratch_shapes=[pltpu.VMEM((3, width, cols), BF16), pltpu.VMEM((4 * block, width), BF16)]
-        + head_scratch(cp_size, 3, 4 * block, 5) + [DMA((3,)), DMA, DMA((10,)), DMA((10,))],
+        scratch_shapes=[pltpu.VMEM((len(weights), width, cols), BF16), pltpu.VMEM((rows, width), BF16)]
+        + head_scratch(cp_size, len(weights), rows) + [DMA((len(weights),)), DMA, each, each, each, each],
         compiler_params=params(0),
-        cost_estimate=pl.CostEstimate(flops=6 * block * tp_size * width * cols, bytes_accessed=6 * width * cols, transcendentals=0),
+        cost_estimate=pl.CostEstimate(flops=6 * rows * width * cols, bytes_accessed=6 * width * cols, transcendentals=0),
         name="project_qkv",
     )(x_blk, dy_blk, *weights)
 
@@ -235,69 +263,30 @@
         copy.start() if start else copy.wait_send()
 
 
-def wait_pieces(cp_size, src_of, dst_of, send, recv, local):
-    me = lax.axis_index('cp')
-
-    def sent(i, _):
-        send_piece(cp_size, i, src_of(i), dst_of, send, recv, local, False)
-        return 0
-
-    lax.fori_loop(0, 2 * cp_size, sent, 0)
-    for d in range(1, cp_size):
-        peer = lax.rem(me + d, cp_size)
-        for half in range(2):
-            pltpu.make_async_remote_copy(
-                src_ref=src_of(0), dst_ref=dst_of(half, peer), send_sem=send.at[0], recv_sem=recv.at[peer, half],
-                device_id={'cp': peer}, device_id_type=MESH).wait_recv()
-
-
-def forward_kernel(cp_size, tp_size, qkv_ref, dy_ref, dy1_ref, wo_ref, o_ref, l_ref, rows_ref, do_ref,
-                   qkv, o_v, l_v, vt_ref, s_ref, acc_ref, dyg, wo, res, h_send, h_recv, h_local,
-                   in_sem, send, recv, local, y_send, y_recv, out_sem):
+def forward_kernel(cp_size, tp_size, qkv_ref, dy_ref, dy1_ref, wo_ref, o_ref, ot_ref, l_ref, do_ref,
+                   qkv, o_v, ot_v, l_v, vt_ref, s_ref, acc_ref, dyg, wo, res, h_send, h_recv, h_local, in_sem, y_send, y_recv, out_sem):
     seq = qkv.shape[1]
     bq = s_ref.shape[0]
     nblk = seq // bq
     c = HEAD_DIM ** -0.5 * LOG2E
-    _, right, left = ring('tp', tp_size)
-    block = dy_ref.shape[0]
-    half, part = block // 2, block // 4
-    groups = row_groups(tp_size, block, False)
-    heads = HeadSender(cp_size, tp_size, block, groups, res, do_ref, h_send, h_recv, h_local)
-
-    def gathered(start, size):
-        return dyg.at[pl.ds(start, size), :]
+    gather = Gather(tp_size, dy_ref, dyg, y_send, y_recv)
+    heads = HeadSender(cp_size, tp_size, gather, res, do_ref, h_send, h_recv, h_local)
+    block, part = gather.block, gather.part
 
     loads = [
-        pltpu.make_async_copy(dy_ref, gathered(0, block), in_sem.at[0]),
-        pltpu.make_async_copy(wo_ref, wo, in_sem.at[1]),
-        pltpu.make_async_copy(dy1_ref.at[pl.ds(0, part), :], gathered(block, part), in_sem.at[2]),
-        pltpu.make_async_copy(dy1_ref.at[pl.ds(part, part), :], gathered(block + half, part), in_sem.at[3]),
-        pltpu.make_async_copy(qkv_ref, qkv, in_sem.at[4]),
-    ]
+        pltpu.make_async_copy(src, dst, in_sem.at[n])
+        for n, (src, dst) in enumerate(((dy_ref, dyg.at[pl.ds(0, block), :]), (wo_ref, wo), (dy1_ref, dyg.at[pl.ds(block, 2 * part), :]), (qkv_ref, qkv)))]
     for load in loads:
         load.start()
     meet(*others('cp', cp_size), *beside(tp_size))
-    hops = [
-        pltpu.make_async_remote_copy(
-            src_ref=src, dst_ref=gathered(start, size), send_sem=y_send.at[k], recv_sem=y_recv.at[k],
-            device_id={'tp': peer}, device_id_type=MESH)
-        for k, (src, start, size, peer) in enumerate((
-            (dy_ref.at[pl.ds(part, part), :], block + part, part, left),
-            (dy_ref.at[pl.ds(half + part, part), :], block + half + part, part, right),
-            (dy_ref.at[pl.ds(half, half), :], 2 * block, half, left),
-            (dy_ref.at[pl.ds(0, half), :], 2 * block + half, half, right),
-            (dy1_ref.at[pl.ds(0, part), :], 3 * block, part, left),
-            (dy1_ref.at[pl.ds(part, part), :], 3 * block + half, part, right),
-            (gathered(block + part, part), 3 * block + part, part, left),
-            (gathered(block + half + part, part), 3 * block + half + part, part, right)))]
-    for hop in hops[:6]:
-        hop.start()
+    for j in range(2, 5):
+        gather.start(j, False)
 
     per_step = min(4, cp_size)
     cols = per_step * HEAD_DIM
 
-    def compute(g):
-        rows = pl.ds(groups[g][0], block)
+    def compute(n):
+        rows = rows_at(n * block, block)
 
         def body(s, _):
             out = dot_nt(dyg[rows, :], wo[rows_at(s * cols, cols), :]).astype(BF16)
@@ -306,13 +295,19 @@
             return 0
 
         lax.fori_loop(0, cp_size // per_step, body, 0)
-        heads.start(g)
+
+    def compute_steps(n, _):
+        compute(n)
+        lax.fori_loop(2 * n - 1, 2 * n + 1, lambda j, _: (heads.start(j), 0)[1], 0)
+        return 0
 
     for load in loads[:2]:
         load.wait()
     compute(0)
+    heads.start(0)
     for load in loads[2:]:
         load.wait()
+    gather.start(5, True)
 
     def transpose_step(b, _):
         rows = rows_at(b * bq, bq)
@@ -321,26 +316,16 @@
 
     lax.fori_loop(0, nblk, transpose_step, 0)
 
-    def src_of(i):
-        return o_v.at[rows_at(i * bq, bq), :]
-
-    def dst_of(part, head):
-        return rows_ref.at[rows_at(part * bq, bq), rows_at(head * HEAD_DIM, HEAD_DIM)]
-
     def q_step(i, _):
         @pl.when(i == nblk // 2)
         def _():
-            for arrived, hop in zip(hops, hops[6:]):
-                arrived.wait_recv()
-                hop.start()
-            compute(1)
+            gather.arrive(2)
+            gather.start(6, True)
 
         @pl.when(i == nblk - 1)
         def _():
-            for k, hop in enumerate(hops):
-                hop.wait_send() if k < 2 else hop.wait()
-            compute(2)
-            compute(3)
+            lax.fori_loop(3, Gather.STEPS + 1, lambda j, _: (gather.arrive(j), 0)[1], 0)
+            lax.fori_loop(1, tp_size, compute_steps, 0)
 
         rows = rows_at(i * bq, bq)
         q = qkv[0, rows, :]
@@ -372,20 +357,20 @@
 
         carry = lax.fori_loop(0, i, body, (first, first, jnp.zeros((1, bq), F32)))
         m, _, l = use(jnp.where(i == 0, i, i - 1), *carry, None)
-        o_v[rows, :] = (acc_ref[...] * (1.0 / l)).T.astype(BF16)
+        out = (acc_ref[...] * (1.0 / l)).astype(BF16)
+        ot_v[:, rows] = out
+        o_v[rows, :] = out.T
         l_v[i] = jnp.broadcast_to(m * c + jnp.log2(l), (8, bq))
-        send_piece(cp_size, i, src_of(i), dst_of, send, recv, local, True)
         return 0
 
     lax.fori_loop(0, nblk, q_step, 0)
-    out_o = pltpu.make_async_copy(o_v, o_ref, out_sem.at[0])
-    out_l = pltpu.make_async_copy(l_v, l_ref, out_sem.at[1])
-    out_o.start()
-    out_l.start()
-    wait_pieces(cp_size, src_of, dst_of, send, recv, local)
+    stores = [pltpu.make_async_copy(src, dst, out_sem.at[n]) for n, (src, dst) in enumerate(((o_v, o_ref), (ot_v, ot_ref), (l_v, l_ref)))]
+    for store in stores:
+        store.start()
     heads.wait()
-    out_o.wait()
-    out_l.wait()
+    lax.fori_loop(2, Gather.STEPS + 1, lambda j, _: (gather.leave(j), 0)[1], 0)
+    for store in stores:
+        store.wait()
 
 
 def forward(qkv, dy_blk, dy1, w_out, cp_size, tp_size):
@@ -394,36 +379,38 @@
     block, width = dy_blk.shape
     cols = w_out.shape[0]
     pairs = seq * seq // 2
+    rows, turned = (seq, HEAD_DIM), (HEAD_DIM, seq)
+    logs = (seq // bq, 8, bq)
+    each = DMA((Gather.STEPS, 2))
     return pl.pallas_call(
         functools.partial(forward_kernel, cp_size, tp_size),
         out_shape=(
-            jax.ShapeDtypeStruct((seq, HEAD_DIM), BF16),
-            jax.ShapeDtypeStruct((seq // bq, 8, bq), F32),
-            jax.ShapeDtypeStruct((2 * bq, cp_size * HEAD_DIM), BF16),
+            jax.ShapeDtypeStruct(rows, BF16),
+            jax.ShapeDtypeStruct(turned, BF16),
+            jax.ShapeDtypeStruct(logs, F32),
             jax.ShapeDtypeStruct((1, seq, HEAD_DIM), BF16),
         ),
         in_specs=[ANYWHERE] * 4,
         out_specs=(ANYWHERE,) * 4,
         scratch_shapes=[
-            pltpu.VMEM((3, seq, HEAD_DIM), BF16),
-            pltpu.VMEM((seq, HEAD_DIM), BF16),
-            pltpu.VMEM((seq // bq, 8, bq), F32),
-            pltpu.VMEM((HEAD_DIM, seq), BF16),
+            pltpu.VMEM(qkv.shape, BF16),
+            pltpu.VMEM(rows, BF16),
+            pltpu.VMEM(turned, BF16),
+            pltpu.VMEM(logs, F32),
+            pltpu.VMEM(turned, BF16),
             pltpu.VMEM((bq, bq), F32),
             pltpu.VMEM((HEAD_DIM, bq), F32),
-            pltpu.VMEM((4 * block, width), BF16),
+            pltpu.VMEM((tp_size * block, width), BF16),
             pltpu.VMEM((cols, width), BF16),
-        ] + head_scratch(cp_size, 1, 4 * block, 4) + [
-            DMA((5,)), DMA((2 * cp_size,)), DMA((cp_size, 2)), DMA((2,)), DMA((8,)), DMA((8,)), DMA((2,)),
-        ],
+        ] + head_scratch(cp_size, 1, tp_size * block) + [DMA((4,)), each, each, DMA((3,))],
         compiler_params=params(1),
         cost_estimate=pl.CostEstimate(flops=4 * pairs * HEAD_DIM, bytes_accessed=8 * seq * HEAD_DIM, transcendentals=pairs),
         name="attention_forward",
     )(qkv, dy_blk, dy1, w_out)
 
 
-def backward_kernel(cp_size, tp_size, qkv_ref, do_ref, o_ref, l_ref, o_rows_ref, wo_ref, rows_ref, oy_ref, wy_ref,
-                    qkv, do_v, o_v, l_v, delta_v, kt_ref, qt_ref, dot_ref, p_ref, ds_ref, dst_ref, dq_acc, dk_acc, dv_acc, grads,
+def backward_kernel(cp_size, tp_size, qkv_ref, do_ref, o_ref, ot_ref, l_ref, wo_ref, rows_ref, o_rows_ref, oy_ref, wy_ref,
+                    qkv, do_v, ot_v, l_v, delta_v, kt_ref, qt_ref, dot_ref, p_ref, ds_ref, dst_ref, dq_acc, dk_acc, dv_acc, grads,
                     in_sem, send, recv, local, y_send, y_recv):
     seq = qkv.shape[1]
     bq = p_ref.shape[0]
@@ -434,7 +421,7 @@
     loads = [
         pltpu.make_async_copy(qkv_ref, qkv, in_sem.at[0]),
         pltpu.make_async_copy(do_ref.at[0], do_v, in_sem.at[1]),
-        pltpu.make_async_copy(o_ref, o_v, in_sem.at[2]),
+        pltpu.make_async_copy(ot_ref, ot_v, in_sem.at[2]),
         pltpu.make_async_copy(l_ref, l_v, in_sem.at[3]),
     ]
     for load in loads:
@@ -442,17 +429,16 @@
     meet(*others('cp', cp_size), *others('tp', tp_size))
     me_c, me_t = lax.axis_index('cp'), lax.axis_index('tp')
     share, block = wy_ref.shape[1], oy_ref.shape[1]
-    y_hops = []
+
+    def over_tp(kind, r):
+        peer = lax.rem(me_t + r, tp_size)
+        src, dst = ((wo_ref.at[rows_at(me_c * share, share), :], wy_ref), (o_rows_ref.at[rows_at(peer * block, block), :], oy_ref))[kind]
+        return pltpu.make_async_remote_copy(
+            src_ref=src, dst_ref=dst.at[r - 1], send_sem=y_send.at[kind, r - 1], recv_sem=y_recv.at[kind, r - 1],
+            device_id={'tp': peer}, device_id_type=MESH)
+
     for r in range(1, tp_size):
-        peer = lax.rem(me_t + r, tp_size)
-        y_hops.append((wo_ref.at[rows_at(me_c * share, share), :], wy_ref.at[r - 1], peer))
-        y_hops.append((o_rows_ref.at[rows_at(peer * block, block), :], oy_ref.at[r - 1], peer))
-    y_hops = [
-        pltpu.make_async_remote_copy(
-            src_ref=src, dst_ref=dst, send_sem=y_send.at[k], recv_sem=y_recv.at[k], device_id={'tp': peer}, device_id_type=MESH)
-        for k, (src, dst, peer) in enumerate(y_hops)]
-    for hop in y_hops:
-        hop.start()
+        over_tp(0, r).start()
     for load in loads:
         load.wait()
 
@@ -464,8 +450,8 @@
         kt_ref[:, rows] = qkv[1, rows, :].T
         qt_ref[:, rows] = qkv[0, rows, :].T
         dot_ref[:, rows] = do_v[rows, :].T
-        prod = do_v[rows, :].astype(F32) * o_v[rows, :].astype(F32)
-        delta_v[b] = jnp.broadcast_to(jnp.sum(prod.T, axis=0, keepdims=True), (8, bq))
+        prod = dot_ref[:, rows].astype(F32) * ot_v[:, rows].astype(F32)
+        delta_v[b] = jnp.broadcast_to(jnp.sum(prod, axis=0, keepdims=True), (8, bq))
         for acc in (dq_acc, dk_acc, dv_acc):
             acc[:, rows] = jnp.zeros((HEAD_DIM, bq), F32)
         return 0
@@ -500,22 +486,39 @@
         dq_acc[:, piece(prev[0])] += out
         return q, k
 
-    def send_q(i, start):
-        send_piece(cp_size, i, grads.at[pl.ds(0, 1), piece(i), :], lambda part, head: rows_ref.at[pl.ds(0, 1), piece(part), rows_at(head * HEAD_DIM, HEAD_DIM)],
-                   send.at[0], recv.at[0], local.at[0], start)
-
-    def send_kv(i, start):
-        send_piece(cp_size, i, grads.at[pl.ds(1, 2), piece(i), :], lambda part, head: rows_ref.at[pl.ds(1, 2), piece(part), rows_at(head * HEAD_DIM, HEAD_DIM)],
-                   send.at[1], recv.at[1], local.at[1], start)
+    def source(kind, i):
+        return (grads.at[pl.ds(0, 1), piece(i), :], grads.at[pl.ds(1, 2), piece(i), :], o_ref.at[piece(i), :])[kind]
+
+    def target(kind, part, head):
+        cols = rows_at(head * HEAD_DIM, HEAD_DIM)
+        return (rows_ref.at[pl.ds(0, 1), piece(part), cols], rows_ref.at[pl.ds(1, 2), piece(part), cols], o_rows_ref.at[piece(part), cols])[kind]
+
+    def send_kind(kind, i, start):
+        send_piece(cp_size, i, source(kind, i), functools.partial(target, kind), send.at[kind], recv.at[kind], local.at[kind], start)
+
+    def settle(kind):
+        def sent(i, _):
+            send_kind(kind, i, False)
+            return 0
+
+        lax.fori_loop(0, nblk, sent, 0)
+        for d in range(1, cp_size):
+            peer = lax.rem(me_c + d, cp_size)
+            for half in range(2):
+                pltpu.make_async_remote_copy(
+                    src_ref=source(kind, 0), dst_ref=target(kind, half, peer), send_sem=send.at[kind, 0], recv_sem=recv.at[kind, peer, half],
+                    device_id={'cp': peer}, device_id_type=MESH).wait_recv()
+
+    lax.fori_loop(0, nblk, lambda i, _: (send_kind(2, i, True), 0)[1], 0)
 
     def finish_q(i):
         grads[0, piece(i), :] = (dq_acc[:, piece(i)] * scale).T.astype(BF16)
-        send_q(i, True)
+        send_kind(0, i, True)
 
     def finish_kv(i):
         grads[1, piece(i), :] = (dk_acc[:, piece(i)] * scale).T.astype(BF16)
         grads[2, piece(i), :] = dv_acc[:, piece(i)].T.astype(BF16)
-        send_kv(i, True)
+        send_kind(1, i, True)
 
     for r in range(2):
         half_pair(r, 0, 0, None, True)
@@ -534,6 +537,9 @@
         @pl.when(q == 1)
         def _():
             finish_kv(nblk - 2)
+            settle(2)
+            for r in range(1, tp_size):
+                over_tp(1, r).start()
 
         finish_q(q - 1)
         return lax.fori_loop(1, jnp.minimum(q, half_blk), lambda k, prev: pair(q, k, prev), prev)
@@ -570,28 +576,17 @@
         lax.fori_loop(0, half_blk, lambda k, _: (finish_kv(k), 0)[1], 0)
         finish_q(rows_done - 1)
 
-    def sent(i, _):
-        send_q(i, False)
-        send_kv(i, False)
-        return 0
-
-    lax.fori_loop(0, nblk, sent, 0)
-    for d in range(1, cp_size):
-        peer = lax.rem(me_c + d, cp_size)
-        for half in range(2):
-            for kind, parts in enumerate((pl.ds(0, 1), pl.ds(1, 2))):
-                pltpu.make_async_remote_copy(
-                    src_ref=grads.at[parts, piece(0), :], dst_ref=rows_ref.at[parts, piece(half), rows_at(peer * HEAD_DIM, HEAD_DIM)],
-                    send_sem=send.at[kind, 0], recv_sem=recv.at[kind, peer, half],
-                    device_id={'cp': peer}, device_id_type=MESH).wait_recv()
-    for hop in y_hops:
-        hop.wait()
-
-
-def backward(qkv, do, o, lse, o_rows, w_out, cp_size, tp_size):
+    settle(0)
+    settle(1)
+    for r in range(1, tp_size):
+        over_tp(0, r).wait()
+        over_tp(1, r).wait()
+
+
+def backward(qkv, do, o, ot, lse, w_out, cp_size, tp_size):
     seq = qkv.shape[1]
     cols, width = w_out.shape
-    block = o_rows.shape[0] // tp_size
+    block = seq // (cp_size * tp_size)
     share = cols // cp_size
     bq = seq // (2 * cp_size)
     pairs = seq * seq // 2
@@ -601,26 +596,27 @@
     return pl.pallas_call(
         functools.partial(backward_kernel, cp_size, tp_size),
         out_shape=(
-            jax.ShapeDtypeStruct((3, 2 * bq, cp_size * HEAD_DIM), BF16),
+            jax.ShapeDtypeStruct((3, 2 * bq, cols), BF16),
+            jax.ShapeDtypeStruct((2 * bq, cols), BF16),
             jax.ShapeDtypeStruct((tp_size - 1, block, cols), BF16),
             jax.ShapeDtypeStruct((tp_size - 1, share, width), BF16),
         ),
         in_specs=[ANYWHERE] * 6,
-        out_specs=(ANYWHERE,) * 3,
+        out_specs=(ANYWHERE,) * 4,
         scratch_shapes=[
-            pltpu.VMEM((3, seq, HEAD_DIM), BF16),
+            pltpu.VMEM(qkv.shape, BF16),
             pltpu.VMEM((seq, HEAD_DIM), BF16),
-            pltpu.VMEM((seq, HEAD_DIM), BF16),
-            pltpu.VMEM((seq // bq, 8, bq), F32),
-            pltpu.VMEM((seq // bq, 8, bq), F32),
+            turned,
+            pltpu.VMEM(lse.shape, F32),
+            pltpu.VMEM(lse.shape, F32),
             turned, turned, turned, square, square, square, total, total, total,
-            pltpu.VMEM((3, seq, HEAD_DIM), BF16),
-            DMA((4,)), DMA((2, 2 * cp_size)), DMA((2, cp_size, 2)), DMA((2, 2)), DMA((6,)), DMA((6,)),
+            pltpu.VMEM(qkv.shape, BF16),
+            DMA((4,)), DMA((3, 2 * cp_size)), DMA((3, cp_size, 2)), DMA((3, 2)), DMA((2, tp_size)), DMA((2, tp_size)),
         ],
         compiler_params=params(2),
         cost_estimate=pl.CostEstimate(flops=10 * pairs * HEAD_DIM, bytes_accessed=16 * seq * HEAD_DIM, transcendentals=pairs),
         name="attention_backward",
-    )(qkv, do, o, lse, o_rows, w_out)
+    )(qkv, do, o, ot, lse, w_out)
 
 
 def reduce_kernel(cp_size, tp_size, chunks, rows_ref, wq_ref, wk_ref, wv_ref, o_rows_ref, oy_ref, wo_ref, wy_ref,
@@ -873,8 +869,8 @@
     def local_step(x_blk, dy_blk, w_query, w_key, w_value, w_out):
         weights = (w_query, w_key, w_value)
         qkv, dy1 = project(x_blk, dy_blk, weights, cp_size, tp_size)
-        o, lse, o_rows, do = forward(qkv, dy_blk, dy1, w_out, cp_size, tp_size)
-        grad_rows, oy, wy = backward(qkv, do, o, lse, o_rows, w_out, cp_size, tp_size)
+        o, ot, lse, do = forward(qkv, dy_blk, dy1, w_out, cp_size, tp_size)
+        grad_rows, o_rows, oy, wy = backward(qkv, do, o, ot, lse, w_out, cp_size, tp_size)
         dx_blk, y_blk, _, _ = reduce_out(grad_rows, weights, o_rows, oy, w_out, wy, cp_size, tp_size)
         return y_blk, dx_blk
 

time: 459 us -> 451 us (0.983)
  Pallas kernels: 451 us -> 443 us
    pallas_call x1, Pallas kernels: 99.1 us -> 94 us  [project(): pl.pallas_call(functools.partial(project_kernel, cp_size, tp_size), out_s...]
where the time goes in v5:
time: 451 us; the launch traced here: 448 us
  Pallas kernels  443 us (98%)
  local copies, waits for them, and re-layouts  4.6 us (1%)
    pallas_call x1, Pallas kernels, reduce_out(): pl.pallas_call(functools.partial(reduce_kernel, cp_size, tp_size, chunks)...  143 us
    pallas_call x1, Pallas kernels, backward(): pl.pallas_call(functools.partial(backward_kernel, cp_size, tp_size), out_...  120 us
    pallas_call x1, Pallas kernels, project(): pl.pallas_call(functools.partial(project_kernel, cp_size, tp_size), out_s...  94 us
    pallas_call x1, Pallas kernels, forward(): pl.pallas_call(functools.partial(forward_kernel, cp_size, tp_size), out_s...  86 us

profile of v5, /device:TPU:97, one launch (start us, length us, event | category | flops | bytes accessed | tf_op | source)
XLA Modules:
  0.0 448.0 jit_solution(15331408203417034526)
XLA Ops:
  0.6 94.0 %project_qkv.1 = (bf16[3,8192,128]{2,1,0:T(8,128)(2,1)}, bf16[128,4096]{1,0:T(8,128)(2,1)}) custom-call(bf16[256,4096]{1,0:T(8,128)(2,1)} %x_ref.1, bf16[256,4096]{1,0:T(8,128)(2,1)} %dy_ref.3, bf16[4096,1024]{1,0:T(8,128)(2,1)} %wq_ref.3, bf16[4096,1024]{1,0:T(8,128)(2,1)} %wk_ref.3, bf16[4096,1024]{1,0:T(8,128)(2,1)} %wv_ref.3), custom_call_target="tpu_custom_call" | custom-call | flops 25769803776 | bytes 25165824 | tf_op jit(solution)/shard_map/project_qkv/pallas_call | solution.py:235
  94.6 86.0 %attention_forward.1 = (bf16[8192,128]{1,0:T(8,128)(2,1)}, bf16[128,8192]{1,0:T(8,128)(2,1)}, f32[16,8,512]{2,1,0:T(8,128)}, bf16[1,8192,128]{2,1,0:T(8,128)(2,1)}) custom-call(bf16[3,8192,128]{2,1,0:T(8,128)(2,1)} %get-tuple-element.14.qkv_ref, bf16[256,4096]{1,0:T(8,128)(2,1)} %dy_ref.3, bf16[128,4096]{1,0:T(8,128)(2,1)} %get-tuple-element.15.dy1_ref, ...), custom_call_target="tpu_custom_call" | custom-call | flops 17179869184 | bytes 8388608 | tf_op jit(solution)/shard_map/attention_forward/pallas_call | solution.py:385
  180.6 119.6 %attention_backward.1 = (bf16[3,1024,1024]{2,1,0:T(8,128)(2,1)}, bf16[1024,1024]{1,0:T(8,128)(2,1)}, bf16[3,256,1024]{2,1,0:T(8,128)(2,1)}, bf16[3,128,4096]{2,1,0:T(8,128)(2,1)}) custom-call(bf16[3,8192,128]{2,1,0:T(8,128)(2,1)} %get-tuple-element.14.qkv_ref, bf16[1,8192,128]{2,1,0:T(8,128)(2,1)} %get-tuple-element.16.do_ref, ...), custom_call_target="tpu_custom_call" | custom-call | flops 42949672960 | bytes 16777216 | tf_op jit(solution)/shard_map/attention_backward/pallas_call | solution.py:596
  300.2 143.2 %project_reduce.1 = (bf16[256,4096]{1,0:T(8,128)(2,1)}, bf16[256,4096]{1,0:T(8,128)(2,1)}, bf16[3,3,128,4096]{3,2,1,0:T(8,128)(2,1)}, bf16[3,4,128,4096]{3,2,1,0:T(8,128)(2,1)}) custom-call(bf16[3,1024,1024]{2,1,0:T(8,128)(2,1)} %get-tuple-element.20.rows_ref, bf16[4096,1024]{1,0:T(8,128)(2,1)} %wq_ref.3, bf16[4096,1024]{1,0:T(8,128)(2,1)} %wk_ref.3, ...), custom_call_target="tpu_custom_call" | custom-call | flops 25769803776 | bytes 25165824 | tf_op jit(solution)/shard_map/project_reduce/pallas_call | solution.py:835
  443.4 0.0 copy-start
  443.4 3.3 copy.10
  446.7 0.0 copy-done
  446.7 1.3 copy.11
Async XLA Ops:
  443.4 3.3 copy-start

commit v6 on v5

--- a/solution.py
+++ b/solution.py
@@ -98,10 +98,10 @@
             (jnp.where(near, self.left, self.far), self.first_row(j, 1)),
         )
 
-    def hop(self, j, side, relayed, dst=None):
+    def hop(self, j, side, relayed):
         src = self.rows(j - 4, side) if relayed else self.src.at[rows_at(self.first_row(j, side), self.part), :]
         return pltpu.make_async_remote_copy(
-            src_ref=src, dst_ref=self.rows(j, side) if dst is None else dst,
+            src_ref=src, dst_ref=self.rows(j, side),
             send_sem=self.sems[0].at[j - 1, side], recv_sem=self.sems[1].at[j - 1, side],
             device_id={'tp': self.right if side else self.left}, device_id_type=MESH)
 
@@ -159,26 +159,18 @@
         lax.fori_loop(1, Gather.STEPS + 1, step, 0)
 
 
-def head_scratch(cp_size, arrays, rows):
+def head_sems(cp_size):
     each = (cp_size - 1, Gather.STEPS + 1, 2)
-    return [pltpu.VMEM((cp_size, arrays, rows, HEAD_DIM), BF16), DMA(each), DMA(each), DMA(each[1:])]
-
-
-def project_kernel(cp_size, tp_size, x_ref, dy_ref, wq_ref, wk_ref, wv_ref, qkv_ref, dy1_ref,
-                   w_v, xg, res, send, recv, local, w_sem, x_sem, y_send, y_recv, dy_send, dy_recv):
+    return DMA(each), DMA(each), DMA(each[1:])
+
+
+def project_phase(cp_size, tp_size, x_ref, weights, qkv, xg, dy_gather, send, recv, local, w_sem, x_sem, y_send, y_recv, w_v, res):
     block = x_ref.shape[0]
     gather = Gather(tp_size, x_ref, xg, y_send, y_recv)
-    early = Gather(tp_size, dy_ref, None, dy_send, dy_recv)
-    heads = HeadSender(cp_size, tp_size, gather, res, qkv_ref, send, recv, local)
-    part = gather.part
-
-    def early_hop(side):
-        return early.hop(1, side, False, dy1_ref.at[pl.ds(side * part, part), :])
-
+    heads = HeadSender(cp_size, tp_size, gather, res, qkv, send, recv, local)
     own = pltpu.make_async_copy(x_ref, xg.at[pl.ds(0, block), :], x_sem)
     own.start()
-    loads = [pltpu.make_async_copy(w, w_v.at[n], w_sem.at[n]) for n, w in enumerate((wq_ref, wk_ref, wv_ref))]
-    meet(*others('cp', cp_size), *beside(tp_size))
+    loads = [pltpu.make_async_copy(w, w_v.at[n], w_sem.at[n]) for n, w in enumerate(weights)]
     for j in range(1, 5):
         gather.start(j, False)
     for load in loads:
@@ -212,37 +204,17 @@
 
         @pl.when(j == 2)
         def _():
-            for side in range(2):
-                early_hop(side).start()
-
-        rows = rows_at(gather.start_row(j), 2 * part)
+            for n in range(1, 5):
+                dy_gather.start(n, False)
+
+        rows = rows_at(gather.start_row(j), 2 * gather.part)
         lax.fori_loop(0, len(loads), lambda n, _: (compute(rows, n), 0)[1], 0)
         heads.start(j)
         return 0
 
     lax.fori_loop(1, Gather.STEPS + 1, step, 0)
     lax.fori_loop(1, Gather.STEPS + 1, lambda j, _: (gather.leave(j), 0)[1], 0)
-    for side in range(2):
-        early_hop(side).wait()
     heads.wait()
-
-
-def project(x_blk, dy_blk, weights, cp_size, tp_size):
-    block, width = x_blk.shape
-    cols = weights[0].shape[1]
-    rows = block * tp_size
-    each = DMA((Gather.STEPS, 2))
-    return pl.pallas_call(
-        functools.partial(project_kernel, cp_size, tp_size),
-        out_shape=(jax.ShapeDtypeStruct((len(weights), rows * cp_size, HEAD_DIM), BF16), jax.ShapeDtypeStruct((block // 2, width), BF16)),
-        in_specs=[ANYWHERE] * 5,
-        out_specs=(ANYWHERE, ANYWHERE),
-        scratch_shapes=[pltpu.VMEM((len(weights), width, cols), BF16), pltpu.VMEM((rows, width), BF16)]
-        + head_scratch(cp_size, len(weights), rows) + [DMA((len(weights),)), DMA, each, each, each, each],
-        compiler_params=params(0),
-        cost_estimate=pl.CostEstimate(flops=6 * rows * width * cols, bytes_accessed=6 * width * cols, transcendentals=0),
-        name="project_qkv",
-    )(x_blk, dy_blk, *weights)
 
 
 def send_piece(cp_size, i, src, dst_of, send, recv, local, start):
@@ -263,24 +235,20 @@
         copy.start() if start else copy.wait_send()
 
 
-def forward_kernel(cp_size, tp_size, qkv_ref, dy_ref, dy1_ref, wo_ref, o_ref, ot_ref, l_ref, do_ref,
-                   qkv, o_v, ot_v, l_v, vt_ref, s_ref, acc_ref, dyg, wo, res, h_send, h_recv, h_local, in_sem, y_send, y_recv, out_sem):
+def forward_phase(cp_size, tp_size, gather, wo_ref, qkv, do_v, h_send, h_recv, h_local, in_sem, o_v, ot_v, l_v,
+                  vt_ref, qt_ref, s_ref, acc_ref, wo, res):
     seq = qkv.shape[1]
     bq = s_ref.shape[0]
     nblk = seq // bq
     c = HEAD_DIM ** -0.5 * LOG2E
-    gather = Gather(tp_size, dy_ref, dyg, y_send, y_recv)
-    heads = HeadSender(cp_size, tp_size, gather, res, do_ref, h_send, h_recv, h_local)
-    block, part = gather.block, gather.part
-
+    heads = HeadSender(cp_size, tp_size, gather, res, do_v, h_send, h_recv, h_local)
+    block = gather.block
     loads = [
-        pltpu.make_async_copy(src, dst, in_sem.at[n])
-        for n, (src, dst) in enumerate(((dy_ref, dyg.at[pl.ds(0, block), :]), (wo_ref, wo), (dy1_ref, dyg.at[pl.ds(block, 2 * part), :]), (qkv_ref, qkv)))]
+        pltpu.make_async_copy(wo_ref, wo, in_sem.at[0]),
+        pltpu.make_async_copy(gather.src, gather.buf.at[pl.ds(0, block), :], in_sem.at[1]),
+    ]
     for load in loads:
         load.start()
-    meet(*others('cp', cp_size), *beside(tp_size))
-    for j in range(2, 5):
-        gather.start(j, False)
 
     per_step = min(4, cp_size)
     cols = per_step * HEAD_DIM
@@ -289,25 +257,16 @@
         rows = rows_at(n * block, block)
 
         def body(s, _):
-            out = dot_nt(dyg[rows, :], wo[rows_at(s * cols, cols), :]).astype(BF16)
+            out = dot_nt(gather.buf[rows, :], wo[rows_at(s * cols, cols), :]).astype(BF16)
             for k in range(per_step):
                 res[per_step * s + k, 0, rows, :] = out[:, k * HEAD_DIM:(k + 1) * HEAD_DIM]
             return 0
 
         lax.fori_loop(0, cp_size // per_step, body, 0)
 
-    def compute_steps(n, _):
+    def compute_steps(n):
         compute(n)
         lax.fori_loop(2 * n - 1, 2 * n + 1, lambda j, _: (heads.start(j), 0)[1], 0)
-        return 0
-
-    for load in loads[:2]:
-        load.wait()
-    compute(0)
-    heads.start(0)
-    for load in loads[2:]:
-        load.wait()
-    gather.start(5, True)
 
     def transpose_step(b, _):
         rows = rows_at(b * bq, bq)
@@ -317,20 +276,26 @@
     lax.fori_loop(0, nblk, transpose_step, 0)
 
     def q_step(i, _):
-        @pl.when(i == nblk // 2)
-        def _():
-            gather.arrive(2)
-            gather.start(6, True)
-
-        @pl.when(i == nblk - 1)
-        def _():
-            lax.fori_loop(3, Gather.STEPS + 1, lambda j, _: (gather.arrive(j), 0)[1], 0)
-            lax.fori_loop(1, tp_size, compute_steps, 0)
+        for n, at in enumerate((nblk // 4, nblk // 2, nblk - nblk // 4, nblk - 2)):
+            @pl.when(i == at)
+            def _():
+                if n == 0:
+                    for load in loads:
+                        load.wait()
+                    for j in range(1, 3):
+                        gather.arrive(j)
+                        gather.start(j + 4, True)
+                    compute(0)
+                    heads.start(0)
+                else:
+                    for j in range(max(3, 2 * n - 1), 2 * n + 1):
+                        gather.arrive(j)
+                    compute_steps(n)
 
         rows = rows_at(i * bq, bq)
-        q = qkv[0, rows, :]
+        qt_ref[...] = qkv[0, rows, :].T
         acc_ref[...] = jnp.zeros_like(acc_ref)
-        s = dot_nt(qkv[1, rows, :], q)
+        s = dot_nn(qkv[1, rows, :], qt_ref[...]) * c
         kk = lax.broadcasted_iota(jnp.int32, (bq, bq), 0)
         qq = lax.broadcasted_iota(jnp.int32, (bq, bq), 1)
         s = jnp.where(kk <= qq, s, -jnp.inf)
@@ -338,12 +303,11 @@
         first = jnp.max(s, axis=0, keepdims=True)
 
         def use(blk, m_old, m, l, following):
-            mc = m * c
-            alpha = jnp.exp2(m_old * c - mc)
-            p = jnp.exp2(s_ref[...] * c - mc)
+            alpha = jnp.exp2(m_old - m)
+            p = jnp.exp2(s_ref[...] - m)
             m_new = m
             if following is not None:
-                s = dot_nt(qkv[1, rows_at(following * bq, bq), :], q)
+                s = dot_nn(qkv[1, rows_at(following * bq, bq), :], qt_ref[...]) * c
             part = jnp.sum(p, axis=0, keepdims=True)
             out = dot_nn(vt_ref[:, rows_at(blk * bq, bq)], p.astype(BF16))
             if following is not None:
@@ -360,73 +324,23 @@
         out = (acc_ref[...] * (1.0 / l)).astype(BF16)
         ot_v[:, rows] = out
         o_v[rows, :] = out.T
-        l_v[i] = jnp.broadcast_to(m * c + jnp.log2(l), (8, bq))
+        l_v[i] = jnp.broadcast_to(m + jnp.log2(l), (8, bq))
         return 0
 
     lax.fori_loop(0, nblk, q_step, 0)
-    stores = [pltpu.make_async_copy(src, dst, out_sem.at[n]) for n, (src, dst) in enumerate(((o_v, o_ref), (ot_v, ot_ref), (l_v, l_ref)))]
-    for store in stores:
-        store.start()
     heads.wait()
-    lax.fori_loop(2, Gather.STEPS + 1, lambda j, _: (gather.leave(j), 0)[1], 0)
-    for store in stores:
-        store.wait()
-
-
-def forward(qkv, dy_blk, dy1, w_out, cp_size, tp_size):
-    seq = qkv.shape[1]
-    bq = seq // (2 * cp_size)
-    block, width = dy_blk.shape
-    cols = w_out.shape[0]
-    pairs = seq * seq // 2
-    rows, turned = (seq, HEAD_DIM), (HEAD_DIM, seq)
-    logs = (seq // bq, 8, bq)
-    each = DMA((Gather.STEPS, 2))
-    return pl.pallas_call(
-        functools.partial(forward_kernel, cp_size, tp_size),
-        out_shape=(
-            jax.ShapeDtypeStruct(rows, BF16),
-            jax.ShapeDtypeStruct(turned, BF16),
-            jax.ShapeDtypeStruct(logs, F32),
-            jax.ShapeDtypeStruct((1, seq, HEAD_DIM), BF16),
-        ),
-        in_specs=[ANYWHERE] * 4,
-        out_specs=(ANYWHERE,) * 4,
-        scratch_shapes=[
-            pltpu.VMEM(qkv.shape, BF16),
-            pltpu.VMEM(rows, BF16),
-            pltpu.VMEM(turned, BF16),
-            pltpu.VMEM(logs, F32),
-            pltpu.VMEM(turned, BF16),
-            pltpu.VMEM((bq, bq), F32),
-            pltpu.VMEM((HEAD_DIM, bq), F32),
-            pltpu.VMEM((tp_size * block, width), BF16),
-            pltpu.VMEM((cols, width), BF16),
-        ] + head_scratch(cp_size, 1, tp_size * block) + [DMA((4,)), each, each, DMA((3,))],
-        compiler_params=params(1),
-        cost_estimate=pl.CostEstimate(flops=4 * pairs * HEAD_DIM, bytes_accessed=8 * seq * HEAD_DIM, transcendentals=pairs),
-        name="attention_forward",
-    )(qkv, dy_blk, dy1, w_out)
-
-
-def backward_kernel(cp_size, tp_size, qkv_ref, do_ref, o_ref, ot_ref, l_ref, wo_ref, rows_ref, o_rows_ref, oy_ref, wy_ref,
-                    qkv, do_v, ot_v, l_v, delta_v, kt_ref, qt_ref, dot_ref, p_ref, ds_ref, dst_ref, dq_acc, dk_acc, dv_acc, grads,
-                    in_sem, send, recv, local, y_send, y_recv):
+    lax.fori_loop(1, Gather.STEPS + 1, lambda j, _: (gather.leave(j), 0)[1], 0)
+
+
+def backward_phase(cp_size, tp_size, wo_ref, rows_ref, o_rows_ref, oy_ref, wy_ref, qkv, do_v, o_v, ot_v, l_v,
+                   send, recv, local, y_send, y_recv,
+                   delta_v, kt_ref, qt_ref, dot_ref, p_ref, ds_ref, dst_ref, dq_acc, dk_acc, dv_acc, grads):
     seq = qkv.shape[1]
     bq = p_ref.shape[0]
     nblk, half_blk = 2 * cp_size, cp_size
     sub = bq // 2
     scale = HEAD_DIM ** -0.5
     c = scale * LOG2E
-    loads = [
-        pltpu.make_async_copy(qkv_ref, qkv, in_sem.at[0]),
-        pltpu.make_async_copy(do_ref.at[0], do_v, in_sem.at[1]),
-        pltpu.make_async_copy(ot_ref, ot_v, in_sem.at[2]),
-        pltpu.make_async_copy(l_ref, l_v, in_sem.at[3]),
-    ]
-    for load in loads:
-        load.start()
-    meet(*others('cp', cp_size), *others('tp', tp_size))
     me_c, me_t = lax.axis_index('cp'), lax.axis_index('tp')
     share, block = wy_ref.shape[1], oy_ref.shape[1]
 
@@ -439,8 +353,6 @@
 
     for r in range(1, tp_size):
         over_tp(0, r).start()
-    for load in loads:
-        load.wait()
 
     def piece(i):
         return rows_at(i * bq, bq)
@@ -449,7 +361,7 @@
         rows = piece(b)
         kt_ref[:, rows] = qkv[1, rows, :].T
         qt_ref[:, rows] = qkv[0, rows, :].T
-        dot_ref[:, rows] = do_v[rows, :].T
+        dot_ref[:, rows] = do_v[0, rows, :].T
         prod = dot_ref[:, rows].astype(F32) * ot_v[:, rows].astype(F32)
         delta_v[b] = jnp.broadcast_to(jnp.sum(prod, axis=0, keepdims=True), (8, bq))
         for acc in (dq_acc, dk_acc, dv_acc):
@@ -464,7 +376,7 @@
         if prev is not None:
             prev_q, prev_k = piece(prev[0]), rows_at(prev[1] * bq + r * sub, sub)
             old_p, old_ds_t, old_ds = p_ref[:, sl], ds_ref[sl, :], dst_ref[:, sl]
-        s = dot_nt(qkv[1, krows, :], qkv[0, piece(q), :])
+        s = dot_nn(qkv[1, krows, :], qt_ref[:, piece(q)])
         if prev is not None:
             dv_acc[:, prev_k] += dot_nn(dot_ref[:, prev_q], old_p)
         p = jnp.exp2(s * c - l_v[q][0:1, :])
@@ -472,7 +384,7 @@
             kk = lax.broadcasted_iota(jnp.int32, (sub, bq), 0) + r * sub
             p = jnp.where(kk <= lax.broadcasted_iota(jnp.int32, (sub, bq), 1), p, 0.0)
         p = p.astype(BF16)
-        dp = dot_nt(qkv[2, krows, :], do_v[piece(q), :])
+        dp = dot_nn(qkv[2, krows, :], dot_ref[:, piece(q)])
         if prev is not None:
             dk_acc[:, prev_k] += dot_nn(qt_ref[:, prev_q], old_ds)
         ds = (p.astype(F32) * (dp - delta_v[q][0:1, :])).astype(BF16)
@@ -487,7 +399,7 @@
         return q, k
 
     def source(kind, i):
-        return (grads.at[pl.ds(0, 1), piece(i), :], grads.at[pl.ds(1, 2), piece(i), :], o_ref.at[piece(i), :])[kind]
+        return (grads.at[pl.ds(0, 1), piece(i), :], grads.at[pl.ds(1, 2), piece(i), :], o_v.at[piece(i), :])[kind]
 
     def target(kind, part, head):
         cols = rows_at(head * HEAD_DIM, HEAD_DIM)
@@ -583,40 +495,63 @@
         over_tp(1, r).wait()
 
 
-def backward(qkv, do, o, ot, lse, w_out, cp_size, tp_size):
+def layer_kernel(cp_size, tp_size, x_ref, dy_ref, wq_ref, wk_ref, wv_ref, wo_ref, rows_ref, o_rows_ref, oy_ref, wy_ref,
+                 qkv, do_v, xg, dyg, w_sem, in_sem, p_send, p_recv, p_local, h_send, h_recv, h_local,
+                 x_send, x_recv, g_send, g_recv, send, recv, local, y_send, y_recv):
     seq = qkv.shape[1]
-    cols, width = w_out.shape
-    block = seq // (cp_size * tp_size)
-    share = cols // cp_size
     bq = seq // (2 * cp_size)
+    meet(*others('cp', cp_size), *others('tp', tp_size))
+    gather = Gather(tp_size, dy_ref, dyg, g_send, g_recv)
+    pl.run_scoped(
+        functools.partial(
+            project_phase, cp_size, tp_size, x_ref, (wq_ref, wk_ref, wv_ref), qkv, xg, gather,
+            p_send, p_recv, p_local, w_sem, in_sem.at[0], x_send, x_recv),
+        pltpu.VMEM((3, *wq_ref.shape), BF16), pltpu.VMEM((cp_size, 3, xg.shape[0], HEAD_DIM), BF16))
+    turned, total, square = pltpu.VMEM((HEAD_DIM, seq), BF16), pltpu.VMEM((HEAD_DIM, seq), F32), pltpu.VMEM((bq, bq), BF16)
+    logs = pltpu.VMEM((2 * cp_size, 8, bq), F32)
+
+    def attend(o_v, ot_v, l_v):
+        pl.run_scoped(
+            functools.partial(forward_phase, cp_size, tp_size, gather, wo_ref, qkv, do_v, h_send, h_recv, h_local, in_sem, o_v, ot_v, l_v),
+            turned, pltpu.VMEM((HEAD_DIM, bq), BF16), pltpu.VMEM((bq, bq), F32), pltpu.VMEM((HEAD_DIM, bq), F32),
+            pltpu.VMEM(wo_ref.shape, BF16), pltpu.VMEM((cp_size, 1, dyg.shape[0], HEAD_DIM), BF16))
+        pl.run_scoped(
+            functools.partial(
+                backward_phase, cp_size, tp_size, wo_ref, rows_ref, o_rows_ref, oy_ref, wy_ref, qkv, do_v, o_v, ot_v, l_v,
+                send, recv, local, y_send, y_recv),
+            logs, turned, turned, turned, square, square, square, total, total, total, pltpu.VMEM(qkv.shape, BF16))
+
+    pl.run_scoped(attend, pltpu.VMEM((seq, HEAD_DIM), BF16), turned, logs)
+
+
+def layer(x_blk, dy_blk, weights, w_out, cp_size, tp_size):
+    block, width = x_blk.shape
+    cols = w_out.shape[0]
+    rows = block * tp_size
+    seq = rows * cp_size
     pairs = seq * seq // 2
-    turned = pltpu.VMEM((HEAD_DIM, seq), BF16)
-    total = pltpu.VMEM((HEAD_DIM, seq), F32)
-    square = pltpu.VMEM((bq, bq), BF16)
+    each = DMA((Gather.STEPS, 2))
+    gathered = pltpu.VMEM((rows, width), BF16)
     return pl.pallas_call(
-        functools.partial(backward_kernel, cp_size, tp_size),
+        functools.partial(layer_kernel, cp_size, tp_size),
         out_shape=(
-            jax.ShapeDtypeStruct((3, 2 * bq, cols), BF16),
-            jax.ShapeDtypeStruct((2 * bq, cols), BF16),
+            jax.ShapeDtypeStruct((3, rows, cols), BF16),
+            jax.ShapeDtypeStruct((rows, cols), BF16),
             jax.ShapeDtypeStruct((tp_size - 1, block, cols), BF16),
-            jax.ShapeDtypeStruct((tp_size - 1, share, width), BF16),
+            jax.ShapeDtypeStruct((tp_size - 1, cols // cp_size, width), BF16),
         ),
         in_specs=[ANYWHERE] * 6,
         out_specs=(ANYWHERE,) * 4,
         scratch_shapes=[
-            pltpu.VMEM(qkv.shape, BF16),
-            pltpu.VMEM((seq, HEAD_DIM), BF16),
-            turned,
-            pltpu.VMEM(lse.shape, F32),
-            pltpu.VMEM(lse.shape, F32),
-            turned, turned, turned, square, square, square, total, total, total,
-            pltpu.VMEM(qkv.shape, BF16),
-            DMA((4,)), DMA((3, 2 * cp_size)), DMA((3, cp_size, 2)), DMA((3, 2)), DMA((2, tp_size)), DMA((2, tp_size)),
+            pltpu.VMEM((3, seq, HEAD_DIM), BF16),
+            pltpu.VMEM((1, seq, HEAD_DIM), BF16),
+            gathered, gathered, DMA((3,)), DMA((2,)), *head_sems(cp_size), *head_sems(cp_size), each, each, each, each,
+            DMA((3, 2 * cp_size)), DMA((3, cp_size, 2)), DMA((3, 2)), DMA((2, tp_size)), DMA((2, tp_size)),
         ],
-        compiler_params=params(2),
-        cost_estimate=pl.CostEstimate(flops=10 * pairs * HEAD_DIM, bytes_accessed=16 * seq * HEAD_DIM, transcendentals=pairs),
-        name="attention_backward",
-    )(qkv, do, o, ot, lse, w_out)
+        compiler_params=params(0),
+        cost_estimate=pl.CostEstimate(flops=14 * pairs * HEAD_DIM + 8 * rows * width * cols, bytes_accessed=8 * width * cols, transcendentals=2 * pairs),
+        name="project_attend",
+    )(x_blk, dy_blk, *weights, w_out)
 
 
 def reduce_kernel(cp_size, tp_size, chunks, rows_ref, wq_ref, wk_ref, wv_ref, o_rows_ref, oy_ref, wo_ref, wy_ref,
@@ -634,10 +569,14 @@
     def w_load(n, a):
         return pltpu.make_async_copy(weights[a].at[rows_at(n * wide, wide), :], w_v.at[lax.rem(n, 2), a], w_sem.at[lax.rem(n, 2), a])
 
-    load = pltpu.make_async_copy(rows_ref, g_v, in_sem)
-    load.start()
+    owners = (far, right, left, me)
+    blocks = [rows_at(owner * block, block) for owner in owners]
+    loads = [pltpu.make_async_copy(rows_ref.at[:, rows, :], g_v.at[:, rows, :], in_sem.at[k]) for k, rows in enumerate(blocks)]
+    loads[FAR].start()
     for a in range(3):
         w_load(0, a).start()
+    for load in loads[RIGHT:]:
+        load.start()
     me_c, mate = lax.axis_index('cp'), partner()
     chips = cp_size // 2
     ahead, behind = lax.rem(me_c + 2, cp_size), lax.rem(me_c + cp_size - 2, cp_size)
@@ -691,8 +630,6 @@
         return pltpu.make_async_remote_copy(
             src_ref=src, dst_ref=dst, send_sem=sends.at[k, n], recv_sem=recvs.at[k, n], device_id={'tp': peer}, device_id_type=MESH)
 
-    load.wait()
-
     def compute(n, _):
         slot = lax.rem(n, 2)
 
@@ -705,8 +642,11 @@
             w_load(n, a).wait()
         cols = rows_at(n * wide, wide)
         ready = {FAR: ('far_r', 'far_l'), RIGHT: ('plain_r',), LEFT: ('plain_l',), OWN: ()}
-        for k, owner in enumerate((far, right, left, me)):
-            rows = rows_at(owner * block, block)
+        for k, rows in enumerate(blocks):
+            @pl.when(n == 0)
+            def _():
+                loads[k].wait()
+
             total = dot_nt(g_v[0, rows, :], w_v[slot, 0])
             total = total + dot_nt(g_v[1, rows, :], w_v[slot, 1])
             part[k, :, cols] = total + dot_nt(g_v[2, rows, :], w_v[slot, 2])
@@ -790,7 +730,7 @@
             return 0
 
         lax.fori_loop(0, span // tile, y_step, 0)
-    y_out = pltpu.make_async_copy(out_v, y_ref, in_sem)
+    y_out = pltpu.make_async_copy(out_v, y_ref, in_sem.at[OWN])
     y_out.start()
     y_out.wait()
 
@@ -852,11 +792,11 @@
             pltpu.VMEM((2, cols, width // 4), BF16),
             pltpu.VMEM((block, width), F32),
             pltpu.VMEM((tp_size, block, cols), BF16),
-            DMA, DMA((2, 3)), DMA((chunks,)), DMA((6, chunks)), DMA((6, chunks)),
+            DMA((4,)), DMA((2, 3)), DMA((chunks,)), DMA((6, chunks)), DMA((6, chunks)),
             DMA((tp_size - 1, 4)), DMA((tp_size - 1, 4)), DMA((tp_size - 1, pairs)), DMA((tp_size - 1, pairs)),
             DMA((tp_size,)), DMA((2, cp_size)),
         ],
-        compiler_params=params(3),
+        compiler_params=params(1),
         cost_estimate=pl.CostEstimate(flops=6 * rows * width * cols, bytes_accessed=6 * width * cols, transcendentals=0),
         name="project_reduce",
     )(grad_rows, *weights, o_rows, oy, w_out, wy)
@@ -868,9 +808,7 @@
 
     def local_step(x_blk, dy_blk, w_query, w_key, w_value, w_out):
         weights = (w_query, w_key, w_value)
-        qkv, dy1 = project(x_blk, dy_blk, weights, cp_size, tp_size)
-        o, ot, lse, do = forward(qkv, dy_blk, dy1, w_out, cp_size, tp_size)
-        grad_rows, o_rows, oy, wy = backward(qkv, do, o, ot, lse, w_out, cp_size, tp_size)
+        grad_rows, o_rows, oy, wy = layer(x_blk, dy_blk, weights, w_out, cp_size, tp_size)
         dx_blk, y_blk, _, _ = reduce_out(grad_rows, weights, o_rows, oy, w_out, wy, cp_size, tp_size)
         return y_blk, dx_blk
 

time: 451 us -> 432 us (0.958)
  Pallas kernels: 443 us -> 423 us
    pallas_call x3 -> x1, Pallas kernels: 300 us -> 282 us  [layer(): pl.pallas_call(functools.partial(layer_kernel, cp_size, tp_size), out_sha...]
where the time goes in v6:
time: 432 us; the launch traced here: 429 us
  Pallas kernels  423 us (98%)
  local copies, waits for them, and re-layouts  4.6 us (1%)
    pallas_call x1, Pallas kernels, layer(): pl.pallas_call(functools.partial(layer_kernel, cp_size, tp_size), out_sha...  282 us
    pallas_call x1, Pallas kernels, reduce_out(): pl.pallas_call(functools.partial(reduce_kernel, cp_size, tp_size, chunks)...  142 us

profile of v6, /device:TPU:97, one launch (start us, length us, event | category | flops | bytes accessed | tf_op | source)
XLA Modules:
  0.0 428.5 jit_solution(1365503811045861515)
XLA Ops:
  0.6 281.6 %project_attend.1 = (bf16[3,1024,1024]{2,1,0:T(8,128)(2,1)}, bf16[1024,1024]{1,0:T(8,128)(2,1)}, bf16[3,256,1024]{2,1,0:T(8,128)(2,1)}, bf16[3,128,4096]{2,1,0:T(8,128)(2,1)}) custom-call(bf16[256,4096]{1,0:T(8,128)(2,1)} %x_ref.1, bf16[256,4096]{1,0:T(8,128)(2,1)} %dy_ref.1, bf16[4096,1024]{1,0:T(8,128)(2,1)} %wq_ref.3, bf16[4096,1024]{1,0:T(8,128)(2,1)} %wk_ref.3, ...), custom_call_target="tpu_custom_call" | custom-call | flops 94489280512 | bytes 33554432 | tf_op jit(solution)/shard_map/project_attend/pallas_call | solution.py:535
  282.3 141.6 %project_reduce.1 = (bf16[256,4096]{1,0:T(8,128)(2,1)}, bf16[256,4096]{1,0:T(8,128)(2,1)}, bf16[3,3,128,4096]{3,2,1,0:T(8,128)(2,1)}, bf16[3,4,128,4096]{3,2,1,0:T(8,128)(2,1)}) custom-call(bf16[3,1024,1024]{2,1,0:T(8,128)(2,1)} %get-tuple-element.8.rows_ref, bf16[4096,1024]{1,0:T(8,128)(2,1)} %wq_ref.3, bf16[4096,1024]{1,0:T(8,128)(2,1)} %wk_ref.3, ...), custom_call_target="tpu_custom_call" | custom-call | flops 25769803776 | bytes 25165824 | tf_op jit(solution)/shard_map/project_reduce/pallas_call | solution.py:775
  423.9 0.0 copy-start
  423.9 3.3 copy.10
  427.2 0.0 copy-done
  427.2 1.3 copy.11
Async XLA Ops:
  423.9 3.3 copy-start
